TPU v7x, 32 devices: a whole 2x2x4 slice. The times are simulated.
32 devices in a mesh: gz: 4 (over z), gy: 2 (over y), gx: 4 (over x, core).
Axes of the slice: x: 2, y: 2, z: 4, core: 2. Of those that a mesh axis runs over, the one named last changes fastest.
Arguments:
- k_cell: float32 [192, 192, 192], P('gx', 'gy', 'gz')
- k_ghost: float32 [6, 192, 192], replicated
- f_rhs: float32 [192, 192, 192], P('gx', 'gy', 'gz')
- u_init: float32 [192, 192, 192], P('gx', 'gy', 'gz')
Outputs:
- output 1: float32 [192, 192, 192], P('gx', 'gy', 'gz')
- output 2: float32 [192, 192, 192], P('gx', 'gy', 'gz')
- output 3: float32 [8], replicated
All inputs are finite; a program needn't handle non-finite values.
Results may differ from a plain program's by a relative error of at most 0.001.
Values sent between devices are 32-bit elements.
A program may use at most 1 GiB of HBM per device.

v0:
```python
import jax
import jax.numpy as jnp
from jax import lax
from jax.sharding import PartitionSpec as P

CG_ITERS = 8
GRID_AXES = ('gx', 'gy', 'gz')
MESH_AXES = ('gz', 'gy', 'gx')


def neighbour_layers(grid_field, axis_dim, axis_len):
    size_here = grid_field.shape[axis_dim]
    low_layer = lax.slice_in_dim(grid_field, 0, 1, axis=axis_dim)
    top_layer = lax.slice_in_dim(grid_field, size_here - 1, size_here, axis=axis_dim)
    if axis_len == 1:
        return jnp.zeros_like(top_layer), jnp.zeros_like(low_layer)
    upward = [(src_rank, src_rank + 1) for src_rank in range(axis_len - 1)]
    downward = [(src_rank + 1, src_rank) for src_rank in range(axis_len - 1)]
    from_below = lax.ppermute(top_layer, GRID_AXES[axis_dim], upward)
    from_above = lax.ppermute(low_layer, GRID_AXES[axis_dim], downward)
    return from_below, from_above


def harmonic_faces(k_ext, axis_dim):
    size_here = k_ext.shape[axis_dim]
    left_k = lax.slice_in_dim(k_ext, 0, size_here - 1, axis=axis_dim)
    right_k = lax.slice_in_dim(k_ext, 1, size_here, axis=axis_dim)
    return 2.0 * left_k * right_k / (left_k + right_k)


def apply_operator(grid_field, face_coefs, layers):
    op_total = None
    for axis_dim in range(3):
        from_below, from_above = layers[axis_dim]
        padded = jnp.concatenate([from_below, grid_field, from_above], axis=axis_dim)
        size_here = padded.shape[axis_dim]
        face_flux = face_coefs[axis_dim] * (lax.slice_in_dim(padded, 1, size_here, axis=axis_dim) - lax.slice_in_dim(padded, 0, size_here - 1, axis=axis_dim))
        axis_part = lax.slice_in_dim(face_flux, 0, size_here - 2, axis=axis_dim) - lax.slice_in_dim(face_flux, 1, size_here - 1, axis=axis_dim)
        op_total = axis_part if op_total is None else op_total + axis_part
    return op_total


def diagonal(face_coefs):
    diag_sum = None
    for axis_dim in range(3):
        size_here = face_coefs[axis_dim].shape[axis_dim]
        low_coef = lax.slice_in_dim(face_coefs[axis_dim], 0, size_here - 1, axis=axis_dim)
        high_coef = lax.slice_in_dim(face_coefs[axis_dim], 1, size_here, axis=axis_dim)
        diag_sum = low_coef + high_coef if diag_sum is None else diag_sum + low_coef + high_coef
    return diag_sum


def local_coefs(k_cell, k_ghost, coords, counts):
    block_shape = k_cell.shape
    face_coefs = []
    for axis_dim in range(3):
        others = [other_dim for other_dim in range(3) if other_dim != axis_dim]
        starts = (coords[others[0]] * block_shape[others[0]], coords[others[1]] * block_shape[others[1]])
        extent = (block_shape[others[0]], block_shape[others[1]])
        low_wall = jnp.expand_dims(lax.dynamic_slice(k_ghost[2 * axis_dim], starts, extent), axis_dim)
        high_wall = jnp.expand_dims(lax.dynamic_slice(k_ghost[2 * axis_dim + 1], starts, extent), axis_dim)
        from_below, from_above = neighbour_layers(k_cell, axis_dim, counts[axis_dim])
        from_below = jnp.where(coords[axis_dim] == 0, low_wall, from_below)
        from_above = jnp.where(coords[axis_dim] == counts[axis_dim] - 1, high_wall, from_above)
        face_coefs.append(harmonic_faces(jnp.concatenate([from_below, k_cell, from_above], axis=axis_dim), axis_dim))
    return face_coefs


def solution(mesh):
    counts = tuple(mesh.shape[axis_name] for axis_name in GRID_AXES)
    grid_spec = P('gx', 'gy', 'gz')

    def global_sum(local_value):
        return lax.psum(local_value, MESH_AXES)

    def local_solve(k_cell, k_ghost, f_rhs, u_init):
        coords = [lax.axis_index(axis_name) for axis_name in GRID_AXES]
        face_coefs = local_coefs(k_cell, k_ghost, coords, counts)
        inv_diag = 1.0 / diagonal(face_coefs)

        def apply_stencil(grid_field):
            layers = [neighbour_layers(grid_field, axis_dim, counts[axis_dim]) for axis_dim in range(3)]
            return apply_operator(grid_field, face_coefs, layers)

        residual = f_rhs - apply_stencil(u_init)
        precond = residual * inv_diag
        rz_old = global_sum(jnp.sum(residual * precond))
        approx = u_init
        direction = precond
        history = []
        for iteration in range(CG_ITERS):
            q_vec = apply_stencil(direction)
            step_alpha = rz_old / global_sum(jnp.sum(direction * q_vec))
            approx = approx + step_alpha * direction
            residual = residual - step_alpha * q_vec
            precond = residual * inv_diag
            pair_sums = global_sum(jnp.stack([jnp.sum(residual * precond), jnp.sum(residual * residual)]))
            direction = precond + (pair_sums[0] / rz_old) * direction
            rz_old = pair_sums[0]
            history.append(pair_sums[1])
        return approx, residual, jnp.stack(history)

    return jax.shard_map(local_solve, mesh=mesh, in_specs=(grid_spec, P(), grid_spec, grid_spec), out_specs=(grid_spec, grid_spec, P()), check_vma=False)
```

profile of v0, /device:TPU:0, one launch (start us, length us, event | category | flops | bytes accessed | tf_op | source)
XLA Modules:
  0.0 1232.3 jit_solution(16049257003942732464)
XLA Ops:
  3.6 6.2 collective-permute-start.11
  36.0 5.7 collective-permute-start.4
  43.2 4.2 collective-permute-start.7
  48.3 4.5 collective-permute-start.8
  54.3 4.5 fusion.8
  64.7 4.2 collective-permute-start
  80.1 4.5 copy.251
  84.6 4.5 copy.252
  89.1 4.5 copy.246
  93.6 4.5 copy.248
  104.1 6.9 fusion.38
  111.1 5.8 subtract_multiply_fusion
  117.1 6.6 fusion.55
  127.9 4.5 collective-permute-start.15
  139.1 4.5 collective-permute-start.17
  148.1 5.0 fusion.9
  157.7 5.9 fusion.39
  169.1 41.2 %all-reduce = (f32[]{:T(128)}, f32[]{:T(128)}) all-reduce(f32[]{:T(128)} %get-tuple-element.32, f32[]{:T(128)} %get-tuple-element.31), channel_id=1, replica_groups=mesh['gz'=4,'gy'=2,'gx'=4] {'gz','gy','gx'}, use_global_device_ids=true, to_apply=%region_1.2 | all-reduce | flops 2 | bytes 16 | tf_op jit(solution)/shard_map/psum | solution.py:74
  211.6 6.7 multiply_reduce_fusion.21
  219.6 40.0 %psum.121 = f32[2]{0:T(128)S(1)} all-reduce(f32[2]{0:T(128)S(1)} %pad_maximum_fusion.8), channel_id=1, replica_groups=mesh['gz'=4,'gy'=2,'gx'=4] {'gz','gy','gx'}, use_global_device_ids=true, to_apply=%region_6.7 | all-reduce | flops 2 | bytes 16 | tf_op jit(solution)/shard_map/psum | solution.py:74
  267.6 4.5 collective-permute-start.21
  278.8 4.6 collective-permute-start.23
  296.2 4.4 fusion.40
  306.4 40.2 %psum.122 = f32[]{:T(128)} all-reduce(f32[]{:T(128)} %get-tuple-element.60), channel_id=1, replica_groups=mesh['gz'=4,'gy'=2,'gx'=4] {'gz','gy','gx'}, use_global_device_ids=true, to_apply=%region_8.9 | all-reduce | flops 1 | bytes 8 | tf_op jit(solution)/shard_map/psum | solution.py:74
  347.9 6.5 multiply_reduce_fusion.18
  355.8 40.0 %psum.123 = f32[2]{0:T(128)S(1)} all-reduce(f32[2]{0:T(128)S(1)} %pad_maximum_fusion.9), channel_id=1, replica_groups=mesh['gz'=4,'gy'=2,'gx'=4] {'gz','gy','gx'}, use_global_device_ids=true, to_apply=%region_11.12 | all-reduce | flops 2 | bytes 16 | tf_op jit(solution)/shard_map/psum | solution.py:74
  404.0 4.5 collective-permute-start.27
  415.1 4.5 collective-permute-start.29
  432.1 4.4 fusion.41
  442.3 40.2 %psum.124 = f32[]{:T(128)} all-reduce(f32[]{:T(128)} %get-tuple-element.56), channel_id=1, replica_groups=mesh['gz'=4,'gy'=2,'gx'=4] {'gz','gy','gx'}, use_global_device_ids=true, to_apply=%region_13.14 | all-reduce | flops 1 | bytes 8 | tf_op jit(solution)/shard_map/psum | solution.py:74
  483.8 6.6 multiply_reduce_fusion.15
  491.7 40.0 %psum.125 = f32[2]{0:T(128)S(1)} all-reduce(f32[2]{0:T(128)S(1)} %pad_maximum_fusion.10), channel_id=1, replica_groups=mesh['gz'=4,'gy'=2,'gx'=4] {'gz','gy','gx'}, use_global_device_ids=true, to_apply=%region_16.17 | all-reduce | flops 2 | bytes 16 | tf_op jit(solution)/shard_map/psum | solution.py:74
  539.9 4.5 collective-permute-start.33
  551.0 4.5 collective-permute-start.35
  568.1 4.4 fusion.42
  578.2 40.2 %psum.126 = f32[]{:T(128)} all-reduce(f32[]{:T(128)} %get-tuple-element.52), channel_id=1, replica_groups=mesh['gz'=4,'gy'=2,'gx'=4] {'gz','gy','gx'}, use_global_device_ids=true, to_apply=%region_18.19 | all-reduce | flops 1 | bytes 8 | tf_op jit(solution)/shard_map/psum | solution.py:74
  619.8 6.5 multiply_reduce_fusion.12
  627.7 40.0 %psum.127 = f32[2]{0:T(128)S(1)} all-reduce(f32[2]{0:T(128)S(1)} %pad_maximum_fusion.11), channel_id=1, replica_groups=mesh['gz'=4,'gy'=2,'gx'=4] {'gz','gy','gx'}, use_global_device_ids=true, to_apply=%region_21.22 | all-reduce | flops 2 | bytes 16 | tf_op jit(solution)/shard_map/psum | solution.py:74
  675.8 4.5 collective-permute-start.39
  687.0 4.6 collective-permute-start.41
  704.3 4.4 fusion.43
  714.4 40.2 %psum.128 = f32[]{:T(128)} all-reduce(f32[]{:T(128)} %get-tuple-element.48), channel_id=1, replica_groups=mesh['gz'=4,'gy'=2,'gx'=4] {'gz','gy','gx'}, use_global_device_ids=true, to_apply=%region_23.24 | all-reduce | flops 1 | bytes 8 | tf_op jit(solution)/shard_map/psum | solution.py:74
  755.9 6.6 multiply_reduce_fusion.9
  763.9 40.0 %psum.129 = f32[2]{0:T(128)S(1)} all-reduce(f32[2]{0:T(128)S(1)} %pad_maximum_fusion.12), channel_id=1, replica_groups=mesh['gz'=4,'gy'=2,'gx'=4] {'gz','gy','gx'}, use_global_device_ids=true, to_apply=%region_26.27 | all-reduce | flops 2 | bytes 16 | tf_op jit(solution)/shard_map/psum | solution.py:74
  812.0 4.5 collective-permute-start.45
  823.1 4.6 collective-permute-start.47
  840.2 4.4 fusion.44
  850.2 40.2 %psum.130 = f32[]{:T(128)} all-reduce(f32[]{:T(128)} %get-tuple-element.44), channel_id=1, replica_groups=mesh['gz'=4,'gy'=2,'gx'=4] {'gz','gy','gx'}, use_global_device_ids=true, to_apply=%region_28.29 | all-reduce | flops 1 | bytes 8 | tf_op jit(solution)/shard_map/psum | solution.py:74
  891.8 6.5 multiply_reduce_fusion.6
  899.7 40.0 %psum.131 = f32[2]{0:T(128)S(1)} all-reduce(f32[2]{0:T(128)S(1)} %pad_maximum_fusion.13), channel_id=1, replica_groups=mesh['gz'=4,'gy'=2,'gx'=4] {'gz','gy','gx'}, use_global_device_ids=true, to_apply=%region_31.32 | all-reduce | flops 2 | bytes 16 | tf_op jit(solution)/shard_map/psum | solution.py:74
  947.8 4.5 collective-permute-start.51
  959.0 4.6 collective-permute-start.53
  976.1 4.4 fusion.45
  986.3 40.2 %psum.132 = f32[]{:T(128)} all-reduce(f32[]{:T(128)} %get-tuple-element.40), channel_id=1, replica_groups=mesh['gz'=4,'gy'=2,'gx'=4] {'gz','gy','gx'}, use_global_device_ids=true, to_apply=%region_33.34 | all-reduce | flops 1 | bytes 8 | tf_op jit(solution)/shard_map/psum | solution.py:74
  1027.8 6.5 multiply_reduce_fusion.3
  1035.7 40.0 %psum.133 = f32[2]{0:T(128)S(1)} all-reduce(f32[2]{0:T(128)S(1)} %pad_maximum_fusion.14), channel_id=1, replica_groups=mesh['gz'=4,'gy'=2,'gx'=4] {'gz','gy','gx'}, use_global_device_ids=true, to_apply=%region_36.37 | all-reduce | flops 2 | bytes 16 | tf_op jit(solution)/shard_map/psum | solution.py:74
  1083.9 4.5 collective-permute-start.57
  1095.1 4.6 collective-permute-start.59
  1112.3 4.4 fusion.46
  1123.1 40.2 %psum.134 = f32[]{:T(128)} all-reduce(f32[]{:T(128)} %get-tuple-element.36), channel_id=1, replica_groups=mesh['gz'=4,'gy'=2,'gx'=4] {'gz','gy','gx'}, use_global_device_ids=true, to_apply=%region_38.39 | all-reduce | flops 1 | bytes 8 | tf_op jit(solution)/shard_map/psum | solution.py:74
  1164.6 9.2 multiply_add_fusion
  1176.8 5.1 fusion.17
  1186.1 40.0 %psum.135 = f32[2]{0:T(128)S(1)} all-reduce(f32[2]{0:T(128)S(1)} %pad_maximum_fusion.15), channel_id=1, replica_groups=mesh['gz'=4,'gy'=2,'gx'=4] {'gz','gy','gx'}, use_global_device_ids=true, to_apply=%region_41.42 | all-reduce | flops 2 | bytes 16 | tf_op jit(solution)/shard_map/psum | solution.py:74
  1226.7 5.4 stack.99
  (317 shorter events, 320.3 us)
Async XLA Ops:
  2.3 95.8 %collective-permute-start.10 = (f32[48,96,1]{1,0,2:T(8,128)}, f32[48,96,1]{1,0,2:T(8,128)}, u32[]{:S(2)}, u32[]{:S(2)}) collective-permute-start(f32[48,96,1]{1,0,2:T(8,128)} %bitcast.29), channel_id=1, source_target_pairs={{8,0},{16,8},{24,16},{9,1},{17,9},{25,17},{10,2},{18,10},{26,18},{... | collective-permute-start | bytes 55304 | tf_op jit(solution)/shard_map/ppermute | solution.py:20
  3.6 97.5 %collective-permute-start.11 = (f32[48,96,1]{1,0,2:T(8,128)}, f32[48,96,1]{1,0,2:T(8,128)}, u32[]{:S(2)}, u32[]{:S(2)}) collective-permute-start(f32[48,96,1]{1,0,2:T(8,128)} %bitcast.30), channel_id=1, source_target_pairs={{0,8},{8,16},{16,24},{1,9},{9,17},{17,25},{2,10},{10,18},{18,26},{... | collective-permute-start | bytes 55304 | tf_op jit(solution)/shard_map/ppermute | solution.py:19
  11.5 50.4 %collective-permute-start.9 = (f32[48,96,1]{1,0,2:T(8,128)}, f32[48,96,1]{1,0,2:T(8,128)}, u32[]{:S(2)}, u32[]{:S(2)}) collective-permute-start(f32[48,96,1]{1,0,2:T(8,128)} %bitcast.28), channel_id=1, source_target_pairs={{8,0},{16,8},{24,16},{9,1},{17,9},{25,17},{10,2},{18,10},{26,18},{... | collective-permute-start | bytes 55304 | tf_op jit(solution)/shard_map/ppermute | solution.py:20
  14.8 89.3 %copy-start.23 = (f32[48,96,48]{2,0,1:T(8,128)}, f32[48,96,48]{2,0,1:T(8,128)S(1)}, u32[]{:S(2)}) copy-start(f32[48,96,48]{2,0,1:T(8,128)S(1)} %copy.278) | copy-start | bytes 2654212
  15.4 32.9 %collective-permute-start.6 = (f32[48,1,48]{2,0,1:T(8,128)}, f32[48,1,48]{2,0,1:T(8,128)}, u32[]{:S(2)}, u32[]{:S(2)}) collective-permute-start(f32[48,1,48]{2,0,1:T(8,128)} %get-tuple-element.125), channel_id=1, source_target_pairs={{4,0},{5,1},{6,2},{7,3},{12,8},{13,9},{14,10},{15,11},{20,16},{21,... | collective-permute-start | bytes 27656 | tf_op jit(solution)/shard_map/ppermute | solution.py:20
  21.1 14.8 %collective-permute-start.5 = (f32[48,1,48]{2,0,1:T(8,128)}, f32[48,1,48]{2,0,1:T(8,128)}, u32[]{:S(2)}, u32[]{:S(2)}) collective-permute-start(f32[48,1,48]{2,0,1:T(8,128)} %get-tuple-element.123), channel_id=1, source_target_pairs={{4,0},{5,1},{6,2},{7,3},{12,8},{13,9},{14,10},{15,11},{20,16},{21,... | collective-permute-start | bytes 27656 | tf_op jit(solution)/shard_map/ppermute | solution.py:20
  36.0 7.2 collective-permute-start.4
  43.2 9.7 collective-permute-start.7
  48.3 16.5 %collective-permute-start.8 = (f32[48,96,1]{1,0,2:T(8,128)}, f32[48,96,1]{1,0,2:T(8,128)S(1)}, u32[]{:S(2)}, u32[]{:S(2)}) collective-permute-start(f32[48,96,1]{1,0,2:T(8,128)} %bitcast.35), channel_id=1, source_target_pairs={{0,8},{8,16},{16,24},{1,9},{9,17},{17,25},{2,10},{10,18},{18,26},{... | collective-permute-start | bytes 55304 | tf_op jit(solution)/shard_map/ppermute | solution.py:19
  52.9 5.9 collective-permute-start.1
  58.8 13.4 %collective-permute-start.3 = (f32[1,96,48]{1,2,0:T(8,128)S(1)}, f32[1,96,48]{1,2,0:T(8,128)S(1)}, u32[]{:S(2)}, u32[]{:S(2)}) collective-permute-start(f32[1,96,48]{1,2,0:T(8,128)S(1)} %copy-done.42), channel_id=1, source_target_pairs={{0,1},{1,2},{2,3},{4,5},{5,6},{6,7},{8,9},{9,10},{10,11},{12,13},{... | collective-permute-start | bytes 55304 | tf_op jit(solution)/shard_map/ppermute | solution.py:19
  61.9 10.3 collective-permute-start.2
  64.7 5.8 collective-permute-start
  116.9 46.7 %copy-start = (f32[49,96,48]{2,0,1:T(8,128)}, f32[49,96,48]{2,0,1:T(8,128)S(1)}, u32[]{:S(2)}) copy-start(f32[49,96,48]{2,0,1:T(8,128)S(1)} %get-tuple-element.69) | copy-start | bytes 2709508
  126.6 18.3 %collective-permute-start.14 = (f32[48,1,48]{2,0,1:T(8,128)S(1)}, f32[48,1,48]{2,0,1:T(8,128)S(1)}, u32[]{:S(2)}, u32[]{:S(2)}) collective-permute-start(f32[48,1,48]{2,0,1:T(8,128)S(1)} %get-tuple-element.119), channel_id=1, source_target_pairs={{4,0},{5,1},{6,2},{7,3},{12,8},{13,9},{14,10},{15,11},{20,16},{21,... | collective-permute-start | bytes 27656 | tf_op jit(solution)/shard_map/ppermute | solution.py:20
  127.9 20.2 %collective-permute-start.15 = (f32[48,1,48]{2,0,1:T(8,128)S(1)}, f32[48,1,48]{2,0,1:T(8,128)S(1)}, u32[]{:S(2)}, u32[]{:S(2)}) collective-permute-start(f32[48,1,48]{2,0,1:T(8,128)S(1)} %get-tuple-element.118), channel_id=1, source_target_pairs={{0,4},{1,5},{2,6},{3,7},{8,12},{9,13},{10,14},{11,15},{16,20},{17,... | collective-permute-start | bytes 27656 | tf_op jit(solution)/shard_map/ppermute | solution.py:19
  135.1 18.0 %collective-permute-start.16 = (f32[48,96,1]{1,0,2:T(8,128)S(1)}, f32[48,96,1]{1,0,2:T(8,128)S(1)}, u32[]{:S(2)}, u32[]{:S(2)}) collective-permute-start(f32[48,96,1]{1,0,2:T(8,128)S(1)} %copy.274), channel_id=1, source_target_pairs={{8,0},{16,8},{24,16},{9,1},{17,9},{25,17},{10,2},{18,10},{26,18},{... | collective-permute-start | bytes 55304 | tf_op jit(solution)/shard_map/ppermute | solution.py:20
  139.1 16.3 %collective-permute-start.17 = (f32[48,96,1]{1,0,2:T(8,128)S(1)}, f32[48,96,1]{1,0,2:T(8,128)S(1)}, u32[]{:S(2)}, u32[]{:S(2)}) collective-permute-start(f32[48,96,1]{1,0,2:T(8,128)S(1)} %copy.276), channel_id=1, source_target_pairs={{0,8},{8,16},{16,24},{1,9},{9,17},{17,25},{2,10},{10,18},{18,26},{... | collective-permute-start | bytes 55304 | tf_op jit(solution)/shard_map/ppermute | solution.py:19
  143.6 19.9 %collective-permute-start.12 = (f32[1,96,48]{2,0,1:T(1,128)S(1)}, f32[1,96,48]{2,0,1:T(1,128)S(1)}, u32[]{:S(2)}, u32[]{:S(2)}) collective-permute-start(f32[1,96,48]{2,0,1:T(1,128)S(1)} %get-tuple-element.117), channel_id=1, source_target_pairs={{1,0},{2,1},{3,2},{5,4},{6,5},{7,6},{9,8},{10,9},{11,10},{13,12},{... | collective-permute-start | bytes 55304 | tf_op jit(solution)/shard_map/ppermute | solution.py:20
  144.9 18.6 %collective-permute-start.13 = (f32[1,96,48]{2,0,1:T(1,128)S(1)}, f32[1,96,48]{2,0,1:T(1,128)S(1)}, u32[]{:S(2)}, u32[]{:S(2)}) collective-permute-start(f32[1,96,48]{2,0,1:T(1,128)S(1)} %get-tuple-element.116), channel_id=1, source_target_pairs={{0,1},{1,2},{2,3},{4,5},{5,6},{6,7},{8,9},{9,10},{10,11},{12,13},{... | collective-permute-start | bytes 55304 | tf_op jit(solution)/shard_map/ppermute | solution.py:19
  211.6 49.9 %copy-start.5 = (f32[48,96,48]{2,0,1:T(8,128)S(1)}, f32[48,96,48]{2,0,1:T(8,128)}, u32[]{:S(2)}) copy-start(f32[48,96,48]{2,0,1:T(8,128)} %copy-done.3) | copy-start | bytes 2654212
  266.3 18.4 %collective-permute-start.20 = (f32[48,1,48]{2,0,1:T(8,128)S(1)}, f32[48,1,48]{2,0,1:T(8,128)S(1)}, u32[]{:S(2)}, u32[]{:S(2)}) collective-permute-start(f32[48,1,48]{2,0,1:T(8,128)S(1)} %get-tuple-element.113), channel_id=1, source_target_pairs={{4,0},{5,1},{6,2},{7,3},{12,8},{13,9},{14,10},{15,11},{20,16},{21,... | collective-permute-start | bytes 27656 | tf_op jit(solution)/shard_map/ppermute | solution.py:20
  267.6 20.5 %collective-permute-start.21 = (f32[48,1,48]{2,0,1:T(8,128)S(1)}, f32[48,1,48]{2,0,1:T(8,128)S(1)}, u32[]{:S(2)}, u32[]{:S(2)}) collective-permute-start(f32[48,1,48]{2,0,1:T(8,128)S(1)} %get-tuple-element.112), channel_id=1, source_target_pairs={{0,4},{1,5},{2,6},{3,7},{8,12},{9,13},{10,14},{11,15},{16,20},{17,... | collective-permute-start | bytes 27656 | tf_op jit(solution)/shard_map/ppermute | solution.py:19
  275.0 16.7 %collective-permute-start.22 = (f32[48,96,1]{1,0,2:T(8,128)S(1)}, f32[48,96,1]{1,0,2:T(8,128)S(1)}, u32[]{:S(2)}, u32[]{:S(2)}) collective-permute-start(f32[48,96,1]{1,0,2:T(8,128)S(1)} %copy.279), channel_id=1, source_target_pairs={{8,0},{16,8},{24,16},{9,1},{17,9},{25,17},{10,2},{18,10},{26,18},{... | collective-permute-start | bytes 55304 | tf_op jit(solution)/shard_map/ppermute | solution.py:20
  278.8 15.1 %collective-permute-start.23 = (f32[48,96,1]{1,0,2:T(8,128)S(1)}, f32[48,96,1]{1,0,2:T(8,128)S(1)}, u32[]{:S(2)}, u32[]{:S(2)}) collective-permute-start(f32[48,96,1]{1,0,2:T(8,128)S(1)} %copy.281), channel_id=1, source_target_pairs={{0,8},{8,16},{16,24},{1,9},{9,17},{17,25},{2,10},{10,18},{18,26},{... | collective-permute-start | bytes 55304 | tf_op jit(solution)/shard_map/ppermute | solution.py:19
  283.4 17.2 %collective-permute-start.18 = (f32[1,96,48]{2,0,1:T(1,128)S(1)}, f32[1,96,48]{2,0,1:T(1,128)S(1)}, u32[]{:S(2)}, u32[]{:S(2)}) collective-permute-start(f32[1,96,48]{2,0,1:T(1,128)S(1)} %get-tuple-element.111), channel_id=1, source_target_pairs={{1,0},{2,1},{3,2},{5,4},{6,5},{7,6},{9,8},{10,9},{11,10},{13,12},{... | collective-permute-start | bytes 55304 | tf_op jit(solution)/shard_map/ppermute | solution.py:20
  284.7 15.9 %collective-permute-start.19 = (f32[1,96,48]{2,0,1:T(1,128)S(1)}, f32[1,96,48]{2,0,1:T(1,128)S(1)}, u32[]{:S(2)}, u32[]{:S(2)}) collective-permute-start(f32[1,96,48]{2,0,1:T(1,128)S(1)} %get-tuple-element.110), channel_id=1, source_target_pairs={{0,1},{1,2},{2,3},{4,5},{5,6},{6,7},{8,9},{9,10},{10,11},{12,13},{... | collective-permute-start | bytes 55304 | tf_op jit(solution)/shard_map/ppermute | solution.py:19
  402.7 18.3 %collective-permute-start.26 = (f32[48,1,48]{2,0,1:T(8,128)S(1)}, f32[48,1,48]{2,0,1:T(8,128)S(1)}, u32[]{:S(2)}, u32[]{:S(2)}) collective-permute-start(f32[48,1,48]{2,0,1:T(8,128)S(1)} %get-tuple-element.107), channel_id=1, source_target_pairs={{4,0},{5,1},{6,2},{7,3},{12,8},{13,9},{14,10},{15,11},{20,16},{21,... | collective-permute-start | bytes 27656 | tf_op jit(solution)/shard_map/ppermute | solution.py:20
  404.0 20.2 %collective-permute-start.27 = (f32[48,1,48]{2,0,1:T(8,128)S(1)}, f32[48,1,48]{2,0,1:T(8,128)S(1)}, u32[]{:S(2)}, u32[]{:S(2)}) collective-permute-start(f32[48,1,48]{2,0,1:T(8,128)S(1)} %get-tuple-element.106), channel_id=1, source_target_pairs={{0,4},{1,5},{2,6},{3,7},{8,12},{9,13},{10,14},{11,15},{16,20},{17,... | collective-permute-start | bytes 27656 | tf_op jit(solution)/shard_map/ppermute | solution.py:19
  411.3 16.3 %collective-permute-start.28 = (f32[48,96,1]{1,0,2:T(8,128)S(1)}, f32[48,96,1]{1,0,2:T(8,128)S(1)}, u32[]{:S(2)}, u32[]{:S(2)}) collective-permute-start(f32[48,96,1]{1,0,2:T(8,128)S(1)} %copy.283), channel_id=1, source_target_pairs={{8,0},{16,8},{24,16},{9,1},{17,9},{25,17},{10,2},{18,10},{26,18},{... | collective-permute-start | bytes 55304 | tf_op jit(solution)/shard_map/ppermute | solution.py:20
  415.1 14.8 %collective-permute-start.29 = (f32[48,96,1]{1,0,2:T(8,128)S(1)}, f32[48,96,1]{1,0,2:T(8,128)S(1)}, u32[]{:S(2)}, u32[]{:S(2)}) collective-permute-start(f32[48,96,1]{1,0,2:T(8,128)S(1)} %copy.285), channel_id=1, source_target_pairs={{0,8},{8,16},{16,24},{1,9},{9,17},{17,25},{2,10},{10,18},{18,26},{... | collective-permute-start | bytes 55304 | tf_op jit(solution)/shard_map/ppermute | solution.py:19
  419.6 16.9 %collective-permute-start.24 = (f32[1,96,48]{2,0,1:T(1,128)S(1)}, f32[1,96,48]{2,0,1:T(1,128)S(1)}, u32[]{:S(2)}, u32[]{:S(2)}) collective-permute-start(f32[1,96,48]{2,0,1:T(1,128)S(1)} %get-tuple-element.105), channel_id=1, source_target_pairs={{1,0},{2,1},{3,2},{5,4},{6,5},{7,6},{9,8},{10,9},{11,10},{13,12},{... | collective-permute-start | bytes 55304 | tf_op jit(solution)/shard_map/ppermute | solution.py:20
  421.0 15.6 %collective-permute-start.25 = (f32[1,96,48]{2,0,1:T(1,128)S(1)}, f32[1,96,48]{2,0,1:T(1,128)S(1)}, u32[]{:S(2)}, u32[]{:S(2)}) collective-permute-start(f32[1,96,48]{2,0,1:T(1,128)S(1)} %get-tuple-element.104), channel_id=1, source_target_pairs={{0,1},{1,2},{2,3},{4,5},{5,6},{6,7},{8,9},{9,10},{10,11},{12,13},{... | collective-permute-start | bytes 55304 | tf_op jit(solution)/shard_map/ppermute | solution.py:19
  538.6 18.3 %collective-permute-start.32 = (f32[48,1,48]{2,0,1:T(8,128)S(1)}, f32[48,1,48]{2,0,1:T(8,128)S(1)}, u32[]{:S(2)}, u32[]{:S(2)}) collective-permute-start(f32[48,1,48]{2,0,1:T(8,128)S(1)} %get-tuple-element.101), channel_id=1, source_target_pairs={{4,0},{5,1},{6,2},{7,3},{12,8},{13,9},{14,10},{15,11},{20,16},{21,... | collective-permute-start | bytes 27656 | tf_op jit(solution)/shard_map/ppermute | solution.py:20
  539.9 20.3 %collective-permute-start.33 = (f32[48,1,48]{2,0,1:T(8,128)S(1)}, f32[48,1,48]{2,0,1:T(8,128)S(1)}, u32[]{:S(2)}, u32[]{:S(2)}) collective-permute-start(f32[48,1,48]{2,0,1:T(8,128)S(1)} %get-tuple-element.100), channel_id=1, source_target_pairs={{0,4},{1,5},{2,6},{3,7},{8,12},{9,13},{10,14},{11,15},{16,20},{17,... | collective-permute-start | bytes 27656 | tf_op jit(solution)/shard_map/ppermute | solution.py:19
  547.2 16.4 %collective-permute-start.34 = (f32[48,96,1]{1,0,2:T(8,128)S(1)}, f32[48,96,1]{1,0,2:T(8,128)S(1)}, u32[]{:S(2)}, u32[]{:S(2)}) collective-permute-start(f32[48,96,1]{1,0,2:T(8,128)S(1)} %copy.287), channel_id=1, source_target_pairs={{8,0},{16,8},{24,16},{9,1},{17,9},{25,17},{10,2},{18,10},{26,18},{... | collective-permute-start | bytes 55304 | tf_op jit(solution)/shard_map/ppermute | solution.py:20
  551.0 14.9 %collective-permute-start.35 = (f32[48,96,1]{1,0,2:T(8,128)S(1)}, f32[48,96,1]{1,0,2:T(8,128)S(1)}, u32[]{:S(2)}, u32[]{:S(2)}) collective-permute-start(f32[48,96,1]{1,0,2:T(8,128)S(1)} %copy.289), channel_id=1, source_target_pairs={{0,8},{8,16},{16,24},{1,9},{9,17},{17,25},{2,10},{10,18},{18,26},{... | collective-permute-start | bytes 55304 | tf_op jit(solution)/shard_map/ppermute | solution.py:19
  555.6 17.0 %collective-permute-start.30 = (f32[1,96,48]{2,0,1:T(1,128)S(1)}, f32[1,96,48]{2,0,1:T(1,128)S(1)}, u32[]{:S(2)}, u32[]{:S(2)}) collective-permute-start(f32[1,96,48]{2,0,1:T(1,128)S(1)} %get-tuple-element.99), channel_id=1, source_target_pairs={{1,0},{2,1},{3,2},{5,4},{6,5},{7,6},{9,8},{10,9},{11,10},{13,12},{... | collective-permute-start | bytes 55304 | tf_op jit(solution)/shard_map/ppermute | solution.py:20
  556.9 15.7 %collective-permute-start.31 = (f32[1,96,48]{2,0,1:T(1,128)S(1)}, f32[1,96,48]{2,0,1:T(1,128)S(1)}, u32[]{:S(2)}, u32[]{:S(2)}) collective-permute-start(f32[1,96,48]{2,0,1:T(1,128)S(1)} %get-tuple-element.98), channel_id=1, source_target_pairs={{0,1},{1,2},{2,3},{4,5},{5,6},{6,7},{8,9},{9,10},{10,11},{12,13},{... | collective-permute-start | bytes 55304 | tf_op jit(solution)/shard_map/ppermute | solution.py:19
  674.5 18.3 %collective-permute-start.38 = (f32[48,1,48]{2,0,1:T(8,128)S(1)}, f32[48,1,48]{2,0,1:T(8,128)S(1)}, u32[]{:S(2)}, u32[]{:S(2)}) collective-permute-start(f32[48,1,48]{2,0,1:T(8,128)S(1)} %get-tuple-element.95), channel_id=1, source_target_pairs={{4,0},{5,1},{6,2},{7,3},{12,8},{13,9},{14,10},{15,11},{20,16},{21,... | collective-permute-start | bytes 27656 | tf_op jit(solution)/shard_map/ppermute | solution.py:20
  675.8 20.5 %collective-permute-start.39 = (f32[48,1,48]{2,0,1:T(8,128)S(1)}, f32[48,1,48]{2,0,1:T(8,128)S(1)}, u32[]{:S(2)}, u32[]{:S(2)}) collective-permute-start(f32[48,1,48]{2,0,1:T(8,128)S(1)} %get-tuple-element.94), channel_id=1, source_target_pairs={{0,4},{1,5},{2,6},{3,7},{8,12},{9,13},{10,14},{11,15},{16,20},{17,... | collective-permute-start | bytes 27656 | tf_op jit(solution)/shard_map/ppermute | solution.py:19
  683.2 16.6 %collective-permute-start.40 = (f32[48,96,1]{1,0,2:T(8,128)S(1)}, f32[48,96,1]{1,0,2:T(8,128)S(1)}, u32[]{:S(2)}, u32[]{:S(2)}) collective-permute-start(f32[48,96,1]{1,0,2:T(8,128)S(1)} %copy.291), channel_id=1, source_target_pairs={{8,0},{16,8},{24,16},{9,1},{17,9},{25,17},{10,2},{18,10},{26,18},{... | collective-permute-start | bytes 55304 | tf_op jit(solution)/shard_map/ppermute | solution.py:20
  687.0 15.0 %collective-permute-start.41 = (f32[48,96,1]{1,0,2:T(8,128)S(1)}, f32[48,96,1]{1,0,2:T(8,128)S(1)}, u32[]{:S(2)}, u32[]{:S(2)}) collective-permute-start(f32[48,96,1]{1,0,2:T(8,128)S(1)} %copy.293), channel_id=1, source_target_pairs={{0,8},{8,16},{16,24},{1,9},{9,17},{17,25},{2,10},{10,18},{18,26},{... | collective-permute-start | bytes 55304 | tf_op jit(solution)/shard_map/ppermute | solution.py:19
  691.5 17.1 %collective-permute-start.36 = (f32[1,96,48]{2,0,1:T(1,128)S(1)}, f32[1,96,48]{2,0,1:T(1,128)S(1)}, u32[]{:S(2)}, u32[]{:S(2)}) collective-permute-start(f32[1,96,48]{2,0,1:T(1,128)S(1)} %get-tuple-element.93), channel_id=1, source_target_pairs={{1,0},{2,1},{3,2},{5,4},{6,5},{7,6},{9,8},{10,9},{11,10},{13,12},{... | collective-permute-start | bytes 55304 | tf_op jit(solution)/shard_map/ppermute | solution.py:20
  692.9 15.8 %collective-permute-start.37 = (f32[1,96,48]{2,0,1:T(1,128)S(1)}, f32[1,96,48]{2,0,1:T(1,128)S(1)}, u32[]{:S(2)}, u32[]{:S(2)}) collective-permute-start(f32[1,96,48]{2,0,1:T(1,128)S(1)} %get-tuple-element.92), channel_id=1, source_target_pairs={{0,1},{1,2},{2,3},{4,5},{5,6},{6,7},{8,9},{9,10},{10,11},{12,13},{... | collective-permute-start | bytes 55304 | tf_op jit(solution)/shard_map/ppermute | solution.py:19
  810.7 18.3 %collective-permute-start.44 = (f32[48,1,48]{2,0,1:T(8,128)S(1)}, f32[48,1,48]{2,0,1:T(8,128)S(1)}, u32[]{:S(2)}, u32[]{:S(2)}) collective-permute-start(f32[48,1,48]{2,0,1:T(8,128)S(1)} %get-tuple-element.89), channel_id=1, source_target_pairs={{4,0},{5,1},{6,2},{7,3},{12,8},{13,9},{14,10},{15,11},{20,16},{21,... | collective-permute-start | bytes 27656 | tf_op jit(solution)/shard_map/ppermute | solution.py:20
  812.0 20.3 %collective-permute-start.45 = (f32[48,1,48]{2,0,1:T(8,128)S(1)}, f32[48,1,48]{2,0,1:T(8,128)S(1)}, u32[]{:S(2)}, u32[]{:S(2)}) collective-permute-start(f32[48,1,48]{2,0,1:T(8,128)S(1)} %get-tuple-element.88), channel_id=1, source_target_pairs={{0,4},{1,5},{2,6},{3,7},{8,12},{9,13},{10,14},{11,15},{16,20},{17,... | collective-permute-start | bytes 27656 | tf_op jit(solution)/shard_map/ppermute | solution.py:19
  819.3 16.3 %collective-permute-start.46 = (f32[48,96,1]{1,0,2:T(8,128)S(1)}, f32[48,96,1]{1,0,2:T(8,128)S(1)}, u32[]{:S(2)}, u32[]{:S(2)}) collective-permute-start(f32[48,96,1]{1,0,2:T(8,128)S(1)} %copy.295), channel_id=1, source_target_pairs={{8,0},{16,8},{24,16},{9,1},{17,9},{25,17},{10,2},{18,10},{26,18},{... | collective-permute-start | bytes 55304 | tf_op jit(solution)/shard_map/ppermute | solution.py:20
  823.1 14.8 %collective-permute-start.47 = (f32[48,96,1]{1,0,2:T(8,128)S(1)}, f32[48,96,1]{1,0,2:T(8,128)S(1)}, u32[]{:S(2)}, u32[]{:S(2)}) collective-permute-start(f32[48,96,1]{1,0,2:T(8,128)S(1)} %copy.297), channel_id=1, source_target_pairs={{0,8},{8,16},{16,24},{1,9},{9,17},{17,25},{2,10},{10,18},{18,26},{... | collective-permute-start | bytes 55304 | tf_op jit(solution)/shard_map/ppermute | solution.py:19
  827.7 16.9 %collective-permute-start.42 = (f32[1,96,48]{2,0,1:T(1,128)S(1)}, f32[1,96,48]{2,0,1:T(1,128)S(1)}, u32[]{:S(2)}, u32[]{:S(2)}) collective-permute-start(f32[1,96,48]{2,0,1:T(1,128)S(1)} %get-tuple-element.87), channel_id=1, source_target_pairs={{1,0},{2,1},{3,2},{5,4},{6,5},{7,6},{9,8},{10,9},{11,10},{13,12},{... | collective-permute-start | bytes 55304 | tf_op jit(solution)/shard_map/ppermute | solution.py:20
  829.0 15.6 %collective-permute-start.43 = (f32[1,96,48]{2,0,1:T(1,128)S(1)}, f32[1,96,48]{2,0,1:T(1,128)S(1)}, u32[]{:S(2)}, u32[]{:S(2)}) collective-permute-start(f32[1,96,48]{2,0,1:T(1,128)S(1)} %get-tuple-element.86), channel_id=1, source_target_pairs={{0,1},{1,2},{2,3},{4,5},{5,6},{6,7},{8,9},{9,10},{10,11},{12,13},{... | collective-permute-start | bytes 55304 | tf_op jit(solution)/shard_map/ppermute | solution.py:19
  946.5 18.4 %collective-permute-start.50 = (f32[48,1,48]{2,0,1:T(8,128)S(1)}, f32[48,1,48]{2,0,1:T(8,128)S(1)}, u32[]{:S(2)}, u32[]{:S(2)}) collective-permute-start(f32[48,1,48]{2,0,1:T(8,128)S(1)} %get-tuple-element.83), channel_id=1, source_target_pairs={{4,0},{5,1},{6,2},{7,3},{12,8},{13,9},{14,10},{15,11},{20,16},{21,... | collective-permute-start | bytes 27656 | tf_op jit(solution)/shard_map/ppermute | solution.py:20
  947.8 20.3 %collective-permute-start.51 = (f32[48,1,48]{2,0,1:T(8,128)S(1)}, f32[48,1,48]{2,0,1:T(8,128)S(1)}, u32[]{:S(2)}, u32[]{:S(2)}) collective-permute-start(f32[48,1,48]{2,0,1:T(8,128)S(1)} %get-tuple-element.82), channel_id=1, source_target_pairs={{0,4},{1,5},{2,6},{3,7},{8,12},{9,13},{10,14},{11,15},{16,20},{17,... | collective-permute-start | bytes 27656 | tf_op jit(solution)/shard_map/ppermute | solution.py:19
  955.1 16.4 %collective-permute-start.52 = (f32[48,96,1]{1,0,2:T(8,128)S(1)}, f32[48,96,1]{1,0,2:T(8,128)S(1)}, u32[]{:S(2)}, u32[]{:S(2)}) collective-permute-start(f32[48,96,1]{1,0,2:T(8,128)S(1)} %copy.299), channel_id=1, source_target_pairs={{8,0},{16,8},{24,16},{9,1},{17,9},{25,17},{10,2},{18,10},{26,18},{... | collective-permute-start | bytes 55304 | tf_op jit(solution)/shard_map/ppermute | solution.py:20
  959.0 14.9 %collective-permute-start.53 = (f32[48,96,1]{1,0,2:T(8,128)S(1)}, f32[48,96,1]{1,0,2:T(8,128)S(1)}, u32[]{:S(2)}, u32[]{:S(2)}) collective-permute-start(f32[48,96,1]{1,0,2:T(8,128)S(1)} %copy.301), channel_id=1, source_target_pairs={{0,8},{8,16},{16,24},{1,9},{9,17},{17,25},{2,10},{10,18},{18,26},{... | collective-permute-start | bytes 55304 | tf_op jit(solution)/shard_map/ppermute | solution.py:19
  963.6 16.9 %collective-permute-start.48 = (f32[1,96,48]{2,0,1:T(1,128)S(1)}, f32[1,96,48]{2,0,1:T(1,128)S(1)}, u32[]{:S(2)}, u32[]{:S(2)}) collective-permute-start(f32[1,96,48]{2,0,1:T(1,128)S(1)} %get-tuple-element.81), channel_id=1, source_target_pairs={{1,0},{2,1},{3,2},{5,4},{6,5},{7,6},{9,8},{10,9},{11,10},{13,12},{... | collective-permute-start | bytes 55304 | tf_op jit(solution)/shard_map/ppermute | solution.py:20
  964.9 15.6 %collective-permute-start.49 = (f32[1,96,48]{2,0,1:T(1,128)S(1)}, f32[1,96,48]{2,0,1:T(1,128)S(1)}, u32[]{:S(2)}, u32[]{:S(2)}) collective-permute-start(f32[1,96,48]{2,0,1:T(1,128)S(1)} %get-tuple-element.80), channel_id=1, source_target_pairs={{0,1},{1,2},{2,3},{4,5},{5,6},{6,7},{8,9},{9,10},{10,11},{12,13},{... | collective-permute-start | bytes 55304 | tf_op jit(solution)/shard_map/ppermute | solution.py:19
  1082.6 18.3 %collective-permute-start.56 = (f32[48,1,48]{2,0,1:T(8,128)S(1)}, f32[48,1,48]{2,0,1:T(8,128)S(1)}, u32[]{:S(2)}, u32[]{:S(2)}) collective-permute-start(f32[48,1,48]{2,0,1:T(8,128)S(1)} %get-tuple-element.77), channel_id=1, source_target_pairs={{4,0},{5,1},{6,2},{7,3},{12,8},{13,9},{14,10},{15,11},{20,16},{21,... | collective-permute-start | bytes 27656 | tf_op jit(solution)/shard_map/ppermute | solution.py:20
  1083.9 20.3 %collective-permute-start.57 = (f32[48,1,48]{2,0,1:T(8,128)S(1)}, f32[48,1,48]{2,0,1:T(8,128)S(1)}, u32[]{:S(2)}, u32[]{:S(2)}) collective-permute-start(f32[48,1,48]{2,0,1:T(8,128)S(1)} %get-tuple-element.76), channel_id=1, source_target_pairs={{0,4},{1,5},{2,6},{3,7},{8,12},{9,13},{10,14},{11,15},{16,20},{17,... | collective-permute-start | bytes 27656 | tf_op jit(solution)/shard_map/ppermute | solution.py:19
  1091.2 16.4 %collective-permute-start.58 = (f32[48,96,1]{1,0,2:T(8,128)S(1)}, f32[48,96,1]{1,0,2:T(8,128)S(1)}, u32[]{:S(2)}, u32[]{:S(2)}) collective-permute-start(f32[48,96,1]{1,0,2:T(8,128)S(1)} %copy.303), channel_id=1, source_target_pairs={{8,0},{16,8},{24,16},{9,1},{17,9},{25,17},{10,2},{18,10},{26,18},{... | collective-permute-start | bytes 55304 | tf_op jit(solution)/shard_map/ppermute | solution.py:20
  1095.1 14.9 %collective-permute-start.59 = (f32[48,96,1]{1,0,2:T(8,128)S(1)}, f32[48,96,1]{1,0,2:T(8,128)S(1)}, u32[]{:S(2)}, u32[]{:S(2)}) collective-permute-start(f32[48,96,1]{1,0,2:T(8,128)S(1)} %copy.305), channel_id=1, source_target_pairs={{0,8},{8,16},{16,24},{1,9},{9,17},{17,25},{2,10},{10,18},{18,26},{... | collective-permute-start | bytes 55304 | tf_op jit(solution)/shard_map/ppermute | solution.py:19
  1099.7 17.0 %collective-permute-start.54 = (f32[1,96,48]{2,0,1:T(1,128)S(1)}, f32[1,96,48]{2,0,1:T(1,128)S(1)}, u32[]{:S(2)}, u32[]{:S(2)}) collective-permute-start(f32[1,96,48]{2,0,1:T(1,128)S(1)} %get-tuple-element.75), channel_id=1, source_target_pairs={{1,0},{2,1},{3,2},{5,4},{6,5},{7,6},{9,8},{10,9},{11,10},{13,12},{... | collective-permute-start | bytes 55304 | tf_op jit(solution)/shard_map/ppermute | solution.py:20
  1101.0 15.7 %collective-permute-start.55 = (f32[1,96,48]{2,0,1:T(1,128)S(1)}, f32[1,96,48]{2,0,1:T(1,128)S(1)}, u32[]{:S(2)}, u32[]{:S(2)}) collective-permute-start(f32[1,96,48]{2,0,1:T(1,128)S(1)} %get-tuple-element.74), channel_id=1, source_target_pairs={{0,1},{1,2},{2,3},{4,5},{5,6},{6,7},{8,9},{9,10},{10,11},{12,13},{... | collective-permute-start | bytes 55304 | tf_op jit(solution)/shard_map/ppermute | solution.py:19
  1119.9 44.8 %copy-start.6 = (f32[48,96,48]{2,0,1:T(8,128)S(1)}, f32[48,96,48]{2,0,1:T(8,128)}, u32[]{:S(2)}) copy-start(f32[48,96,48]{2,0,1:T(8,128)} %copy-done.3) | copy-start | bytes 2654212
  (40 other events, 330.2 us)
where the time goes:
time: 1240 us; the launch traced here: 1230 us
  blocking collectives  643 us (52%)
  other arithmetic  226 us (18%)
  local copies, waits for them, and re-layouts  175 us (14%)
  starting transfers between devices  166 us (13%)
  between operations  22.6 us (2%)
    psum x16, blocking collectives, global_sum(): return lax.psum(local_value, MESH_AXES)  643 us
    ppermute x30, starting transfers between devices, neighbour_layers(): from_below = lax.ppermute(top_layer, GRID_AXES[axis_dim], upward)  127 us
    mul x27, other arithmetic, apply_operator(): face_coefs[axis_dim]  100 us
    reduce_sum x8, other arithmetic, local_solve(): jnp.sum(residual * precond)  51 us
    slice x37, local copies, waits for them, and re-layouts, neighbour_layers(): lax.slice_in_dim(grid_field, size_here - 1, size_here, axis=axis_dim)  50 us
    ppermute x30, starting transfers between devices, neighbour_layers(): from_above = lax.ppermute(low_layer, GRID_AXES[axis_dim], downward)  39 us
    reduce_sum x8, other arithmetic, local_solve(): step_alpha = rz_old / global_sum(jnp.sum(direction * q_vec))  25.7 us
  transfers between devices with their start and end apart: 60, of which 1 were waited for; matrix products, arithmetic and copies ran while one was open for 17% of the time, Pallas kernels for 0%

commit v1 on v0

v1 whole, which is shorter than its diff:
```python
import functools

import jax
import jax.numpy as jnp
from jax import lax
from jax.experimental import pallas as pl
from jax.experimental.pallas import tpu as pltpu
from jax.sharding import PartitionSpec as P

CG_ITERS = 8
LANES = 128
PAD = 8
MESH = pl.DeviceIdType.MESH
F32 = jnp.float32


def solve_kernel(dims, counts, kg_ref, k_ref, f_ref, u_ref, x_out, r_out, hist_ref,
                 kp, mp, cx, cy, cz, inv, x, r, w, s, z, p, n,
                 ys, zs, xr, yr, zr, red_s, red_r,
                 xs_sem, ys_sem, zs_sem, xr_sem, yr_sem, zr_sem, rs_sem, rr_sem):
    ni, nl, nj = dims
    ngx, ngy, ngz = counts
    gx, gy, gz = lax.axis_index('gx'), lax.axis_index('gy'), lax.axis_index('gz')
    rows = pl.ds(PAD, nl)
    rows_dn = pl.ds(PAD - 1, nl)
    rows_up = pl.ds(PAD + 1, nl)
    lane = lax.broadcasted_iota(jnp.int32, (nl, LANES), 1)
    lane_row = lax.broadcasted_iota(jnp.int32, (1, LANES), 1)
    inside = lane < nj
    has_xlo, has_xhi = gx > 0, gx < ngx - 1
    has_zlo, has_zhi = gz > 0, gz < ngz - 1
    face_lane = jnp.where(gy == 0, nj - 1, 0)
    halo_lane = jnp.where(gy == 0, nj, LANES - 1)
    wall_lane = jnp.where(gy == 0, LANES - 1, nj)

    def x_copy(ref, slot, up):
        src = ref.at[ni if up else 1, rows]
        return pltpu.make_async_remote_copy(
            src_ref=src, dst_ref=xr.at[slot, 0 if up else 1], send_sem=xs_sem.at[slot, 0 if up else 1],
            recv_sem=xr_sem.at[slot, 0 if up else 1], device_id=(gz, gy, gx + 1 if up else gx - 1), device_id_type=MESH)

    def z_copy(slot, up):
        return pltpu.make_async_remote_copy(
            src_ref=zs.at[slot, 0 if up else 1], dst_ref=zr.at[slot, 0 if up else 1],
            send_sem=zs_sem.at[slot, 0 if up else 1], recv_sem=zr_sem.at[slot, 0 if up else 1],
            device_id=(gz + 1 if up else gz - 1, gy, gx), device_id_type=MESH)

    def y_copy(slot):
        return pltpu.make_async_remote_copy(
            src_ref=ys.at[slot], dst_ref=yr.at[slot], send_sem=ys_sem.at[slot], recv_sem=yr_sem.at[slot],
            device_id=(gz, 1 - gy, gx), device_id_type=MESH)

    def exchange_start(ref, slot):
        pl.when(has_xlo)(lambda: x_copy(ref, slot, False).start())
        pl.when(has_xhi)(lambda: x_copy(ref, slot, True).start())

        def pack(i, acc):
            slab = ref[i + 1, rows, :]
            zs[slot, 1, pl.ds(i, 1), :] = slab[0:1, :]
            zs[slot, 0, pl.ds(i, 1), :] = slab[nl - 1:nl, :]
            shift = lax.rem(i - face_lane + LANES, LANES)
            return jnp.where(lane == i, pltpu.roll(slab, shift, 1), acc)

        ys[slot] = lax.fori_loop(0, ni, pack, jnp.zeros((nl, LANES), F32))
        pl.when(has_zlo)(lambda: z_copy(slot, False).start())
        pl.when(has_zhi)(lambda: z_copy(slot, True).start())
        y_copy(slot).start()

    def exchange_wait(ref, slot):
        @pl.when(has_xlo)
        def _():
            x_copy(ref, slot, False).wait_send()
            x_copy(ref, slot, True).wait_recv()
            ref[0, rows, :] = xr[slot, 0]

        @pl.when(has_xhi)
        def _():
            x_copy(ref, slot, True).wait_send()
            x_copy(ref, slot, False).wait_recv()
            ref[ni + 1, rows, :] = xr[slot, 1]

        @pl.when(has_zlo)
        def _():
            z_copy(slot, False).wait_send()
            z_copy(slot, True).wait_recv()
            for i in range(ni):
                ref[i + 1, PAD - 1:PAD, :] = zr[slot, 0, i:i + 1, :]

        @pl.when(has_zhi)
        def _():
            z_copy(slot, True).wait_send()
            z_copy(slot, False).wait_recv()
            for i in range(ni):
                ref[i + 1, PAD + nl:PAD + nl + 1, :] = zr[slot, 1, i:i + 1, :]

        y_copy(slot).wait()

    def put_lane(slab, column, i, target):
        return jnp.where(lane == target, pltpu.roll(column, lax.rem(target - i + LANES, LANES), 1), slab)

    def stencil(ref, slot, emit, init):
        halo = yr[slot]
        below = ref[0, rows, :]
        first = ref[1, rows, :]

        def step(i, carry):
            v, flux_x, state = carry
            above = ref[i + 2, rows, :]
            flux_next = cx[i + 1] * (above - v)
            flux_zl = cz[i, rows, :] * (v - ref[i + 1, rows_dn, :])
            flux_zh = cz[i, rows_up, :] * (ref[i + 1, rows_up, :] - v)
            vy = put_lane(v, halo, i, halo_lane)
            flux_y = cy[i] * (vy - pltpu.roll(vy, 1, 1))
            total = (flux_x - flux_next) + (flux_y - pltpu.roll(flux_y, LANES - 1, 1)) + (flux_zl - flux_zh)
            state = emit(i, jnp.where(inside, total, 0.0), v, state)
            return above, flux_next, state

        return lax.fori_loop(0, ni, step, (first, cx[0] * (first - below), init))[2]

    def fold(slab):
        out = slab[0:8]
        for part in range(8, nl, 8):
            out = out + slab[part:part + 8]
        return out

    def reduce_start(slot, accs):
        row = jnp.zeros((1, LANES), F32)
        for q, acc in enumerate(accs):
            row = jnp.where(lane_row == q, jnp.sum(jnp.sum(acc, axis=0, keepdims=True), axis=1, keepdims=True), row)
        me = (gz * ngy + gy) * ngx + gx
        red_s[slot] = row
        red_r[slot, me] = row
        for a in reversed(range(ngz)):
            for b in reversed(range(ngy)):
                for c in reversed(range(ngx)):
                    if a or b or c:
                        tgt = (lax.rem(gz + a, ngz), lax.rem(gy + b, ngy), lax.rem(gx + c, ngx))
                        pltpu.make_async_remote_copy(
                            src_ref=red_s.at[slot], dst_ref=red_r.at[slot, me], send_sem=rs_sem.at[slot],
                            recv_sem=rr_sem.at[slot], device_id=tgt, device_id_type=MESH).start()

    def reduce_wait(slot, count):
        others = ngx * ngy * ngz - 1
        whole = red_r.at[slot, pl.ds(0, others)]
        done = pltpu.make_async_remote_copy(
            src_ref=whole, dst_ref=whole, send_sem=rs_sem.at[slot], recv_sem=rr_sem.at[slot],
            device_id=(gz, gy, gx), device_id_type=MESH)
        done.wait_recv()
        done.wait_send()
        total = jnp.sum(red_r[slot], axis=0)
        return [jnp.sum(jnp.where(lane_row == q, total, 0.0), axis=1, keepdims=True) for q in range(count)]

    zero_slab = jnp.zeros((nl, LANES), F32)
    zero_acc = jnp.zeros((8, LANES), F32)

    def load(i, _):
        kp[i + 1, rows, :] = jnp.full((nl, LANES), 1.0, F32)
        kp[i + 1, rows, 0:nj] = k_ref[i]
        kp[i + 1, pl.ds(0, PAD), :] = jnp.ones((PAD, LANES), F32)
        kp[i + 1, pl.ds(PAD + nl, PAD), :] = jnp.ones((PAD, LANES), F32)
        mp[i + 1, rows, :] = zero_slab
        mp[i + 1, rows, 0:nj] = u_ref[i]
        mp[i + 1, pl.ds(0, PAD), :] = jnp.zeros((PAD, LANES), F32)
        mp[i + 1, pl.ds(PAD + nl, PAD), :] = jnp.zeros((PAD, LANES), F32)
        s[i] = zero_slab
        z[i] = zero_slab
        p[i] = zero_slab
        return 0

    lax.fori_loop(0, ni, load, 0)
    for edge in (0, ni + 1):
        mp[edge] = jnp.zeros((nl + 2 * PAD, LANES), F32)
        kp[edge] = jnp.ones((nl + 2 * PAD, LANES), F32)
    exchange_start(kp, 0)
    exchange_start(mp, 1)

    @pl.when(gx == 0)
    def _():
        kp[0, rows, 0:nj] = kg_ref[0, :, 0:nj]

    @pl.when(gx == ngx - 1)
    def _():
        kp[ni + 1, rows, 0:nj] = kg_ref[0, :, 0:nj]

    @pl.when(gz == 0)
    def _():
        for i in range(ni):
            kp[i + 1, PAD - 1:PAD, 0:nj] = kg_ref[2, i:i + 1, 0:nj]

    @pl.when(gz == ngz - 1)
    def _():
        for i in range(ni):
            kp[i + 1, PAD + nl:PAD + nl + 1, 0:nj] = kg_ref[2, i:i + 1, 0:nj]

    exchange_wait(kp, 0)
    wall_y = kg_ref[1, 0:nl, :]
    halo_y = yr[0]

    def harmonic(left, right):
        return 2.0 * left * right / (left + right)

    cx[0] = jnp.where(inside, harmonic(kp[0, rows, :], kp[1, rows, :]), 0.0)

    def coefs(i, _):
        here = kp[i + 1, rows, :]
        x_hi = jnp.where(inside, harmonic(here, kp[i + 2, rows, :]), 0.0)
        cx[i + 1] = x_hi
        z_lo = jnp.where(inside, harmonic(kp[i + 1, rows_dn, :], here), 0.0)
        z_hi = jnp.where(inside, harmonic(here, kp[i + 1, rows_up, :]), 0.0)
        cz[i, rows, :] = z_lo
        cz[i, pl.ds(PAD + nl, 1), :] = z_hi[nl - 1:nl, :]
        ky = put_lane(put_lane(here, halo_y, i, halo_lane), wall_y, i, wall_lane)
        y_lo = jnp.where(lane <= nj, harmonic(pltpu.roll(ky, 1, 1), ky), 0.0)
        cy[i] = y_lo
        diag = cx[i] + x_hi + y_lo + pltpu.roll(y_lo, LANES - 1, 1) + z_lo + z_hi
        inv[i] = jnp.where(inside, 1.0 / jnp.where(inside, diag, 1.0), 0.0)
        return 0

    lax.fori_loop(0, ni, coefs, 0)
    exchange_wait(mp, 1)

    def first_residual(i, av, v, acc):
        x[i] = v
        r[i] = zero_slab
        r[i, :, 0:nj] = f_ref[i]
        res = r[i] - av
        r[i] = res
        u = res * inv[i]
        n[i] = u
        return (acc[0] + fold(res * u),)

    (gamma_acc,) = stencil(mp, 1, first_residual, (zero_acc,))

    def copy_u(i, _):
        mp[i + 1, rows, :] = n[i]
        return 0

    lax.fori_loop(0, ni, copy_u, 0)
    exchange_start(mp, 2)
    exchange_wait(mp, 2)

    def first_w(i, av, v, acc):
        w[i] = av
        n[i] = av * inv[i]
        return (acc[0] + fold(av * v),)

    (delta_acc,) = stencil(mp, 2, first_w, (zero_acc,))
    lax.fori_loop(0, ni, copy_u, 0)

    def scalars(t, sums, gamma_old, pap_old):
        gamma, delta, sigma = sums[0], sums[1], sums[2]
        beta = jnp.where(t == 0, 0.0, gamma / gamma_old)
        pap = delta + 2.0 * beta * sigma + beta * beta * pap_old
        return gamma, pap, beta, gamma / pap

    def advance_x(alpha):
        def step(i, _):
            x[i] = x[i] + alpha * p[i]
            return 0
        lax.fori_loop(0, ni, step, 0)

    def iteration(t, carry):
        accs, gamma_old, pap_old, alpha_old = carry
        reduce_start(t, accs)
        exchange_start(mp, t + 3)
        advance_x(alpha_old)
        exchange_wait(mp, t + 3)

        def store_n(i, av, v, state):
            n[i] = av
            return state

        stencil(mp, t + 3, store_n, 0)
        sums = reduce_wait(t, 4)

        @pl.when(t > 0)
        def _():
            hist_ref[lax.max(t - 1, 0)] = sums[3][0, 0]

        gamma, pap, beta_v, alpha_v = scalars(t, sums, gamma_old, pap_old)
        beta, alpha = beta_v[0, 0], alpha_v[0, 0]

        def update(i, acc):
            iv, r_old, w_old = inv[i], r[i], w[i]
            z_new = n[i] + beta * z[i]
            s_new = w_old + beta * s[i]
            p[i] = iv * r_old + beta * p[i]
            r_new = r_old - alpha * s_new
            w_new = w_old - alpha * z_new
            u_new = iv * r_new
            z[i] = z_new
            s[i] = s_new
            r[i] = r_new
            w[i] = w_new
            mp[i + 1, rows, :] = iv * w_new
            return (acc[0] + fold(r_new * u_new), acc[1] + fold(w_new * u_new),
                    acc[2] + fold(u_new * s_new), acc[3] + fold(r_new * r_new))

        accs = lax.fori_loop(0, ni, update, (zero_acc,) * 4)
        return accs, gamma, pap, alpha

    one = jnp.ones((1, 1), F32)
    accs, gamma_old, pap_old, alpha_old = lax.fori_loop(
        0, CG_ITERS - 1, iteration, ((gamma_acc, delta_acc, zero_acc, zero_acc), one, one, jnp.float32(0.0)))

    last = CG_ITERS - 1
    reduce_start(last, accs)
    advance_x(alpha_old)
    sums = reduce_wait(last, 4)
    hist_ref[last - 1] = sums[3][0, 0]
    _, _, beta_v, alpha_v = scalars(last, sums, gamma_old, pap_old)
    beta, alpha = beta_v[0, 0], alpha_v[0, 0]

    def final(i, acc):
        r_old = r[i]
        s_new = w[i] + beta * s[i]
        p_new = inv[i] * r_old + beta * p[i]
        r_new = r_old - alpha * s_new
        x_new = x[i] + alpha * p_new
        x_out[i] = x_new[:, 0:nj]
        r_out[i] = r_new[:, 0:nj]
        return acc + fold(r_new * r_new)

    acc = lax.fori_loop(0, ni, final, zero_acc)
    reduce_start(CG_ITERS, (acc,))
    hist_ref[last] = reduce_wait(CG_ITERS, 1)[0][0, 0]


def solution(mesh):
    counts = (mesh.shape['gx'], mesh.shape['gy'], mesh.shape['gz'])
    grid_spec = P('gx', 'gy', 'gz')

    def local_solve(k_cell, k_ghost, f_rhs, u_init):
        ni, nj, nl = k_cell.shape
        ngx, ngy, ngz = counts
        gx, gy, gz = lax.axis_index('gx'), lax.axis_index('gy'), lax.axis_index('gz')
        pad_to = lambda a: jnp.pad(a, ((0, max(ni, nl) - a.shape[0]), (0, LANES - a.shape[1])), constant_values=1.0)
        wall = lambda row, start, extent: lax.dynamic_slice(k_ghost, (row,) + start, (1,) + extent)[0]
        wall_x = wall(jnp.where(gx == 0, 0, 1), (gy * nj, gz * nl), (nj, nl)).T
        wall_y = wall(2 + gy, (gx * ni, gz * nl), (ni, nl)).T
        wall_z = wall(jnp.where(gz == 0, 4, 5), (gx * ni, gy * nj), (ni, nj))
        walls = jnp.stack([pad_to(wall_x), pad_to(wall_y), pad_to(wall_z)])
        flip = lambda a: jnp.swapaxes(a, 1, 2)

        slots = CG_ITERS + 2
        whole = (ni, nl, LANES)
        padded = (ni + 2, nl + 2 * PAD, LANES)
        dma = pltpu.SemaphoreType.DMA
        devices = ngx * ngy * ngz
        vmem = pl.BlockSpec(memory_space=pltpu.VMEM)
        out_block = jax.ShapeDtypeStruct((ni, nl, nj), F32)
        x_new, r_new, hist = pl.pallas_call(
            functools.partial(solve_kernel, (ni, nl, nj), counts),
            out_shape=(out_block, out_block, jax.ShapeDtypeStruct((CG_ITERS,), F32)),
            in_specs=[vmem] * 4,
            out_specs=(vmem, vmem, pl.BlockSpec(memory_space=pltpu.SMEM)),
            scratch_shapes=[
                pltpu.VMEM(padded, F32), pltpu.VMEM(padded, F32),
                pltpu.VMEM((ni + 1, nl, LANES), F32), pltpu.VMEM(whole, F32), pltpu.VMEM((ni, nl + 2 * PAD, LANES), F32),
                pltpu.VMEM(whole, F32),
                pltpu.VMEM(whole, F32), pltpu.VMEM(whole, F32), pltpu.VMEM(whole, F32), pltpu.VMEM(whole, F32),
                pltpu.VMEM(whole, F32), pltpu.VMEM(whole, F32), pltpu.VMEM(whole, F32),
                pltpu.VMEM((slots, nl, LANES), F32), pltpu.VMEM((slots, 2, ni, LANES), F32),
                pltpu.VMEM((slots, 2, nl, LANES), F32), pltpu.VMEM((slots, nl, LANES), F32), pltpu.VMEM((slots, 2, ni, LANES), F32),
                pltpu.VMEM((CG_ITERS + 1, 1, LANES), F32), pltpu.VMEM((CG_ITERS + 1, devices, 1, LANES), F32),
                dma((slots, 2)), dma((slots,)), dma((slots, 2)), dma((slots, 2)), dma((slots,)), dma((slots, 2)),
                dma((CG_ITERS + 1,)), dma((CG_ITERS + 1,)),
            ],
            compiler_params=pltpu.CompilerParams(has_side_effects=True),
        )(walls, flip(k_cell), flip(f_rhs), flip(u_init))
        return flip(x_new), flip(r_new), hist

    return jax.shard_map(local_solve, mesh=mesh, in_specs=(grid_spec, P(), grid_spec, grid_spec),
                         out_specs=(grid_spec, grid_spec, P()), check_vma=False)
```

time: 1240 us -> 212 us (0.17)
  blocking collectives: 643 us -> 0 us
  other arithmetic: 226 us -> 0.65 us
  Pallas kernels: 0 us -> 203 us
  local copies, waits for them, and re-layouts: 175 us -> 6.9 us
  starting transfers between devices: 166 us -> 0 us
  between operations: 22.6 us -> 0.69 us
    psum x16 -> x0, blocking collectives: 643 us -> none  [global_sum(): return lax.psum(local_value, MESH_AXES)]
    pallas_call x0 -> x1, Pallas kernels: none -> 203 us  [local_solve(): pl.pallas_call(functools.partial(solve_kernel, (ni, nl, nj), counts), out...]
    ppermute x60 -> x0, starting transfers between devices: 166 us -> none  [the longest x30 127 us: neighbour_layers(): from_below = lax.ppermute(top_layer, GRID_AXES[axis_dim], upward)]
    mul x28 -> x0, other arithmetic: 107 us -> none  [the longest x27 100 us: apply_operator(): face_coefs[axis_dim]]
    slice x55 -> x0, local copies, waits for them, and re-layouts: 79.8 us -> none  [the longest x37 50 us: neighbour_layers(): lax.slice_in_dim(grid_field, size_here - 1, size_here, axis=axis_dim)]
    reduce_sum x16 -> x0, other arithmetic: 76.7 us -> none  [the longest x8 51 us: local_solve(): jnp.sum(residual * precond)]
    ppermute x18 -> x0, local copies, waits for them, and re-layouts: 42.6 us -> none  [the longest x9 21.3 us: neighbour_layers(): from_above = lax.ppermute(low_layer, GRID_AXES[axis_dim], downward)]
    add x8 -> x0, other arithmetic: 22.9 us -> none  [the longest x7 13.7 us: local_solve(): direction = precond + pair_sums[0] / rz_old * direction]
  transfers between devices with their start and end apart: 60 -> 0, of which waited for: 1 -> 0; matrix products, arithmetic and copies ran while one was open for 17% -> 0% of each run, Pallas kernels for 0% -> 0%
where the time goes in v1:
time: 212 us; the launch traced here: 211 us
  Pallas kernels  203 us (96%)
  local copies, waits for them, and re-layouts  6.9 us (3%)
    pallas_call x1, Pallas kernels, local_solve(): pl.pallas_call(functools.partial(solve_kernel, (ni, nl, nj), counts), out...  203 us

profile of v1, /device:TPU:0, one launch (start us, length us, event | category | flops | bytes accessed | tf_op | source)
XLA Modules:
  0.0 211.4 jit_solution(7342415090342271876)
XLA Ops:
  0.6 0.9 dynamic-slice_bitcast_fusion
  1.5 0.9 dynamic_slice.10
  2.4 0.1 copy.8
  2.5 1.0 dynamic_slice.9
  3.5 0.1 copy.7
  3.6 0.6 pad_maximum_fusion.kg_ref
  4.2 203.2 %shard_map.67 = (f32[48,48,96]{2,1,0:T(8,128)}, f32[48,48,96]{2,1,0:T(8,128)}, f32[8]{0:T(128)}) custom-call(f32[3,48,128]{2,1,0:T(8,128)} %pad_maximum_fusion.kg_ref, f32[48,48,96]{2,1,0:T(8,128)} %bitcast.19, f32[48,48,96]{2,1,0:T(8,128)} %bitcast.20, f32[48,48,96]{2,1,0:T(8,128)} %bitcast.21), custom_call_target="tpu_custom_call" | custom-call | tf_op jit(solution)/shard_map/pallas_call | solution.py:352
  207.4 0.0 copy-start
  207.4 2.5 %copy.12 = f32[48,96,48]{1,2,0:T(8,128)} copy(f32[48,96,48]{1,2,0:T(8,128)} %bitcast.23) | data formatting | bytes 1769472
  209.9 0.0 copy-done
  209.9 0.0 copy-start.1
  209.9 1.0 copy.13
  210.9 0.0 copy-done.1
  210.9 0.5 copy.14
  (2 shorter events, 0.0 us)
Async XLA Ops:
  207.4 2.5 %copy-start = (f32[48,48,96]{2,1,0:T(8,128)S(1)}, f32[48,48,96]{2,1,0:T(8,128)}, u32[]{:S(2)}) copy-start(f32[48,48,96]{2,1,0:T(8,128)} %get-tuple-element.7) | copy-start | bytes 2654212
  209.9 1.0 copy-start.1

commit v2 on v1

--- a/solution.py
+++ b/solution.py
@@ -15,7 +15,7 @@
 
 
 def solve_kernel(dims, counts, kg_ref, k_ref, f_ref, u_ref, x_out, r_out, hist_ref,
-                 kp, mp, cx, cy, cz, inv, x, r, w, s, z, p, n,
+                 kp, mp, cx, cy, cyh, cz, inv, x, r, w, s, z, p, n,
                  ys, zs, xr, yr, zr, red_s, red_r,
                  xs_sem, ys_sem, zs_sem, xr_sem, yr_sem, zr_sem, rs_sem, rr_sem):
     ni, nl, nj = dims
@@ -30,8 +30,16 @@
     has_xlo, has_xhi = gx > 0, gx < ngx - 1
     has_zlo, has_zhi = gz > 0, gz < ngz - 1
     face_lane = jnp.where(gy == 0, nj - 1, 0)
-    halo_lane = jnp.where(gy == 0, nj, LANES - 1)
-    wall_lane = jnp.where(gy == 0, LANES - 1, nj)
+
+    def column_roll(slab, shift):
+        return pltpu.roll(slab, lax.rem(shift + LANES, LANES), 1)
+
+    def slabs(group, step, init):
+        def body(g, carry):
+            for k in range(group):
+                carry = step(g * group + k, carry)
+            return carry
+        return lax.fori_loop(0, ni // group, body, init)
 
     def x_copy(ref, slot, up):
         src = ref.at[ni if up else 1, rows]
@@ -58,10 +66,9 @@
             slab = ref[i + 1, rows, :]
             zs[slot, 1, pl.ds(i, 1), :] = slab[0:1, :]
             zs[slot, 0, pl.ds(i, 1), :] = slab[nl - 1:nl, :]
-            shift = lax.rem(i - face_lane + LANES, LANES)
-            return jnp.where(lane == i, pltpu.roll(slab, shift, 1), acc)
-
-        ys[slot] = lax.fori_loop(0, ni, pack, jnp.zeros((nl, LANES), F32))
+            return jnp.where(lane == i, column_roll(slab, i - face_lane), acc)
+
+        ys[slot] = slabs(8, pack, jnp.zeros((nl, LANES), F32))
         pl.when(has_zlo)(lambda: z_copy(slot, False).start())
         pl.when(has_zhi)(lambda: z_copy(slot, True).start())
         y_copy(slot).start()
@@ -95,12 +102,16 @@
 
         y_copy(slot).wait()
 
-    def put_lane(slab, column, i, target):
-        return jnp.where(lane == target, pltpu.roll(column, lax.rem(target - i + LANES, LANES), 1), slab)
+    def y_sides(slab, below, above, i):
+        low = jnp.where(lane == 0, column_roll(below, -i), pltpu.roll(slab, 1, 1))
+        high = jnp.where(lane == nj - 1, column_roll(above, nj - 1 - i), pltpu.roll(slab, LANES - 1, 1))
+        return low, high
 
     def stencil(ref, slot, emit, init):
         halo = yr[slot]
         below = ref[0, rows, :]
+        lane_lo = jnp.where(gy == 0, -1, 0)
+        lane_hi = jnp.where(gy == 0, nj - 1, -1)
         first = ref[1, rows, :]
 
         def step(i, carry):
@@ -109,13 +120,16 @@
             flux_next = cx[i + 1] * (above - v)
             flux_zl = cz[i, rows, :] * (v - ref[i + 1, rows_dn, :])
             flux_zh = cz[i, rows_up, :] * (ref[i + 1, rows_up, :] - v)
-            vy = put_lane(v, halo, i, halo_lane)
-            flux_y = cy[i] * (vy - pltpu.roll(vy, 1, 1))
-            total = (flux_x - flux_next) + (flux_y - pltpu.roll(flux_y, LANES - 1, 1)) + (flux_zl - flux_zh)
-            state = emit(i, jnp.where(inside, total, 0.0), v, state)
+            column = column_roll(halo, face_lane - i)
+            low = jnp.where(lane == lane_lo, column, pltpu.roll(v, 1, 1))
+            high = jnp.where(lane == lane_hi, column, pltpu.roll(v, LANES - 1, 1))
+            flux_yl = cy[i] * (v - low)
+            flux_yh = cyh[i] * (high - v)
+            total = (flux_x - flux_next) + (flux_yl - flux_yh) + (flux_zl - flux_zh)
+            state = emit(i, total, v, state)
             return above, flux_next, state
 
-        return lax.fori_loop(0, ni, step, (first, cx[0] * (first - below), init))[2]
+        return slabs(4, step, (first, cx[0] * (first - below), init))[2]
 
     def fold(slab):
         out = slab[0:8]
@@ -193,8 +207,8 @@
             kp[i + 1, PAD + nl:PAD + nl + 1, 0:nj] = kg_ref[2, i:i + 1, 0:nj]
 
     exchange_wait(kp, 0)
-    wall_y = kg_ref[1, 0:nl, :]
-    halo_y = yr[0]
+    y_below = jnp.where(gy == 0, kg_ref[1, 0:nl, :], yr[0])
+    y_above = jnp.where(gy == 0, yr[0], kg_ref[1, 0:nl, :])
 
     def harmonic(left, right):
         return 2.0 * left * right / (left + right)
@@ -209,14 +223,16 @@
         z_hi = jnp.where(inside, harmonic(here, kp[i + 1, rows_up, :]), 0.0)
         cz[i, rows, :] = z_lo
         cz[i, pl.ds(PAD + nl, 1), :] = z_hi[nl - 1:nl, :]
-        ky = put_lane(put_lane(here, halo_y, i, halo_lane), wall_y, i, wall_lane)
-        y_lo = jnp.where(lane <= nj, harmonic(pltpu.roll(ky, 1, 1), ky), 0.0)
+        low, high = y_sides(here, y_below, y_above, i)
+        y_lo = jnp.where(inside, harmonic(low, here), 0.0)
+        y_hi = jnp.where(inside, harmonic(here, high), 0.0)
         cy[i] = y_lo
-        diag = cx[i] + x_hi + y_lo + pltpu.roll(y_lo, LANES - 1, 1) + z_lo + z_hi
+        cyh[i] = y_hi
+        diag = cx[i] + x_hi + y_lo + y_hi + z_lo + z_hi
         inv[i] = jnp.where(inside, 1.0 / jnp.where(inside, diag, 1.0), 0.0)
         return 0
 
-    lax.fori_loop(0, ni, coefs, 0)
+    slabs(4, coefs, 0)
     exchange_wait(mp, 1)
 
     def first_residual(i, av, v, acc):
@@ -356,7 +372,7 @@
             out_specs=(vmem, vmem, pl.BlockSpec(memory_space=pltpu.SMEM)),
             scratch_shapes=[
                 pltpu.VMEM(padded, F32), pltpu.VMEM(padded, F32),
-                pltpu.VMEM((ni + 1, nl, LANES), F32), pltpu.VMEM(whole, F32), pltpu.VMEM((ni, nl + 2 * PAD, LANES), F32),
+                pltpu.VMEM((ni + 1, nl, LANES), F32), pltpu.VMEM(whole, F32), pltpu.VMEM(whole, F32), pltpu.VMEM((ni, nl + 2 * PAD, LANES), F32),
                 pltpu.VMEM(whole, F32),
                 pltpu.VMEM(whole, F32), pltpu.VMEM(whole, F32), pltpu.VMEM(whole, F32), pltpu.VMEM(whole, F32),
                 pltpu.VMEM(whole, F32), pltpu.VMEM(whole, F32), pltpu.VMEM(whole, F32),

time: 212 us -> 98.6 us (0.47)
  Pallas kernels: 203 us -> 90.1 us
    pallas_call x1, Pallas kernels: 203 us -> 90.1 us  [local_solve(): pl.pallas_call(functools.partial(solve_kernel, (ni, nl, nj), counts), out...]
where the time goes in v2:
time: 98.6 us; the launch traced here: 98.3 us
  Pallas kernels  90.1 us (91%)
  local copies, waits for them, and re-layouts  6.9 us (7%)
    pallas_call x1, Pallas kernels, local_solve(): pl.pallas_call(functools.partial(solve_kernel, (ni, nl, nj), counts), out...  90.1 us
    unnamed x7, local copies, waits for them, and re-layouts  3.99 us
    dynamic_slice x4, local copies, waits for them, and re-layouts, local_solve(): lax.dynamic_slice(k_ghost, (row,) + start, (1,) + extent)[0]  2 us

profile of v2, /device:TPU:0, one launch (start us, length us, event | category | flops | bytes accessed | tf_op | source)
XLA Modules:
  0.0 98.3 jit_solution(14988142637173544755)
XLA Ops:
  0.6 0.9 dynamic-slice_bitcast_fusion
  1.5 0.9 dynamic_slice.10
  2.4 0.1 copy.8
  2.5 1.0 %dynamic_slice.9 = f32[1,96,48]{2,1,0:T(8,128)S(1)} dynamic-slice(f32[6,192,192]{2,1,0:T(8,128)} %param.5, s32[]{:T(128)S(6)} %select_n.24, s32[]{:T(128)S(6)} %select_n.25, s32[]{:T(128)S(6)} %select_n.26), dynamic_slice_sizes={1,96,48} | dynamic-slice | bytes 36868 | tf_op jit(solution)/shard_map/dynamic_slice | solution.py:354
  3.5 0.1 copy.7
  3.6 0.6 pad_maximum_fusion.kg_ref
  4.2 90.1 %shard_map.67 = (f32[48,48,96]{2,1,0:T(8,128)}, f32[48,48,96]{2,1,0:T(8,128)}, f32[8]{0:T(128)}) custom-call(f32[3,48,128]{2,1,0:T(8,128)} %pad_maximum_fusion.kg_ref, f32[48,48,96]{2,1,0:T(8,128)} %bitcast.19, f32[48,48,96]{2,1,0:T(8,128)} %bitcast.20, f32[48,48,96]{2,1,0:T(8,128)} %bitcast.21), custom_call_target="tpu_custom_call" | custom-call | tf_op jit(solution)/shard_map/pallas_call | solution.py:368
  94.3 0.0 copy-start
  94.3 2.5 %copy.12 = f32[48,96,48]{1,2,0:T(8,128)} copy(f32[48,96,48]{1,2,0:T(8,128)} %bitcast.23) | data formatting | bytes 1769472
  96.8 0.0 copy-done
  96.8 0.0 copy-start.1
  96.8 1.0 %copy.13 = f32[48,96,48]{1,2,0:T(8,128)} copy(f32[48,96,48]{1,2,0:T(8,128)S(1)} %bitcast.22) | data formatting | bytes 1769472
  97.8 0.0 copy-done.1
  97.8 0.5 copy.14
  (2 shorter events, 0.0 us)
Async XLA Ops:
  94.3 2.5 %copy-start = (f32[48,48,96]{2,1,0:T(8,128)S(1)}, f32[48,48,96]{2,1,0:T(8,128)}, u32[]{:S(2)}) copy-start(f32[48,48,96]{2,1,0:T(8,128)} %get-tuple-element.7) | copy-start | bytes 2654212
  96.8 1.0 %copy-start.1 = (f32[8]{0:T(128)S(1)}, f32[8]{0:T(128)}, u32[]{:S(2)}) copy-start(f32[8]{0:T(128)} %get-tuple-element.16) | copy-start | bytes 100

commit v3 on v2

v3 whole, which is shorter than its diff:
```python
import functools

import jax
import jax.numpy as jnp
from jax import lax
from jax.experimental import pallas as pl
from jax.experimental.pallas import tpu as pltpu
from jax.sharding import PartitionSpec as P

CG_ITERS = 8
LANES = 128
PAD = 8
GROUP = 4
MESH = pl.DeviceIdType.MESH
F32 = jnp.float32


def solve_kernel(dims, counts, kg_hbm, k_hbm, f_hbm, u_hbm, x_hbm, r_hbm, hist_ref,
                 k_in, f_in, u_in, wall_x, wall_y, wall_z, wall_t, x_stage, r_stage,
                 kp, mp, cx, cy, cyh, cz, inv, x, r, w, s, z, p, n,
                 ys, zs, xr, yr, zr, red_s, red_r,
                 xs_sem, ys_sem, zs_sem, xr_sem, yr_sem, zr_sem, rs_sem, rr_sem, in_sem, out_sem):
    ni, nl, nj = dims
    ngx, ngy, ngz = counts
    half = nl // 2
    gx, gy, gz = lax.axis_index('gx'), lax.axis_index('gy'), lax.axis_index('gz')
    rows = pl.ds(PAD, nl)
    rows_dn = pl.ds(PAD - 1, nl)
    rows_up = pl.ds(PAD + 1, nl)
    lane = lax.broadcasted_iota(jnp.int32, (nl, LANES), 1)
    lane_i = lax.broadcasted_iota(jnp.int32, (ni, LANES), 1)
    lane_half = lax.broadcasted_iota(jnp.int32, (half, LANES), 1)
    lane_row = lax.broadcasted_iota(jnp.int32, (1, LANES), 1)
    inside = lane < nj
    has_xlo, has_xhi = gx > 0, gx < ngx - 1
    has_zlo, has_zhi = gz > 0, gz < ngz - 1
    face_lane = jnp.where(gy == 0, nj - 1, 0)
    lane_lo = jnp.where(gy == 0, -1, 0)
    lane_hi = jnp.where(gy == 0, nj - 1, -1)
    zero_slab = jnp.zeros((nl, LANES), F32)
    zero_acc = jnp.zeros((8, LANES), F32)
    relative = [(a, b, c) for a in reversed(range(ngz)) for b in reversed(range(ngy)) for c in reversed(range(ngx))
                if a or b or c]

    def other(a, b, c):
        return lax.rem(gz + a, ngz), lax.rem(gy + b, ngy), lax.rem(gx + c, ngx)

    def column_roll(slab, shift):
        return pltpu.roll(slab, lax.rem(shift + 2 * LANES, LANES), 1)

    def slabs(group, step, init):
        def body(g, carry):
            for k in range(group):
                carry = step(g * group + k, carry)
            return carry
        return lax.fori_loop(0, ni // group, body, init)

    def x_copy(ref, slot, up):
        src = ref.at[ni if up else 1, rows]
        return pltpu.make_async_remote_copy(
            src_ref=src, dst_ref=xr.at[slot, 0 if up else 1], send_sem=xs_sem.at[slot, 0 if up else 1],
            recv_sem=xr_sem.at[slot, 0 if up else 1], device_id=(gz, gy, gx + 1 if up else gx - 1), device_id_type=MESH)

    def z_copy(slot, up):
        return pltpu.make_async_remote_copy(
            src_ref=zs.at[slot, 0 if up else 1], dst_ref=zr.at[slot, 0 if up else 1],
            send_sem=zs_sem.at[slot, 0 if up else 1], recv_sem=zr_sem.at[slot, 0 if up else 1],
            device_id=(gz + 1 if up else gz - 1, gy, gx), device_id_type=MESH)

    def y_copy(slot):
        return pltpu.make_async_remote_copy(
            src_ref=ys.at[slot], dst_ref=yr.at[slot], send_sem=ys_sem.at[slot], recv_sem=yr_sem.at[slot],
            device_id=(gz, 1 - gy, gx), device_id_type=MESH)

    def pack(ref, slot, i, acc):
        row = lax.max(i, 0) if not isinstance(i, int) else i
        slab = ref[row + 1, rows, :]
        zs[slot, 1, pl.ds(row, 1), :] = slab[0:1, :]
        zs[slot, 0, pl.ds(row, 1), :] = slab[nl - 1:nl, :]
        acc = jnp.where(lane_half == i, column_roll(slab[0:half], row - face_lane), acc)
        return jnp.where(lane_half == i + LANES // 2, column_roll(slab[half:nl], row - face_lane + LANES // 2), acc)

    def packed_pass(ref, slot, step, init):
        def body(g, carry):
            state, acc = carry
            for k in range(GROUP):
                acc = pack(ref, slot, (g - 1) * GROUP + k, acc)
            for k in range(GROUP):
                state = step(g * GROUP + k, state)
            return state, acc
        state, acc = lax.fori_loop(0, ni // GROUP, body, (init, jnp.zeros((half, LANES), F32)))
        for k in range(GROUP):
            acc = pack(ref, slot, ni - GROUP + k, acc)
        ys[slot] = acc
        return state

    def exchange_start(ref, slot):
        pl.when(has_xlo)(lambda: x_copy(ref, slot, False).start())
        pl.when(has_xhi)(lambda: x_copy(ref, slot, True).start())
        pl.when(has_zlo)(lambda: z_copy(slot, False).start())
        pl.when(has_zhi)(lambda: z_copy(slot, True).start())
        y_copy(slot).start()

    def exchange_wait(ref, slot, margins=True):
        @pl.when(has_xlo)
        def _():
            x_copy(ref, slot, False).wait_send()
            x_copy(ref, slot, True).wait_recv()
            if margins:
                ref[0, rows, :] = xr[slot, 0]

        @pl.when(has_xhi)
        def _():
            x_copy(ref, slot, True).wait_send()
            x_copy(ref, slot, False).wait_recv()
            if margins:
                ref[ni + 1, rows, :] = xr[slot, 1]

        @pl.when(has_zlo)
        def _():
            z_copy(slot, False).wait_send()
            z_copy(slot, True).wait_recv()
            if margins:
                for i in range(ni):
                    ref[i + 1, PAD - 1:PAD, :] = zr[slot, 0, i:i + 1, :]

        @pl.when(has_zhi)
        def _():
            z_copy(slot, True).wait_send()
            z_copy(slot, False).wait_recv()
            if margins:
                for i in range(ni):
                    ref[i + 1, PAD + nl:PAD + nl + 1, :] = zr[slot, 1, i:i + 1, :]

        y_copy(slot).wait()

    def face_column(packed, i):
        return jnp.concatenate([column_roll(packed, face_lane - i), column_roll(packed, face_lane - i - LANES // 2)], axis=0)

    def stencil_step(ref, halo, i, v, flux_x, cy_i, cyh_i):
        above = ref[i + 2, rows, :]
        flux_next = cx[i + 1] * (above - v)
        flux_zl = cz[i, rows, :] * (v - ref[i + 1, rows_dn, :])
        flux_zh = cz[i, rows_up, :] * (ref[i + 1, rows_up, :] - v)
        column = face_column(halo, i)
        low = jnp.where(lane == lane_lo, column, pltpu.roll(v, 1, 1))
        high = jnp.where(lane == lane_hi, column, pltpu.roll(v, LANES - 1, 1))
        flux_yl = cy_i * (v - low)
        flux_yh = cyh_i * (high - v)
        return (flux_x - flux_next) + (flux_yl - flux_yh) + (flux_zl - flux_zh), above, flux_next

    def stencil_first(ref):
        first = ref[1, rows, :]
        return first, cx[0] * (first - ref[0, rows, :])

    def fold(slab):
        out = slab[0:8]
        for part in range(8, nl, 8):
            out = out + slab[part:part + 8]
        return out

    def reduce_start(slot, accs):
        row = jnp.zeros((1, LANES), F32)
        for q, acc in enumerate(accs):
            row = jnp.where(lane_row == q, jnp.sum(jnp.sum(acc, axis=0, keepdims=True), axis=1, keepdims=True), row)
        me = (gz * ngy + gy) * ngx + gx
        red_s[slot] = row
        red_r[slot, me] = row
        for delta in relative:
            pltpu.make_async_remote_copy(
                src_ref=red_s.at[slot], dst_ref=red_r.at[slot, me], send_sem=rs_sem.at[slot],
                recv_sem=rr_sem.at[slot], device_id=other(*delta), device_id_type=MESH).start()

    def reduce_wait(slot, count):
        whole = red_r.at[slot, pl.ds(0, len(relative))]
        done = pltpu.make_async_remote_copy(
            src_ref=whole, dst_ref=whole, send_sem=rs_sem.at[slot], recv_sem=rr_sem.at[slot],
            device_id=(gz, gy, gx), device_id_type=MESH)
        done.wait_recv()
        done.wait_send()
        total = jnp.sum(red_r[slot], axis=0)
        return [jnp.sum(jnp.where(lane_row == q, total, 0.0), axis=1, keepdims=True) for q in range(count)]

    x_row, z_row = jnp.where(gx == 0, 0, 1), jnp.where(gz == 0, 4, 5)
    slabs_i = pl.ds(pl.multiple_of(gx * ni, 8), ni)
    inputs = [
        pltpu.make_async_copy(k_hbm, k_in, in_sem.at[0]),
        pltpu.make_async_copy(u_hbm, u_in, in_sem.at[1]),
        pltpu.make_async_copy(kg_hbm.at[x_row, pl.ds(pl.multiple_of(gy * nj, 8), nj)], wall_x, in_sem.at[2]),
        pltpu.make_async_copy(kg_hbm.at[2 + gy, slabs_i], wall_y, in_sem.at[3]),
        pltpu.make_async_copy(kg_hbm.at[z_row, slabs_i], wall_z, in_sem.at[4]),
        pltpu.make_async_copy(f_hbm, f_in, in_sem.at[5]),
    ]
    for copy in inputs:
        copy.start()

    barrier = pltpu.get_barrier_semaphore()
    for delta in relative:
        pl.semaphore_signal(barrier, inc=1, device_id=other(*delta), device_id_type=MESH)

    for edge in (0, ni + 1):
        mp[edge] = jnp.zeros((nl + 2 * PAD, LANES), F32)
        kp[edge] = jnp.ones((nl + 2 * PAD, LANES), F32)

    def clear(i, _):
        mp[i + 1, pl.ds(0, PAD), :] = jnp.zeros((PAD, LANES), F32)
        mp[i + 1, pl.ds(PAD + nl, PAD), :] = jnp.zeros((PAD, LANES), F32)
        kp[i + 1, pl.ds(0, PAD), :] = jnp.ones((PAD, LANES), F32)
        kp[i + 1, pl.ds(PAD + nl, PAD), :] = jnp.ones((PAD, LANES), F32)
        mp[i + 1, rows, :] = zero_slab
        s[i] = zero_slab
        z[i] = zero_slab
        p[i] = zero_slab
        r[1, i] = zero_slab
        r[0, i] = zero_slab
        kp[i + 1, rows, :] = jnp.full((nl, LANES), 1.0, F32)
        return 0

    lax.fori_loop(0, ni, clear, 0)

    def load_k(i, _):
        kp[i + 1, rows, 0:nj] = k_in[i]
        return 0

    def load_u(i, _):
        mp[i + 1, rows, 0:nj] = u_in[i]
        return 0

    inputs[0].wait()
    packed_pass(kp, 0, load_k, 0)
    pl.semaphore_wait(barrier, len(relative))
    exchange_start(kp, 0)
    inputs[1].wait()
    packed_pass(mp, 1, load_u, 0)
    exchange_start(mp, 1)

    for copy in inputs[2:5]:
        copy.wait()
    width = wall_x.shape[1]
    l_rows = pl.ds(pl.multiple_of(gz * nl, 8), nl)

    def flipped(wall, count):
        for start in range(0, width, LANES):
            size = min(LANES, width - start)
            block = jnp.concatenate([wall[:, start:start + size], jnp.ones((LANES - count, size), F32)], axis=0)
            wall_t[start:start + size, :] = block.T
        return wall_t[l_rows, :]

    x_wall = flipped(wall_x, nj)
    y_wall = flipped(wall_y, ni)
    if width > LANES:
        rest = jnp.concatenate([wall_z[:, LANES:width], jnp.ones((ni, 2 * LANES - width), F32)], axis=1)
        whole_z = wall_z[:, 0:LANES]
        turn = LANES - nj
        shifted = jnp.where(lane_i < turn, pltpu.roll(whole_z, turn, 1), pltpu.roll(rest, turn, 1))
    else:
        whole_z = jnp.concatenate([wall_z[...], jnp.ones((ni, LANES - width), F32)], axis=1)
        shifted = pltpu.roll(whole_z, LANES - nj, 1)
    z_wall = jnp.where(gy == 0, whole_z, shifted)

    def harmonic(left, right):
        return 2.0 * left * right / (left + right)

    def coefs(i, _):
        here = kp[i + 1, rows, :]
        cx[i + 1] = jnp.where(inside, harmonic(here, kp[i + 2, rows, :]), 0.0)
        z_hi = jnp.where(inside, harmonic(here, kp[i + 1, rows_up, :]), 0.0)
        cz[i, rows_up, :] = z_hi
        wall = column_roll(y_wall, nj - 1 - face_lane - i)
        low = jnp.where(lane == 0, wall, pltpu.roll(here, 1, 1))
        high = jnp.where(lane == nj - 1, wall, pltpu.roll(here, LANES - 1, 1))
        cy[i] = jnp.where(inside, harmonic(low, here), 0.0)
        cyh[i] = jnp.where(inside, harmonic(here, high), 0.0)
        return 0

    slabs(GROUP, coefs, 0)
    exchange_wait(kp, 0, margins=False)
    cx[0] = jnp.where(inside, harmonic(jnp.where(gx == 0, x_wall, xr[0, 0]), kp[1, rows, :]), 0.0)
    cx[ni] = jnp.where(inside, harmonic(kp[ni, rows, :], jnp.where(gx == ngx - 1, x_wall, xr[0, 1])), 0.0)
    z_low = jnp.where(lane_i < nj, harmonic(jnp.where(gz == 0, z_wall, zr[0, 0]), zs[0, 1]), 0.0)
    z_high = jnp.where(lane_i < nj, harmonic(zs[0, 0], jnp.where(gz == ngz - 1, z_wall, zr[0, 1])), 0.0)
    for i in range(ni):
        cz[i, PAD:PAD + 1, :] = z_low[i:i + 1, :]
        cz[i, PAD + nl:PAD + nl + 1, :] = z_high[i:i + 1, :]
    y_face = harmonic(ys[0], yr[0])
    exchange_wait(mp, 1)
    inputs[5].wait()

    u_halo = yr[1]

    def first_residual(i, carry):
        v, flux_x, acc = carry
        column = face_column(y_face, i)
        cy_i = jnp.where(lane == lane_lo, column, cy[i])
        cyh_i = jnp.where(lane == lane_hi, column, cyh[i])
        cy[i] = cy_i
        cyh[i] = cyh_i
        av, above, flux_next = stencil_step(mp, u_halo, i, v, flux_x, cy_i, cyh_i)
        diag = cx[i] + cx[i + 1] + cy_i + cyh_i + cz[i, rows, :] + cz[i, rows_up, :]
        iv = jnp.where(inside, 1.0 / jnp.where(inside, diag, 1.0), 0.0)
        inv[i] = iv
        x[i] = v
        r[0, i, :, 0:nj] = f_in[i]
        res = r[0, i] - av
        r[0, i] = res
        u = res * iv
        mp[i + 1, rows, :] = u
        return above, flux_next, acc + fold(res * u)

    gamma_acc = packed_pass(mp, 2, first_residual, stencil_first(mp) + (zero_acc,))[2]
    exchange_start(mp, 2)
    exchange_wait(mp, 2)
    z_halo = yr[2]

    def first_w(i, carry):
        v, flux_x, acc = carry
        av, above, flux_next = stencil_step(mp, z_halo, i, v, flux_x, cy[i], cyh[i])
        w[i] = av
        mp[i + 1, rows, :] = av * inv[i]
        return above, flux_next, acc + fold(av * v)

    delta_acc = packed_pass(mp, 3, first_w, stencil_first(mp) + (zero_acc,))[2]

    def scalars(t, sums, gamma_old, pap_old):
        gamma, delta, sigma = sums[0], sums[1], sums[2]
        beta = jnp.where(t == 0, 0.0, gamma / gamma_old)
        pap = delta + 2.0 * beta * sigma + beta * beta * pap_old
        return gamma, pap, beta[0, 0], (gamma / pap)[0, 0]

    def advance_x(now, alpha, beta):
        def step(i, _):
            p_new = inv[i] * r[1 - now, i] + beta * p[i]
            p[i] = p_new
            x[i] = x[i] + alpha * p_new
            return 0
        lax.fori_loop(0, ni, step, 0)

    def iteration(t, carry):
        accs, gamma_old, pap_old, alpha_old, beta_old = carry
        now = lax.rem(t, 2)
        exchange_start(mp, t + 3)
        reduce_start(t, accs)
        advance_x(now, alpha_old, beta_old)
        exchange_wait(mp, t + 3)
        halo = yr[t + 3]

        def apply(i, carry):
            av, above, flux_next = stencil_step(mp, halo, i, carry[0], carry[1], cy[i], cyh[i])
            n[i] = av
            return above, flux_next

        slabs(GROUP, apply, stencil_first(mp))
        sums = reduce_wait(t, 4)
        gamma, pap, beta, alpha = scalars(t, sums, gamma_old, pap_old)

        def update(i, acc):
            iv = inv[i]
            z_new = n[i] + beta * z[i]
            s_new = w[i] + beta * s[i]
            r_new = r[now, i] - alpha * s_new
            w_new = w[i] - alpha * z_new
            u_new = iv * r_new
            z[i] = z_new
            s[i] = s_new
            r[1 - now, i] = r_new
            w[i] = w_new
            mp[i + 1, rows, :] = iv * w_new
            return (acc[0] + fold(r_new * u_new), acc[1] + fold(w_new * u_new),
                    acc[2] + fold(u_new * s_new), acc[3] + fold(r_new * r_new))

        accs = packed_pass(mp, t + 4, update, (zero_acc,) * 4)

        @pl.when(t > 0)
        def _():
            hist_ref[lax.max(t - 1, 0)] = sums[3][0, 0]

        return accs, gamma, pap, alpha, beta

    one = jnp.ones((1, 1), F32)
    last = CG_ITERS - 1
    accs, gamma_old, pap_old, alpha_old, beta_old = lax.fori_loop(
        0, last, iteration, ((gamma_acc, delta_acc, zero_acc, zero_acc), one, one, jnp.float32(0.0), jnp.float32(0.0)))

    now = last % 2
    reduce_start(last, accs)
    advance_x(now, alpha_old, beta_old)
    sums = reduce_wait(last, 4)
    hist_ref[last - 1] = sums[3][0, 0]
    _, _, beta, alpha = scalars(last, sums, gamma_old, pap_old)

    def final(i, acc):
        r_old = r[now, i]
        s_new = w[i] + beta * s[i]
        p_new = inv[i] * r_old + beta * p[i]
        r_new = r_old - alpha * s_new
        x_new = x[i] + alpha * p_new
        x_stage[i] = x_new[:, 0:nj]
        r_stage[i] = r_new[:, 0:nj]
        return acc + fold(r_new * r_new)

    acc = lax.fori_loop(0, ni, final, zero_acc)
    outputs = [pltpu.make_async_copy(x_stage, x_hbm, out_sem.at[0]), pltpu.make_async_copy(r_stage, r_hbm, out_sem.at[1])]
    for copy in outputs:
        copy.start()
    reduce_start(CG_ITERS, (acc,))
    hist_ref[last] = reduce_wait(CG_ITERS, 1)[0][0, 0]
    for copy in outputs:
        copy.wait()


def solution(mesh):
    counts = (mesh.shape['gx'], mesh.shape['gy'], mesh.shape['gz'])
    grid_spec = P('gx', 'gy', 'gz')

    def local_solve(k_cell, k_ghost, f_rhs, u_init):
        ni, nj, nl = k_cell.shape
        flip = lambda a: jnp.swapaxes(a, 1, 2)
        slots = CG_ITERS + 3
        devices = counts[0] * counts[1] * counts[2]
        width = k_ghost.shape[2]
        any_spec = pl.BlockSpec(memory_space=pl.ANY)
        vm = lambda *shape: pltpu.VMEM(shape, F32)
        whole = vm(ni, nl, LANES)
        block = vm(ni, nl, nj)
        padded = vm(ni + 2, nl + 2 * PAD, LANES)
        dma = pltpu.SemaphoreType.DMA
        out_block = jax.ShapeDtypeStruct((ni, nl, nj), F32)
        x_new, r_new, hist = pl.pallas_call(
            functools.partial(solve_kernel, (ni, nl, nj), counts),
            out_shape=(out_block, out_block, jax.ShapeDtypeStruct((CG_ITERS,), F32)),
            in_specs=[any_spec] * 4,
            out_specs=(any_spec, any_spec, pl.BlockSpec(memory_space=pltpu.SMEM)),
            scratch_shapes=[
                block, block, block, vm(nj, width), vm(ni, width), vm(ni, width), vm(-(-width // LANES) * LANES, LANES), block, block,
                padded, padded, vm(ni + 1, nl, LANES), whole, whole, vm(ni, nl + 2 * PAD, LANES), whole,
                whole, vm(2, ni, nl, LANES), whole, whole, whole, whole, whole,
                vm(slots, nl // 2, LANES), vm(slots, 2, ni, LANES),
                vm(slots, 2, nl, LANES), vm(slots, nl // 2, LANES), vm(slots, 2, ni, LANES),
                vm(CG_ITERS + 1, 1, LANES), vm(CG_ITERS + 1, devices, 1, LANES),
                dma((slots, 2)), dma((slots,)), dma((slots, 2)), dma((slots, 2)), dma((slots,)), dma((slots, 2)),
                dma((CG_ITERS + 1,)), dma((CG_ITERS + 1,)), dma((6,)), dma((2,)),
            ],
            compiler_params=pltpu.CompilerParams(has_side_effects=True, collective_id=0),
        )(k_ghost, flip(k_cell), flip(f_rhs), flip(u_init))
        return flip(x_new), flip(r_new), hist

    return jax.shard_map(local_solve, mesh=mesh, in_specs=(grid_spec, P(), grid_spec, grid_spec),
                         out_specs=(grid_spec, grid_spec, P()), check_vma=False)
```

time: 98.6 us -> 82.8 us (0.84)
  Pallas kernels: 90.1 us -> 78 us
  local copies, waits for them, and re-layouts: 6.9 us -> 3.99 us
    pallas_call x1, Pallas kernels: 90.1 us -> 78 us  [local_solve(): pl.pallas_call(functools.partial(solve_kernel, (ni, nl, nj), counts), out...]
    dynamic_slice x4 -> x0, local copies, waits for them, and re-layouts: 2 us -> none  [local_solve(): lax.dynamic_slice(k_ghost, (row,) + start, (1,) + extent)[0]]
where the time goes in v3:
time: 82.8 us; the launch traced here: 82.6 us
  Pallas kernels  78 us (94%)
  local copies, waits for them, and re-layouts  3.99 us (5%)
    pallas_call x1, Pallas kernels, local_solve(): pl.pallas_call(functools.partial(solve_kernel, (ni, nl, nj), counts), out...  78 us
    unnamed x7, local copies, waits for them, and re-layouts  3.99 us

profile of v3, /device:TPU:0, one launch (start us, length us, event | category | flops | bytes accessed | tf_op | source)
XLA Modules:
  0.0 82.6 jit_solution(14036160664164064630)
XLA Ops:
  0.6 78.0 %shard_map.67 = (f32[48,48,96]{2,1,0:T(8,128)}, f32[48,48,96]{2,1,0:T(8,128)}, f32[8]{0:T(128)}) custom-call(f32[6,192,192]{2,1,0:T(8,128)} %kg_hbm.1, f32[48,48,96]{2,1,0:T(8,128)} %bitcast.7, f32[48,48,96]{2,1,0:T(8,128)} %bitcast.8, f32[48,48,96]{2,1,0:T(8,128)} %bitcast.9), custom_call_target="tpu_custom_call" | custom-call | tf_op jit(solution)/shard_map/pallas_call | solution.py:428
  78.6 0.0 copy-start
  78.6 2.5 %copy.10 = f32[48,96,48]{1,2,0:T(8,128)} copy(f32[48,96,48]{1,2,0:T(8,128)} %bitcast.6) | data formatting | bytes 1769472
  81.1 0.0 copy-done
  81.1 0.0 copy-start.1
  81.1 1.0 %copy.11 = f32[48,96,48]{1,2,0:T(8,128)} copy(f32[48,96,48]{1,2,0:T(8,128)S(1)} %bitcast.5) | data formatting | bytes 1769472
  82.1 0.0 copy-done.1
  82.1 0.5 copy.12
Async XLA Ops:
  78.6 2.5 %copy-start = (f32[48,48,96]{2,1,0:T(8,128)S(1)}, f32[48,48,96]{2,1,0:T(8,128)}, u32[]{:S(2)}) copy-start(f32[48,48,96]{2,1,0:T(8,128)} %get-tuple-element.7) | copy-start | bytes 2654212
  81.1 1.0 %copy-start.1 = (f32[8]{0:T(128)S(1)}, f32[8]{0:T(128)}, u32[]{:S(2)}) copy-start(f32[8]{0:T(128)} %get-tuple-element.14) | copy-start | bytes 100

commit v4 on v3

--- a/solution.py
+++ b/solution.py
@@ -10,13 +10,14 @@
 CG_ITERS = 8
 LANES = 128
 PAD = 8
-GROUP = 4
+GROUP = 6
+COLUMNS = 16
 MESH = pl.DeviceIdType.MESH
 F32 = jnp.float32
 
 
-def solve_kernel(dims, counts, kg_hbm, k_hbm, f_hbm, u_hbm, x_hbm, r_hbm, hist_ref,
-                 k_in, f_in, u_in, wall_x, wall_y, wall_z, wall_t, x_stage, r_stage,
+def solve_kernel(dims, counts, kg_hbm, k_hbm, f_hbm, u_hbm, x_hbm, u_last_hbm, p_hbm, r_hbm, w_hbm, s_hbm, hist_ref, alpha_ref, beta_ref,
+                 k_in, f_in, u_in, wall_x, wall_y, wall_z, wall_t, bx, by, bz,
                  kp, mp, cx, cy, cyh, cz, inv, x, r, w, s, z, p, n,
                  ys, zs, xr, yr, zr, red_s, red_r,
                  xs_sem, ys_sem, zs_sem, xr_sem, yr_sem, zr_sem, rs_sem, rr_sem, in_sem, out_sem):
@@ -35,8 +36,7 @@
     has_xlo, has_xhi = gx > 0, gx < ngx - 1
     has_zlo, has_zhi = gz > 0, gz < ngz - 1
     face_lane = jnp.where(gy == 0, nj - 1, 0)
-    lane_lo = jnp.where(gy == 0, -1, 0)
-    lane_hi = jnp.where(gy == 0, nj - 1, -1)
+    y_low_wall, y_high_wall = gy == 0, gy > 0
     zero_slab = jnp.zeros((nl, LANES), F32)
     zero_acc = jnp.zeros((8, LANES), F32)
     relative = [(a, b, c) for a in reversed(range(ngz)) for b in reversed(range(ngy)) for c in reversed(range(ngx))
@@ -72,25 +72,30 @@
             src_ref=ys.at[slot], dst_ref=yr.at[slot], send_sem=ys_sem.at[slot], recv_sem=yr_sem.at[slot],
             device_id=(gz, 1 - gy, gx), device_id_type=MESH)
 
-    def pack(ref, slot, i, acc):
+    def pack_rolls(ref, slot, i):
         row = lax.max(i, 0) if not isinstance(i, int) else i
         slab = ref[row + 1, rows, :]
         zs[slot, 1, pl.ds(row, 1), :] = slab[0:1, :]
         zs[slot, 0, pl.ds(row, 1), :] = slab[nl - 1:nl, :]
-        acc = jnp.where(lane_half == i, column_roll(slab[0:half], row - face_lane), acc)
-        return jnp.where(lane_half == i + LANES // 2, column_roll(slab[half:nl], row - face_lane + LANES // 2), acc)
+        return column_roll(slab[0:half], row - face_lane), column_roll(slab[half:nl], row - face_lane + LANES // 2)
+
+    def pack(i, rolled, acc):
+        acc = jnp.where(lane_half == i, rolled[0], acc)
+        return jnp.where(lane_half == i + LANES // 2, rolled[1], acc)
 
     def packed_pass(ref, slot, step, init):
         def body(g, carry):
             state, acc = carry
-            for k in range(GROUP):
-                acc = pack(ref, slot, (g - 1) * GROUP + k, acc)
+            rolled = [pack_rolls(ref, slot, (g - 1) * GROUP + k) for k in range(GROUP)]
             for k in range(GROUP):
                 state = step(g * GROUP + k, state)
+            for k in range(GROUP):
+                acc = pack((g - 1) * GROUP + k, rolled[k], acc)
             return state, acc
         state, acc = lax.fori_loop(0, ni // GROUP, body, (init, jnp.zeros((half, LANES), F32)))
+        rolled = [pack_rolls(ref, slot, ni - GROUP + k) for k in range(GROUP)]
         for k in range(GROUP):
-            acc = pack(ref, slot, ni - GROUP + k, acc)
+            acc = pack(ni - GROUP + k, rolled[k], acc)
         ys[slot] = acc
         return state
 
@@ -101,57 +106,90 @@
         pl.when(has_zhi)(lambda: z_copy(slot, True).start())
         y_copy(slot).start()
 
-    def exchange_wait(ref, slot, margins=True):
+    def exchange_wait(ref, slot):
         @pl.when(has_xlo)
         def _():
             x_copy(ref, slot, False).wait_send()
             x_copy(ref, slot, True).wait_recv()
-            if margins:
-                ref[0, rows, :] = xr[slot, 0]
 
         @pl.when(has_xhi)
         def _():
             x_copy(ref, slot, True).wait_send()
             x_copy(ref, slot, False).wait_recv()
-            if margins:
-                ref[ni + 1, rows, :] = xr[slot, 1]
 
         @pl.when(has_zlo)
         def _():
             z_copy(slot, False).wait_send()
             z_copy(slot, True).wait_recv()
-            if margins:
-                for i in range(ni):
-                    ref[i + 1, PAD - 1:PAD, :] = zr[slot, 0, i:i + 1, :]
 
         @pl.when(has_zhi)
         def _():
             z_copy(slot, True).wait_send()
             z_copy(slot, False).wait_recv()
-            if margins:
-                for i in range(ni):
-                    ref[i + 1, PAD + nl:PAD + nl + 1, :] = zr[slot, 1, i:i + 1, :]
 
         y_copy(slot).wait()
 
-    def face_column(packed, i):
-        return jnp.concatenate([column_roll(packed, face_lane - i), column_roll(packed, face_lane - i - LANES // 2)], axis=0)
-
-    def stencil_step(ref, halo, i, v, flux_x, cy_i, cyh_i):
-        above = ref[i + 2, rows, :]
-        flux_next = cx[i + 1] * (above - v)
-        flux_zl = cz[i, rows, :] * (v - ref[i + 1, rows_dn, :])
-        flux_zh = cz[i, rows_up, :] * (ref[i + 1, rows_up, :] - v)
-        column = face_column(halo, i)
-        low = jnp.where(lane == lane_lo, column, pltpu.roll(v, 1, 1))
-        high = jnp.where(lane == lane_hi, column, pltpu.roll(v, LANES - 1, 1))
-        flux_yl = cy_i * (v - low)
-        flux_yh = cyh_i * (high - v)
-        return (flux_x - flux_next) + (flux_yl - flux_yh) + (flux_zl - flux_zh), above, flux_next
-
-    def stencil_first(ref):
+    def add_rows(ref, layer, row):
+        for i in range(ni):
+            ref[i, row:row + 1, :] = ref[i, row:row + 1, :] + layer[i:i + 1, :]
+
+    def add_columns(ref, packed):
+        mask = lane == face_lane
+
+        def step(g, _):
+            columns = []
+            for k in range(min(COLUMNS, ni)):
+                i = g * min(COLUMNS, ni) + k
+                columns.append((column_roll(packed, face_lane - i), column_roll(packed, face_lane - i - LANES // 2)))
+            for k in range(min(COLUMNS, ni)):
+                i = g * min(COLUMNS, ni) + k
+                ref[i] = ref[i] + jnp.where(mask, jnp.concatenate(columns[k], axis=0), 0.0)
+            return 0
+
+        lax.fori_loop(0, ni // min(COLUMNS, ni), step, 0)
+
+    def join_faces(ref, slot):
+        y_copy(slot).wait()
+        add_columns(n, by[...] * (ys[slot] - yr[slot]))
+
+        @pl.when(has_xlo)
+        def _():
+            x_copy(ref, slot, False).wait_send()
+            x_copy(ref, slot, True).wait_recv()
+            n[0] = n[0] + bx[0] * (ref[1, rows, :] - xr[slot, 0])
+
+        @pl.when(has_xhi)
+        def _():
+            x_copy(ref, slot, True).wait_send()
+            x_copy(ref, slot, False).wait_recv()
+            n[ni - 1] = n[ni - 1] + bx[1] * (ref[ni, rows, :] - xr[slot, 1])
+
+        @pl.when(has_zlo)
+        def _():
+            z_copy(slot, False).wait_send()
+            z_copy(slot, True).wait_recv()
+            add_rows(n, bz[0] * (zs[slot, 1] - zr[slot, 0]), 0)
+
+        @pl.when(has_zhi)
+        def _():
+            z_copy(slot, True).wait_send()
+            z_copy(slot, False).wait_recv()
+            add_rows(n, bz[1] * (zs[slot, 0] - zr[slot, 1]), nl - 1)
+
+    def stencil(ref):
+        def step(i, carry):
+            v, flux_x = carry
+            above = ref[i + 2, rows, :]
+            flux_next = cx[i + 1] * (above - v)
+            flux_zl = cz[i, rows, :] * (v - ref[i + 1, rows_dn, :])
+            flux_zh = cz[i, rows_up, :] * (ref[i + 1, rows_up, :] - v)
+            flux_yl = cy[i] * (v - pltpu.roll(v, 1, 1))
+            flux_yh = cyh[i] * (pltpu.roll(v, LANES - 1, 1) - v)
+            n[i] = (flux_x - flux_next) + (flux_yl - flux_yh) + (flux_zl - flux_zh)
+            return above, flux_next
+
         first = ref[1, rows, :]
-        return first, cx[0] * (first - ref[0, rows, :])
+        slabs(GROUP, step, (first, cx[0] * (first - ref[0, rows, :])))
 
     def fold(slab):
         out = slab[0:8]
@@ -261,65 +299,91 @@
     def harmonic(left, right):
         return 2.0 * left * right / (left + right)
 
+    in_i = lane_i < nj
+    cx[0] = jnp.where(jnp.logical_and(inside, gx == 0), harmonic(x_wall, kp[1, rows, :]), 0.0)
+    z_low = jnp.where(jnp.logical_and(in_i, gz == 0), harmonic(z_wall, zs[0, 1]), 0.0)
+    z_high = jnp.where(jnp.logical_and(in_i, gz == ngz - 1), harmonic(zs[0, 0], z_wall), 0.0)
+    y_low_mask = jnp.logical_and(inside, jnp.logical_or(lane > 0, y_low_wall))
+    y_high_mask = jnp.logical_and(inside, jnp.logical_or(lane < nj - 1, y_high_wall))
+    wall_lane = nj - 1 - face_lane
+
     def coefs(i, _):
         here = kp[i + 1, rows, :]
         cx[i + 1] = jnp.where(inside, harmonic(here, kp[i + 2, rows, :]), 0.0)
-        z_hi = jnp.where(inside, harmonic(here, kp[i + 1, rows_up, :]), 0.0)
-        cz[i, rows_up, :] = z_hi
-        wall = column_roll(y_wall, nj - 1 - face_lane - i)
+        cz[i, rows_up, :] = jnp.where(inside, harmonic(here, kp[i + 1, rows_up, :]), 0.0)
+        wall = column_roll(y_wall, wall_lane - i)
         low = jnp.where(lane == 0, wall, pltpu.roll(here, 1, 1))
         high = jnp.where(lane == nj - 1, wall, pltpu.roll(here, LANES - 1, 1))
-        cy[i] = jnp.where(inside, harmonic(low, here), 0.0)
-        cyh[i] = jnp.where(inside, harmonic(here, high), 0.0)
+        cy[i] = jnp.where(y_low_mask, harmonic(low, here), 0.0)
+        cyh[i] = jnp.where(y_high_mask, harmonic(here, high), 0.0)
         return 0
 
     slabs(GROUP, coefs, 0)
-    exchange_wait(kp, 0, margins=False)
-    cx[0] = jnp.where(inside, harmonic(jnp.where(gx == 0, x_wall, xr[0, 0]), kp[1, rows, :]), 0.0)
-    cx[ni] = jnp.where(inside, harmonic(kp[ni, rows, :], jnp.where(gx == ngx - 1, x_wall, xr[0, 1])), 0.0)
-    z_low = jnp.where(lane_i < nj, harmonic(jnp.where(gz == 0, z_wall, zr[0, 0]), zs[0, 1]), 0.0)
-    z_high = jnp.where(lane_i < nj, harmonic(zs[0, 0], jnp.where(gz == ngz - 1, z_wall, zr[0, 1])), 0.0)
+    cx[ni] = jnp.where(jnp.logical_and(inside, gx == ngx - 1), harmonic(kp[ni, rows, :], x_wall), 0.0)
     for i in range(ni):
         cz[i, PAD:PAD + 1, :] = z_low[i:i + 1, :]
         cz[i, PAD + nl:PAD + nl + 1, :] = z_high[i:i + 1, :]
-    y_face = harmonic(ys[0], yr[0])
-    exchange_wait(mp, 1)
+
+    stencil(mp)
+
+    def diagonal(i, _):
+        inv[i] = cx[i] + cx[i + 1] + cy[i] + cyh[i] + cz[i, rows, :] + cz[i, rows_up, :]
+        return 0
+
+    lax.fori_loop(0, ni, diagonal, 0)
+
+    exchange_wait(kp, 0)
+
+    @pl.when(has_xlo)
+    def _():
+        bx[0] = jnp.where(inside, harmonic(xr[0, 0], kp[1, rows, :]), 0.0)
+        inv[0] = inv[0] + bx[0]
+
+    @pl.when(has_xhi)
+    def _():
+        bx[1] = jnp.where(inside, harmonic(kp[ni, rows, :], xr[0, 1]), 0.0)
+        inv[ni - 1] = inv[ni - 1] + bx[1]
+
+    @pl.when(has_zlo)
+    def _():
+        bz[0] = jnp.where(in_i, harmonic(zr[0, 0], zs[0, 1]), 0.0)
+        add_rows(inv, bz[0], 0)
+
+    @pl.when(has_zhi)
+    def _():
+        bz[1] = jnp.where(in_i, harmonic(zs[0, 0], zr[0, 1]), 0.0)
+        add_rows(inv, bz[1], nl - 1)
+
+    y_face = jnp.where(lax.rem(lane_half, LANES // 2) < ni, harmonic(ys[0], yr[0]), 0.0)
+    by[...] = y_face
+    add_columns(inv, y_face)
+    join_faces(mp, 1)
     inputs[5].wait()
 
-    u_halo = yr[1]
-
-    def first_residual(i, carry):
-        v, flux_x, acc = carry
-        column = face_column(y_face, i)
-        cy_i = jnp.where(lane == lane_lo, column, cy[i])
-        cyh_i = jnp.where(lane == lane_hi, column, cyh[i])
-        cy[i] = cy_i
-        cyh[i] = cyh_i
-        av, above, flux_next = stencil_step(mp, u_halo, i, v, flux_x, cy_i, cyh_i)
-        diag = cx[i] + cx[i + 1] + cy_i + cyh_i + cz[i, rows, :] + cz[i, rows_up, :]
-        iv = jnp.where(inside, 1.0 / jnp.where(inside, diag, 1.0), 0.0)
+    def first_residual(i, acc):
+        iv = jnp.where(inside, 1.0 / jnp.where(inside, inv[i], 1.0), 0.0)
         inv[i] = iv
-        x[i] = v
+        x[i] = mp[i + 1, rows, :]
         r[0, i, :, 0:nj] = f_in[i]
-        res = r[0, i] - av
+        res = r[0, i] - n[i]
         r[0, i] = res
         u = res * iv
         mp[i + 1, rows, :] = u
-        return above, flux_next, acc + fold(res * u)
-
-    gamma_acc = packed_pass(mp, 2, first_residual, stencil_first(mp) + (zero_acc,))[2]
+        return acc + fold(res * u)
+
+    gamma_acc = packed_pass(mp, 2, first_residual, zero_acc)
     exchange_start(mp, 2)
-    exchange_wait(mp, 2)
-    z_halo = yr[2]
-
-    def first_w(i, carry):
-        v, flux_x, acc = carry
-        av, above, flux_next = stencil_step(mp, z_halo, i, v, flux_x, cy[i], cyh[i])
+    stencil(mp)
+    join_faces(mp, 2)
+
+    def first_w(i, acc):
+        av = n[i]
         w[i] = av
+        acc = acc + fold(av * mp[i + 1, rows, :])
         mp[i + 1, rows, :] = av * inv[i]
-        return above, flux_next, acc + fold(av * v)
-
-    delta_acc = packed_pass(mp, 3, first_w, stencil_first(mp) + (zero_acc,))[2]
+        return acc
+
+    delta_acc = packed_pass(mp, 3, first_w, zero_acc)
 
     def scalars(t, sums, gamma_old, pap_old):
         gamma, delta, sigma = sums[0], sums[1], sums[2]
@@ -338,18 +402,11 @@
     def iteration(t, carry):
         accs, gamma_old, pap_old, alpha_old, beta_old = carry
         now = lax.rem(t, 2)
+        reduce_start(t, accs)
         exchange_start(mp, t + 3)
-        reduce_start(t, accs)
+        stencil(mp)
         advance_x(now, alpha_old, beta_old)
-        exchange_wait(mp, t + 3)
-        halo = yr[t + 3]
-
-        def apply(i, carry):
-            av, above, flux_next = stencil_step(mp, halo, i, carry[0], carry[1], cy[i], cyh[i])
-            n[i] = av
-            return above, flux_next
-
-        slabs(GROUP, apply, stencil_first(mp))
+        join_faces(mp, t + 3)
         sums = reduce_wait(t, 4)
         gamma, pap, beta, alpha = scalars(t, sums, gamma_old, pap_old)
 
@@ -383,27 +440,31 @@
 
     now = last % 2
     reduce_start(last, accs)
+    outputs = [pltpu.make_async_copy(src, dst, out_sem.at[j]) for j, (src, dst) in enumerate((
+        (r.at[now], r_hbm), (w, w_hbm), (s, s_hbm), (p, p_hbm), (x, x_hbm), (n, u_last_hbm)))]
+    for copy in outputs[:3]:
+        copy.start()
+
+    def last_dots(i, acc):
+        rv, wv, sv = r[now, i], w[i], s[i]
+        n[i] = inv[i] * rv
+        pairs = ((rv, wv), (rv, sv), (wv, wv), (wv, sv), (sv, sv))
+        return tuple(a + fold(b * c) for a, (b, c) in zip(acc, pairs))
+
+    dots = lax.fori_loop(0, ni, last_dots, (zero_acc,) * 5)
+    reduce_start(CG_ITERS, dots)
     advance_x(now, alpha_old, beta_old)
+    for copy in outputs[3:]:
+        copy.start()
     sums = reduce_wait(last, 4)
     hist_ref[last - 1] = sums[3][0, 0]
-    _, _, beta, alpha = scalars(last, sums, gamma_old, pap_old)
-
-    def final(i, acc):
-        r_old = r[now, i]
-        s_new = w[i] + beta * s[i]
-        p_new = inv[i] * r_old + beta * p[i]
-        r_new = r_old - alpha * s_new
-        x_new = x[i] + alpha * p_new
-        x_stage[i] = x_new[:, 0:nj]
-        r_stage[i] = r_new[:, 0:nj]
-        return acc + fold(r_new * r_new)
-
-    acc = lax.fori_loop(0, ni, final, zero_acc)
-    outputs = [pltpu.make_async_copy(x_stage, x_hbm, out_sem.at[0]), pltpu.make_async_copy(r_stage, r_hbm, out_sem.at[1])]
-    for copy in outputs:
-        copy.start()
-    reduce_start(CG_ITERS, (acc,))
-    hist_ref[last] = reduce_wait(CG_ITERS, 1)[0][0, 0]
+    gamma = sums[0]
+    beta = gamma / gamma_old
+    alpha = gamma / (sums[1] + 2.0 * beta * sums[2] + beta * beta * pap_old)
+    alpha_ref[0] = alpha[0, 0]
+    beta_ref[0] = beta[0, 0]
+    rw, rs, ww, ws, ss = reduce_wait(CG_ITERS, 5)
+    hist_ref[last] = (sums[3] - 2.0 * alpha * (rw + beta * rs) + alpha * alpha * (ww + 2.0 * beta * ws + beta * beta * ss))[0, 0]
     for copy in outputs:
         copy.wait()
 
@@ -424,24 +485,29 @@
         block = vm(ni, nl, nj)
         padded = vm(ni + 2, nl + 2 * PAD, LANES)
         dma = pltpu.SemaphoreType.DMA
-        out_block = jax.ShapeDtypeStruct((ni, nl, nj), F32)
-        x_new, r_new, hist = pl.pallas_call(
+        out_block = jax.ShapeDtypeStruct((ni, nl, LANES), F32)
+        scalar_out = jax.ShapeDtypeStruct((1,), F32)
+        x_old, u, p, r_old, w, s, hist, alpha, beta = pl.pallas_call(
             functools.partial(solve_kernel, (ni, nl, nj), counts),
-            out_shape=(out_block, out_block, jax.ShapeDtypeStruct((CG_ITERS,), F32)),
+            out_shape=(out_block,) * 6 + (jax.ShapeDtypeStruct((CG_ITERS,), F32), scalar_out, scalar_out),
             in_specs=[any_spec] * 4,
-            out_specs=(any_spec, any_spec, pl.BlockSpec(memory_space=pltpu.SMEM)),
+            out_specs=(any_spec,) * 6 + (pl.BlockSpec(memory_space=pltpu.SMEM),) * 3,
             scratch_shapes=[
-                block, block, block, vm(nj, width), vm(ni, width), vm(ni, width), vm(-(-width // LANES) * LANES, LANES), block, block,
+                block, block, block, vm(nj, width), vm(ni, width), vm(ni, width), vm(-(-width // LANES) * LANES, LANES),
+                vm(2, nl, LANES), vm(nl // 2, LANES), vm(2, ni, LANES),
                 padded, padded, vm(ni + 1, nl, LANES), whole, whole, vm(ni, nl + 2 * PAD, LANES), whole,
                 whole, vm(2, ni, nl, LANES), whole, whole, whole, whole, whole,
                 vm(slots, nl // 2, LANES), vm(slots, 2, ni, LANES),
                 vm(slots, 2, nl, LANES), vm(slots, nl // 2, LANES), vm(slots, 2, ni, LANES),
                 vm(CG_ITERS + 1, 1, LANES), vm(CG_ITERS + 1, devices, 1, LANES),
                 dma((slots, 2)), dma((slots,)), dma((slots, 2)), dma((slots, 2)), dma((slots,)), dma((slots, 2)),
-                dma((CG_ITERS + 1,)), dma((CG_ITERS + 1,)), dma((6,)), dma((2,)),
+                dma((CG_ITERS + 1,)), dma((CG_ITERS + 1,)), dma((6,)), dma((6,)),
             ],
             compiler_params=pltpu.CompilerParams(has_side_effects=True, collective_id=0),
         )(k_ghost, flip(k_cell), flip(f_rhs), flip(u_init))
+        alpha, beta = alpha[0], beta[0]
+        x_new = (x_old + alpha * (u + beta * p))[:, :, 0:nj]
+        r_new = (r_old - alpha * (w + beta * s))[:, :, 0:nj]
         return flip(x_new), flip(r_new), hist
 
     return jax.shard_map(local_solve, mesh=mesh, in_specs=(grid_spec, P(), grid_spec, grid_spec),

time: 82.8 us -> 76.3 us (0.921)
  Pallas kernels: 78 us -> 68.7 us
  other arithmetic: 0 us -> 6.26 us
  local copies, waits for them, and re-layouts: 3.99 us -> 0.52 us
    pallas_call x1, Pallas kernels: 78 us -> 68.7 us  [local_solve(): pl.pallas_call(functools.partial(solve_kernel, (ni, nl, nj), counts), out...]
    transpose x0 -> x1, other arithmetic: none -> 6.26 us  [local_solve(): flip = lambda a: jnp.swapaxes(a, 1, 2)]
    unnamed x7 -> x3, local copies, waits for them, and re-layouts: 3.99 us -> 0.52 us
where the time goes in v4:
time: 76.3 us; the launch traced here: 76.1 us
  Pallas kernels  68.7 us (90%)
  other arithmetic  6.26 us (8%)
    pallas_call x1, Pallas kernels, local_solve(): pl.pallas_call(functools.partial(solve_kernel, (ni, nl, nj), counts), out...  68.7 us
    transpose x1, other arithmetic, local_solve(): flip = lambda a: jnp.swapaxes(a, 1, 2)  6.26 us

profile of v4, /device:TPU:0, one launch (start us, length us, event | category | flops | bytes accessed | tf_op | source)
XLA Modules:
  0.0 76.1 jit_solution(13489152379791001707)
XLA Ops:
  0.6 68.7 %shard_map.67 = (f32[48,48,128]{2,1,0:T(8,128)}, f32[48,48,128]{2,1,0:T(8,128)}, f32[48,48,128]{2,1,0:T(8,128)}, f32[48,48,128]{2,1,0:T(8,128)}, f32[48,48,128]{...) custom-call(f32[6,192,192]{2,1,0:T(8,128)} %kg_hbm.1, f32[48,48,96]{2,1,0:T(8,128)} %bitcast.9, ...), custom_call_target="tpu_custom_call" | custom-call | tf_op jit(solution)/shard_map/pallas_call | solution.py:490
  69.3 0.0 copy-start
  69.3 6.3 %fusion = (f32[48,96,48]{1,2,0:T(8,128)}, f32[48,96,48]{1,2,0:T(8,128)}) fusion(f32[48,48,128]{2,1,0:T(8,128)} %get-tuple-element.17, f32[48,48,128]{2,1,0:T(8,128)} %get-tuple-element.18, f32[48,48,128]{2,1,0:T(8,128)} %get-tuple-element.19, f32[]{:T(128)} %bitcast.3, f32[]{:T(128)} %bitcast.4, f32[48,48,128]{2,1,0:T(8,128)} %get-tuple-element.16, ...), kind=kLoop, calls=%fused_computation.1 | loop fusion | flops 1769472 | bytes 7077896 | tf_op jit(solution)/shard_map/transpose | solution.py:478
  75.6 0.0 copy-done
  75.6 0.5 copy.8
Async XLA Ops:
  69.3 6.3 %copy-start = (f32[8]{0:T(128)S(1)}, f32[8]{0:T(128)}, u32[]{:S(2)}) copy-start(f32[8]{0:T(128)} %get-tuple-element.28) | copy-start | bytes 100

commit v5 on v4

--- a/solution.py
+++ b/solution.py
@@ -16,11 +16,11 @@
 F32 = jnp.float32
 
 
-def solve_kernel(dims, counts, kg_hbm, k_hbm, f_hbm, u_hbm, x_hbm, u_last_hbm, p_hbm, r_hbm, w_hbm, s_hbm, hist_ref, alpha_ref, beta_ref,
+def solve_kernel(dims, counts, kg_hbm, k_hbm, f_hbm, u_hbm, x, n, p, r, w, s, hist_ref, alpha_ref, beta_ref,
                  k_in, f_in, u_in, wall_x, wall_y, wall_z, wall_t, bx, by, bz,
-                 kp, mp, cx, cy, cyh, cz, inv, x, r, w, s, z, p, n,
+                 kp, mp, cx, cy, cyh, cz, inv, z,
                  ys, zs, xr, yr, zr, red_s, red_r,
-                 xs_sem, ys_sem, zs_sem, xr_sem, yr_sem, zr_sem, rs_sem, rr_sem, in_sem, out_sem):
+                 xs_sem, ys_sem, zs_sem, xr_sem, yr_sem, zr_sem, rs_sem, rr_sem, in_sem):
     ni, nl, nj = dims
     ngx, ngy, ngz = counts
     half = nl // 2
@@ -440,10 +440,6 @@
 
     now = last % 2
     reduce_start(last, accs)
-    outputs = [pltpu.make_async_copy(src, dst, out_sem.at[j]) for j, (src, dst) in enumerate((
-        (r.at[now], r_hbm), (w, w_hbm), (s, s_hbm), (p, p_hbm), (x, x_hbm), (n, u_last_hbm)))]
-    for copy in outputs[:3]:
-        copy.start()
 
     def last_dots(i, acc):
         rv, wv, sv = r[now, i], w[i], s[i]
@@ -454,8 +450,6 @@
     dots = lax.fori_loop(0, ni, last_dots, (zero_acc,) * 5)
     reduce_start(CG_ITERS, dots)
     advance_x(now, alpha_old, beta_old)
-    for copy in outputs[3:]:
-        copy.start()
     sums = reduce_wait(last, 4)
     hist_ref[last - 1] = sums[3][0, 0]
     gamma = sums[0]
@@ -465,7 +459,24 @@
     beta_ref[0] = beta[0, 0]
     rw, rs, ww, ws, ss = reduce_wait(CG_ITERS, 5)
     hist_ref[last] = (sums[3] - 2.0 * alpha * (rw + beta * rs) + alpha * alpha * (ww + 2.0 * beta * ws + beta * beta * ss))[0, 0]
-    for copy in outputs:
+
+
+def finish_kernel(chunk, alpha_ref, beta_ref, hist_ref, x, u, p, r, w, s, x_hbm, r_hbm, hist_hbm, x_new, r_new, sem, hist_sem):
+    ni, _, nj = x_new.shape
+    alpha, beta = alpha_ref[0], beta_ref[0]
+    copies = [pltpu.make_async_copy(hist_ref, hist_hbm, hist_sem)]
+    copies[0].start()
+    for g in range(ni // chunk):
+        def step(i, _):
+            x_new[i] = (x[i] + alpha * (u[i] + beta * p[i]))[:, 0:nj]
+            r_new[i] = (r[1, i] - alpha * (w[i] + beta * s[i]))[:, 0:nj]
+            return 0
+        lax.fori_loop(g * chunk, (g + 1) * chunk, step, 0)
+        part = pl.ds(g * chunk, chunk)
+        for j, (src, dst) in enumerate(((x_new, x_hbm), (r_new, r_hbm))):
+            copies.append(pltpu.make_async_copy(src.at[part], dst.at[part], sem.at[j, g]))
+            copies[-1].start()
+    for copy in copies:
         copy.wait()
 
 
@@ -485,29 +496,38 @@
         block = vm(ni, nl, nj)
         padded = vm(ni + 2, nl + 2 * PAD, LANES)
         dma = pltpu.SemaphoreType.DMA
-        out_block = jax.ShapeDtypeStruct((ni, nl, LANES), F32)
+        kept = pltpu.VMEM((ni, nl, LANES), F32)
         scalar_out = jax.ShapeDtypeStruct((1,), F32)
-        x_old, u, p, r_old, w, s, hist, alpha, beta = pl.pallas_call(
+        vmem_spec, smem_spec = pl.BlockSpec(memory_space=pltpu.VMEM), pl.BlockSpec(memory_space=pltpu.SMEM)
+        *state, hist, alpha, beta = pl.pallas_call(
             functools.partial(solve_kernel, (ni, nl, nj), counts),
-            out_shape=(out_block,) * 6 + (jax.ShapeDtypeStruct((CG_ITERS,), F32), scalar_out, scalar_out),
+            out_shape=(kept, kept, kept, pltpu.VMEM((2, ni, nl, LANES), F32), kept, kept,
+                       jax.ShapeDtypeStruct((CG_ITERS,), F32), scalar_out, scalar_out),
             in_specs=[any_spec] * 4,
-            out_specs=(any_spec,) * 6 + (pl.BlockSpec(memory_space=pltpu.SMEM),) * 3,
+            out_specs=(vmem_spec,) * 6 + (smem_spec,) * 3,
             scratch_shapes=[
                 block, block, block, vm(nj, width), vm(ni, width), vm(ni, width), vm(-(-width // LANES) * LANES, LANES),
                 vm(2, nl, LANES), vm(nl // 2, LANES), vm(2, ni, LANES),
                 padded, padded, vm(ni + 1, nl, LANES), whole, whole, vm(ni, nl + 2 * PAD, LANES), whole,
-                whole, vm(2, ni, nl, LANES), whole, whole, whole, whole, whole,
+                whole,
                 vm(slots, nl // 2, LANES), vm(slots, 2, ni, LANES),
                 vm(slots, 2, nl, LANES), vm(slots, nl // 2, LANES), vm(slots, 2, ni, LANES),
                 vm(CG_ITERS + 1, 1, LANES), vm(CG_ITERS + 1, devices, 1, LANES),
                 dma((slots, 2)), dma((slots,)), dma((slots, 2)), dma((slots, 2)), dma((slots,)), dma((slots, 2)),
-                dma((CG_ITERS + 1,)), dma((CG_ITERS + 1,)), dma((6,)), dma((6,)),
+                dma((CG_ITERS + 1,)), dma((CG_ITERS + 1,)), dma((6,)),
             ],
-            compiler_params=pltpu.CompilerParams(has_side_effects=True, collective_id=0),
-        )(k_ghost, flip(k_cell), flip(f_rhs), flip(u_init))
-        alpha, beta = alpha[0], beta[0]
-        x_new = (x_old + alpha * (u + beta * p))[:, :, 0:nj]
-        r_new = (r_old - alpha * (w + beta * s))[:, :, 0:nj]
+            compiler_params=pltpu.CompilerParams(has_side_effects=True, collective_id=0, vmem_limit_bytes=28 << 20),
+        )(*(pltpu.with_memory_space_constraint(a, pltpu.HBM) for a in (k_ghost, flip(k_cell), flip(f_rhs), flip(u_init))))
+        chunk = ni // 4
+        out_block = jax.ShapeDtypeStruct((ni, nl, nj), F32)
+        x_new, r_new, hist = pl.pallas_call(
+            functools.partial(finish_kernel, chunk),
+            out_shape=(out_block, out_block, jax.ShapeDtypeStruct((CG_ITERS,), F32)),
+            in_specs=[smem_spec] * 3 + [vmem_spec] * 6,
+            out_specs=(any_spec,) * 3,
+            scratch_shapes=[block, block, dma((2, ni // chunk)), dma],
+            compiler_params=pltpu.CompilerParams(vmem_limit_bytes=28 << 20),
+        )(alpha, beta, hist, *state)
         return flip(x_new), flip(r_new), hist
 
     return jax.shard_map(local_solve, mesh=mesh, in_specs=(grid_spec, P(), grid_spec, grid_spec),

time: 76.3 us -> 73.2 us (0.959)
  other arithmetic: 6.26 us -> 0 us
  Pallas kernels: 68.7 us -> 72.4 us
    transpose x1 -> x0, other arithmetic: 6.26 us -> none  [local_solve(): flip = lambda a: jnp.swapaxes(a, 1, 2)]
    pallas_call x0 -> x1, Pallas kernels: none -> 3.42 us  [local_solve(): pl.pallas_call(functools.partial(finish_kernel, chunk), out_shape=(out_bl...]
where the time goes in v5:
time: 73.2 us; the launch traced here: 73 us
  Pallas kernels  72.4 us (99%)
    pallas_call x1, Pallas kernels, local_solve(): pl.pallas_call(functools.partial(solve_kernel, (ni, nl, nj), counts), out...  69 us
    pallas_call x1, Pallas kernels, local_solve(): pl.pallas_call(functools.partial(finish_kernel, chunk), out_shape=(out_bl...  3.42 us

profile of v5, /device:TPU:0, one launch (start us, length us, event | category | flops | bytes accessed | tf_op | source)
XLA Modules:
  0.0 73.0 jit_solution(14350193410264424892)
XLA Ops:
  0.6 69.0 %shard_map.67 = (f32[48,48,128]{2,1,0:T(8,128)S(1)}, f32[48,48,128]{2,1,0:T(8,128)S(1)}, f32[48,48,128]{2,1,0:T(8,128)S(1)}, f32[2,48,48,128]{3,2,1,0:T(8,128)S(...) custom-call(f32[6,192,192]{2,1,0:T(8,128)} %kg_hbm.1, ...), custom_call_target="tpu_custom_call" | custom-call | tf_op jit(solution)/shard_map/pallas_call | solution.py:502
  69.6 3.4 %shard_map.68 = (f32[48,48,96]{2,1,0:T(8,128)}, f32[48,48,96]{2,1,0:T(8,128)}, f32[8]{0:T(128)}) custom-call(f32[1]{0:T(128)} %get-tuple-element.15.alpha_ref, f32[1]{0:T(128)} %get-tuple-element.16.beta_ref, f32[8]{0:T(128)S(1)} %get-tuple-element.17.hist_ref, f32[48,48,128]{2,1,0:T(8,128)S(1)} %get-tuple-element.18.x, ...), custom_call_target="tpu_custom_call" | custom-call | tf_op jit(solution)/shard_map/pallas_call | solution.py:523

commit v6 on v5

--- a/solution.py
+++ b/solution.py
@@ -16,11 +16,11 @@
 F32 = jnp.float32
 
 
-def solve_kernel(dims, counts, kg_hbm, k_hbm, f_hbm, u_hbm, x, n, p, r, w, s, hist_ref, alpha_ref, beta_ref,
+def solve_kernel(dims, counts, kg_hbm, k_hbm, f_hbm, u_hbm, x, n, p, r, w, s, scal_ref,
                  k_in, f_in, u_in, wall_x, wall_y, wall_z, wall_t, bx, by, bz,
                  kp, mp, cx, cy, cyh, cz, inv, z,
                  ys, zs, xr, yr, zr, red_s, red_r,
-                 xs_sem, ys_sem, zs_sem, xr_sem, yr_sem, zr_sem, rs_sem, rr_sem, in_sem):
+                 xs_sem, ys_sem, zs_sem, xr_sem, yr_sem, zr_sem, rs_sem, rr_sem, in_sem, near_sem):
     ni, nl, nj = dims
     ngx, ngy, ngz = counts
     half = nl // 2
@@ -232,9 +232,24 @@
     for copy in inputs:
         copy.start()
 
+    def tell_neighbours(sem):
+        tell = lambda *target: pl.semaphore_signal(sem, inc=1, device_id=target, device_id_type=MESH)
+        pl.when(has_xlo)(lambda: tell(gz, gy, gx - 1))
+        pl.when(has_xhi)(lambda: tell(gz, gy, gx + 1))
+        pl.when(has_zlo)(lambda: tell(gz - 1, gy, gx))
+        pl.when(has_zhi)(lambda: tell(gz + 1, gy, gx))
+        tell(gz, 1 - gy, gx)
+
+    neighbours = 5 - jnp.where(has_xlo, 0, 1) - jnp.where(has_xhi, 0, 1) - jnp.where(has_zlo, 0, 1) - jnp.where(has_zhi, 0, 1)
+    rounds = (ngx - 1) + (ngy - 1) + (ngz - 1) - 1
+
+    def next_round(k):
+        pl.semaphore_wait(near_sem.at[k], neighbours)
+        if k + 1 < rounds:
+            tell_neighbours(near_sem.at[k + 1])
+
     barrier = pltpu.get_barrier_semaphore()
-    for delta in relative:
-        pl.semaphore_signal(barrier, inc=1, device_id=other(*delta), device_id_type=MESH)
+    tell_neighbours(barrier)
 
     for edge in (0, ni + 1):
         mp[edge] = jnp.zeros((nl + 2 * PAD, LANES), F32)
@@ -266,11 +281,13 @@
 
     inputs[0].wait()
     packed_pass(kp, 0, load_k, 0)
-    pl.semaphore_wait(barrier, len(relative))
+    pl.semaphore_wait(barrier, neighbours)
+    tell_neighbours(near_sem.at[0])
     exchange_start(kp, 0)
     inputs[1].wait()
     packed_pass(mp, 1, load_u, 0)
     exchange_start(mp, 1)
+    next_round(0)
 
     for copy in inputs[2:5]:
         copy.wait()
@@ -299,6 +316,8 @@
     def harmonic(left, right):
         return 2.0 * left * right / (left + right)
 
+    next_round(1)
+
     in_i = lane_i < nj
     cx[0] = jnp.where(jnp.logical_and(inside, gx == 0), harmonic(x_wall, kp[1, rows, :]), 0.0)
     z_low = jnp.where(jnp.logical_and(in_i, gz == 0), harmonic(z_wall, zs[0, 1]), 0.0)
@@ -319,6 +338,7 @@
         return 0
 
     slabs(GROUP, coefs, 0)
+    next_round(2)
     cx[ni] = jnp.where(jnp.logical_and(inside, gx == ngx - 1), harmonic(kp[ni, rows, :], x_wall), 0.0)
     for i in range(ni):
         cz[i, PAD:PAD + 1, :] = z_low[i:i + 1, :]
@@ -331,6 +351,7 @@
         return 0
 
     lax.fori_loop(0, ni, diagonal, 0)
+    next_round(3)
 
     exchange_wait(kp, 0)
 
@@ -373,7 +394,10 @@
 
     gamma_acc = packed_pass(mp, 2, first_residual, zero_acc)
     exchange_start(mp, 2)
+    next_round(4)
     stencil(mp)
+    for k in range(5, rounds):
+        next_round(k)
     join_faces(mp, 2)
 
     def first_w(i, acc):
@@ -427,9 +451,7 @@
 
         accs = packed_pass(mp, t + 4, update, (zero_acc,) * 4)
 
-        @pl.when(t > 0)
-        def _():
-            hist_ref[lax.max(t - 1, 0)] = sums[3][0, 0]
+        scal_ref[lax.rem(t + CG_ITERS - 1, CG_ITERS)] = jnp.broadcast_to(sums[3], (1, LANES))
 
         return accs, gamma, pap, alpha, beta
 
@@ -451,30 +473,38 @@
     reduce_start(CG_ITERS, dots)
     advance_x(now, alpha_old, beta_old)
     sums = reduce_wait(last, 4)
-    hist_ref[last - 1] = sums[3][0, 0]
+    wide = lambda value: jnp.broadcast_to(value, (1, LANES))
+    scal_ref[last - 1] = wide(sums[3])
     gamma = sums[0]
     beta = gamma / gamma_old
     alpha = gamma / (sums[1] + 2.0 * beta * sums[2] + beta * beta * pap_old)
-    alpha_ref[0] = alpha[0, 0]
-    beta_ref[0] = beta[0, 0]
+    scal_ref[CG_ITERS] = wide(alpha)
+    scal_ref[CG_ITERS + 1] = wide(beta)
     rw, rs, ww, ws, ss = reduce_wait(CG_ITERS, 5)
-    hist_ref[last] = (sums[3] - 2.0 * alpha * (rw + beta * rs) + alpha * alpha * (ww + 2.0 * beta * ws + beta * beta * ss))[0, 0]
-
-
-def finish_kernel(chunk, alpha_ref, beta_ref, hist_ref, x, u, p, r, w, s, x_hbm, r_hbm, hist_hbm, x_new, r_new, sem, hist_sem):
-    ni, _, nj = x_new.shape
-    alpha, beta = alpha_ref[0], beta_ref[0]
-    copies = [pltpu.make_async_copy(hist_ref, hist_hbm, hist_sem)]
-    copies[0].start()
+    scal_ref[last] = wide(sums[3] - 2.0 * alpha * (rw + beta * rs) + alpha * alpha * (ww + 2.0 * beta * ws + beta * beta * ss))
+
+
+def finish_kernel(chunk, scal, x, u, p, r, w, s, x_hbm, r_hbm, hist_hbm, x_new, r_new, hist, sem, hist_sem):
+    ni, nl, nj = x_new.shape
+    alpha = jnp.broadcast_to(scal[CG_ITERS], (nl, LANES))
+    beta = jnp.broadcast_to(scal[CG_ITERS + 1], (nl, LANES))
+    copies = []
+
+    def step(i, _):
+        x_new[i] = (x[i] + alpha * (u[i] + beta * p[i]))[:, 0:nj]
+        r_new[i] = (r[1, i] - alpha * (w[i] + beta * s[i]))[:, 0:nj]
+        return 0
+
     for g in range(ni // chunk):
-        def step(i, _):
-            x_new[i] = (x[i] + alpha * (u[i] + beta * p[i]))[:, 0:nj]
-            r_new[i] = (r[1, i] - alpha * (w[i] + beta * s[i]))[:, 0:nj]
-            return 0
         lax.fori_loop(g * chunk, (g + 1) * chunk, step, 0)
         part = pl.ds(g * chunk, chunk)
         for j, (src, dst) in enumerate(((x_new, x_hbm), (r_new, r_hbm))):
             copies.append(pltpu.make_async_copy(src.at[part], dst.at[part], sem.at[j, g]))
+            copies[-1].start()
+        if g == 0:
+            for t in range(CG_ITERS):
+                hist[t] = scal[t, 0, 0]
+            copies.append(pltpu.make_async_copy(hist, hist_hbm, hist_sem))
             copies[-1].start()
     for copy in copies:
         copy.wait()
@@ -497,14 +527,13 @@
         padded = vm(ni + 2, nl + 2 * PAD, LANES)
         dma = pltpu.SemaphoreType.DMA
         kept = pltpu.VMEM((ni, nl, LANES), F32)
-        scalar_out = jax.ShapeDtypeStruct((1,), F32)
-        vmem_spec, smem_spec = pl.BlockSpec(memory_space=pltpu.VMEM), pl.BlockSpec(memory_space=pltpu.SMEM)
-        *state, hist, alpha, beta = pl.pallas_call(
+        vmem_spec = pl.BlockSpec(memory_space=pltpu.VMEM)
+        *state, scal = pl.pallas_call(
             functools.partial(solve_kernel, (ni, nl, nj), counts),
             out_shape=(kept, kept, kept, pltpu.VMEM((2, ni, nl, LANES), F32), kept, kept,
-                       jax.ShapeDtypeStruct((CG_ITERS,), F32), scalar_out, scalar_out),
+                       pltpu.VMEM((CG_ITERS + 2, 1, LANES), F32)),
             in_specs=[any_spec] * 4,
-            out_specs=(vmem_spec,) * 6 + (smem_spec,) * 3,
+            out_specs=(vmem_spec,) * 7,
             scratch_shapes=[
                 block, block, block, vm(nj, width), vm(ni, width), vm(ni, width), vm(-(-width // LANES) * LANES, LANES),
                 vm(2, nl, LANES), vm(nl // 2, LANES), vm(2, ni, LANES),
@@ -514,7 +543,7 @@
                 vm(slots, 2, nl, LANES), vm(slots, nl // 2, LANES), vm(slots, 2, ni, LANES),
                 vm(CG_ITERS + 1, 1, LANES), vm(CG_ITERS + 1, devices, 1, LANES),
                 dma((slots, 2)), dma((slots,)), dma((slots, 2)), dma((slots, 2)), dma((slots,)), dma((slots, 2)),
-                dma((CG_ITERS + 1,)), dma((CG_ITERS + 1,)), dma((6,)),
+                dma((CG_ITERS + 1,)), dma((CG_ITERS + 1,)), dma((6,)), pltpu.SemaphoreType.REGULAR((6,)),
             ],
             compiler_params=pltpu.CompilerParams(has_side_effects=True, collective_id=0, vmem_limit_bytes=28 << 20),
         )(*(pltpu.with_memory_space_constraint(a, pltpu.HBM) for a in (k_ghost, flip(k_cell), flip(f_rhs), flip(u_init))))
@@ -523,11 +552,11 @@
         x_new, r_new, hist = pl.pallas_call(
             functools.partial(finish_kernel, chunk),
             out_shape=(out_block, out_block, jax.ShapeDtypeStruct((CG_ITERS,), F32)),
-            in_specs=[smem_spec] * 3 + [vmem_spec] * 6,
+            in_specs=[vmem_spec] * 7,
             out_specs=(any_spec,) * 3,
-            scratch_shapes=[block, block, dma((2, ni // chunk)), dma],
+            scratch_shapes=[block, block, pltpu.SMEM((CG_ITERS,), F32), dma((2, ni // chunk)), dma],
             compiler_params=pltpu.CompilerParams(vmem_limit_bytes=28 << 20),
-        )(alpha, beta, hist, *state)
+        )(scal, *state)
         return flip(x_new), flip(r_new), hist
 
     return jax.shard_map(local_solve, mesh=mesh, in_specs=(grid_spec, P(), grid_spec, grid_spec),

time: 73.2 us -> 70.6 us (0.964)
  Pallas kernels: 72.4 us -> 69.8 us
    pallas_call x1, Pallas kernels: 3.42 us -> 1.63 us  [local_solve(): pl.pallas_call(functools.partial(finish_kernel, chunk), out_shape=(out_bl...]
    pallas_call x1, Pallas kernels: 69 us -> 68.1 us  [local_solve(): pl.pallas_call(functools.partial(solve_kernel, (ni, nl, nj), counts), out...]
where the time goes in v6:
time: 70.6 us; the launch traced here: 70.4 us
  Pallas kernels  69.8 us (99%)
    pallas_call x1, Pallas kernels, local_solve(): pl.pallas_call(functools.partial(solve_kernel, (ni, nl, nj), counts), out...  68.1 us
    pallas_call x1, Pallas kernels, local_solve(): pl.pallas_call(functools.partial(finish_kernel, chunk), out_shape=(out_bl...  1.63 us

profile of v6, /device:TPU:0, one launch (start us, length us, event | category | flops | bytes accessed | tf_op | source)
XLA Modules:
  0.0 70.4 jit_solution(129920930612210596)
XLA Ops:
  0.6 68.1 %shard_map.67 = (f32[48,48,128]{2,1,0:T(8,128)S(1)}, f32[48,48,128]{2,1,0:T(8,128)S(1)}, f32[48,48,128]{2,1,0:T(8,128)S(1)}, f32[2,48,48,128]{3,2,1,0:T(8,128)S(...) custom-call(f32[6,192,192]{2,1,0:T(8,128)} %kg_hbm.1, ...), custom_call_target="tpu_custom_call" | custom-call | tf_op jit(solution)/shard_map/pallas_call | solution.py:531
  68.8 1.6 %shard_map.68 = (f32[48,48,96]{2,1,0:T(8,128)}, f32[48,48,96]{2,1,0:T(8,128)}, f32[8]{0:T(128)}) custom-call(f32[10,1,128]{2,1,0:T(1,128)S(1)} %get-tuple-element.13.scal, f32[48,48,128]{2,1,0:T(8,128)S(1)} %get-tuple-element.14.x, f32[48,48,128]{2,1,0:T(8,128)S(1)} %get-tuple-element.15.u, f32[48,48,128]{2,1,0:T(8,128)S(1)} %get-tuple-element.16.p, ...), custom_call_target="tpu_custom_call" | custom-call | tf_op jit(solution)/shard_map/pallas_call | solution.py:552

commit v7 on v6

--- a/solution.py
+++ b/solution.py
@@ -18,7 +18,7 @@
 
 def solve_kernel(dims, counts, kg_hbm, k_hbm, f_hbm, u_hbm, x, n, p, r, w, s, scal_ref,
                  k_in, f_in, u_in, wall_x, wall_y, wall_z, wall_t, bx, by, bz,
-                 kp, mp, cx, cy, cyh, cz, inv, z,
+                 kp, mp, cx, cy, cyh, cz, inv, dg, z,
                  ys, zs, xr, yr, zr, red_s, red_r,
                  xs_sem, ys_sem, zs_sem, xr_sem, yr_sem, zr_sem, rs_sem, rr_sem, in_sem, near_sem):
     ni, nl, nj = dims
@@ -83,7 +83,7 @@
         acc = jnp.where(lane_half == i, rolled[0], acc)
         return jnp.where(lane_half == i + LANES // 2, rolled[1], acc)
 
-    def packed_pass(ref, slot, step, init):
+    def packed_pass(ref, slot, step, init, tail=lambda state: state):
         def body(g, carry):
             state, acc = carry
             rolled = [pack_rolls(ref, slot, (g - 1) * GROUP + k) for k in range(GROUP)]
@@ -94,6 +94,7 @@
             return state, acc
         state, acc = lax.fori_loop(0, ni // GROUP, body, (init, jnp.zeros((half, LANES), F32)))
         rolled = [pack_rolls(ref, slot, ni - GROUP + k) for k in range(GROUP)]
+        state = tail(state)
         for k in range(GROUP):
             acc = pack(ni - GROUP + k, rolled[k], acc)
         ys[slot] = acc
@@ -197,13 +198,15 @@
             out = out + slab[part:part + 8]
         return out
 
-    def reduce_start(slot, accs):
+    def reduce_row(slot, accs):
         row = jnp.zeros((1, LANES), F32)
         for q, acc in enumerate(accs):
             row = jnp.where(lane_row == q, jnp.sum(jnp.sum(acc, axis=0, keepdims=True), axis=1, keepdims=True), row)
+        red_s[slot] = row
+        red_r[slot, (gz * ngy + gy) * ngx + gx] = row
+
+    def reduce_send(slot):
         me = (gz * ngy + gy) * ngx + gx
-        red_s[slot] = row
-        red_r[slot, me] = row
         for delta in relative:
             pltpu.make_async_remote_copy(
                 src_ref=red_s.at[slot], dst_ref=red_r.at[slot, me], send_sem=rs_sem.at[slot],
@@ -229,7 +232,7 @@
         pltpu.make_async_copy(kg_hbm.at[z_row, slabs_i], wall_z, in_sem.at[4]),
         pltpu.make_async_copy(f_hbm, f_in, in_sem.at[5]),
     ]
-    for copy in inputs:
+    for copy in inputs[:5]:
         copy.start()
 
     def tell_neighbours(sem):
@@ -280,6 +283,7 @@
         return 0
 
     inputs[0].wait()
+    inputs[5].start()
     packed_pass(kp, 0, load_k, 0)
     pl.semaphore_wait(barrier, neighbours)
     tell_neighbours(near_sem.at[0])
@@ -347,7 +351,7 @@
     stencil(mp)
 
     def diagonal(i, _):
-        inv[i] = cx[i] + cx[i + 1] + cy[i] + cyh[i] + cz[i, rows, :] + cz[i, rows_up, :]
+        dg[i] = cx[i] + cx[i + 1] + cy[i] + cyh[i] + cz[i, rows, :] + cz[i, rows_up, :]
         return 0
 
     lax.fori_loop(0, ni, diagonal, 0)
@@ -358,31 +362,31 @@
     @pl.when(has_xlo)
     def _():
         bx[0] = jnp.where(inside, harmonic(xr[0, 0], kp[1, rows, :]), 0.0)
-        inv[0] = inv[0] + bx[0]
+        dg[0] = dg[0] + bx[0]
 
     @pl.when(has_xhi)
     def _():
         bx[1] = jnp.where(inside, harmonic(kp[ni, rows, :], xr[0, 1]), 0.0)
-        inv[ni - 1] = inv[ni - 1] + bx[1]
+        dg[ni - 1] = dg[ni - 1] + bx[1]
 
     @pl.when(has_zlo)
     def _():
         bz[0] = jnp.where(in_i, harmonic(zr[0, 0], zs[0, 1]), 0.0)
-        add_rows(inv, bz[0], 0)
+        add_rows(dg, bz[0], 0)
 
     @pl.when(has_zhi)
     def _():
         bz[1] = jnp.where(in_i, harmonic(zs[0, 0], zr[0, 1]), 0.0)
-        add_rows(inv, bz[1], nl - 1)
+        add_rows(dg, bz[1], nl - 1)
 
     y_face = jnp.where(lax.rem(lane_half, LANES // 2) < ni, harmonic(ys[0], yr[0]), 0.0)
     by[...] = y_face
-    add_columns(inv, y_face)
+    add_columns(dg, y_face)
     join_faces(mp, 1)
     inputs[5].wait()
 
     def first_residual(i, acc):
-        iv = jnp.where(inside, 1.0 / jnp.where(inside, inv[i], 1.0), 0.0)
+        iv = jnp.where(inside, 1.0 / jnp.where(inside, dg[i], 1.0), 0.0)
         inv[i] = iv
         x[i] = mp[i + 1, rows, :]
         r[0, i, :, 0:nj] = f_in[i]
@@ -402,12 +406,11 @@
 
     def first_w(i, acc):
         av = n[i]
-        w[i] = av
         acc = acc + fold(av * mp[i + 1, rows, :])
         mp[i + 1, rows, :] = av * inv[i]
         return acc
 
-    delta_acc = packed_pass(mp, 3, first_w, zero_acc)
+    packed_pass(mp, 3, first_w, zero_acc, lambda delta_acc: reduce_row(0, (gamma_acc, delta_acc)))
 
     def scalars(t, sums, gamma_old, pap_old):
         gamma, delta, sigma = sums[0], sums[1], sums[2]
@@ -416,72 +419,72 @@
         return gamma, pap, beta[0, 0], (gamma / pap)[0, 0]
 
     def advance_x(now, alpha, beta):
-        def step(i, _):
+        def step(i, acc):
             p_new = inv[i] * r[1 - now, i] + beta * p[i]
             p[i] = p_new
             x[i] = x[i] + alpha * p_new
-            return 0
-        lax.fori_loop(0, ni, step, 0)
+            return acc + fold(r[now, i] * r[now, i])
+        return lax.fori_loop(0, ni, step, zero_acc)
 
     def iteration(t, carry):
-        accs, gamma_old, pap_old, alpha_old, beta_old = carry
+        gamma_old, pap_old, alpha_old, beta_old = carry
         now = lax.rem(t, 2)
-        reduce_start(t, accs)
         exchange_start(mp, t + 3)
+        reduce_send(t)
         stencil(mp)
-        advance_x(now, alpha_old, beta_old)
+        rr_acc = advance_x(now, alpha_old, beta_old)
         join_faces(mp, t + 3)
         sums = reduce_wait(t, 4)
         gamma, pap, beta, alpha = scalars(t, sums, gamma_old, pap_old)
 
         def update(i, acc):
             iv = inv[i]
+            w_old = dg[i] * mp[i + 1, rows, :]
             z_new = n[i] + beta * z[i]
-            s_new = w[i] + beta * s[i]
+            s_new = w_old + beta * s[i]
             r_new = r[now, i] - alpha * s_new
-            w_new = w[i] - alpha * z_new
+            w_new = w_old - alpha * z_new
             u_new = iv * r_new
             z[i] = z_new
             s[i] = s_new
             r[1 - now, i] = r_new
-            w[i] = w_new
             mp[i + 1, rows, :] = iv * w_new
-            return (acc[0] + fold(r_new * u_new), acc[1] + fold(w_new * u_new),
-                    acc[2] + fold(u_new * s_new), acc[3] + fold(r_new * r_new))
-
-        accs = packed_pass(mp, t + 4, update, (zero_acc,) * 4)
-
-        scal_ref[lax.rem(t + CG_ITERS - 1, CG_ITERS)] = jnp.broadcast_to(sums[3], (1, LANES))
-
-        return accs, gamma, pap, alpha, beta
+            return acc[0] + fold(r_new * u_new), acc[1] + fold(w_new * u_new), acc[2] + fold(u_new * s_new)
+
+        packed_pass(mp, t + 4, update, (zero_acc,) * 3, lambda accs: reduce_row(t + 1, accs + (rr_acc,)))
+        scal_ref[lax.rem(t + CG_ITERS - 2, CG_ITERS)] = jnp.broadcast_to(sums[3], (1, LANES))
+        return gamma, pap, alpha, beta
 
     one = jnp.ones((1, 1), F32)
     last = CG_ITERS - 1
-    accs, gamma_old, pap_old, alpha_old, beta_old = lax.fori_loop(
-        0, last, iteration, ((gamma_acc, delta_acc, zero_acc, zero_acc), one, one, jnp.float32(0.0), jnp.float32(0.0)))
+    gamma_old, pap_old, alpha_old, beta_old = lax.fori_loop(
+        0, last, iteration, (one, one, jnp.float32(0.0), jnp.float32(0.0)))
 
     now = last % 2
-    reduce_start(last, accs)
+    reduce_send(last)
 
     def last_dots(i, acc):
-        rv, wv, sv = r[now, i], w[i], s[i]
+        rv, sv = r[now, i], s[i]
+        wv = dg[i] * mp[i + 1, rows, :]
+        w[i] = wv
         n[i] = inv[i] * rv
-        pairs = ((rv, wv), (rv, sv), (wv, wv), (wv, sv), (sv, sv))
+        pairs = ((rv, rv), (rv, wv), (rv, sv), (wv, wv), (wv, sv), (sv, sv))
         return tuple(a + fold(b * c) for a, (b, c) in zip(acc, pairs))
 
-    dots = lax.fori_loop(0, ni, last_dots, (zero_acc,) * 5)
-    reduce_start(CG_ITERS, dots)
+    reduce_row(CG_ITERS, slabs(2, last_dots, (zero_acc,) * 6))
+    reduce_send(CG_ITERS)
     advance_x(now, alpha_old, beta_old)
     sums = reduce_wait(last, 4)
     wide = lambda value: jnp.broadcast_to(value, (1, LANES))
-    scal_ref[last - 1] = wide(sums[3])
+    scal_ref[last - 2] = wide(sums[3])
     gamma = sums[0]
     beta = gamma / gamma_old
     alpha = gamma / (sums[1] + 2.0 * beta * sums[2] + beta * beta * pap_old)
     scal_ref[CG_ITERS] = wide(alpha)
     scal_ref[CG_ITERS + 1] = wide(beta)
-    rw, rs, ww, ws, ss = reduce_wait(CG_ITERS, 5)
-    scal_ref[last] = wide(sums[3] - 2.0 * alpha * (rw + beta * rs) + alpha * alpha * (ww + 2.0 * beta * ws + beta * beta * ss))
+    rr, rw, rs, ww, ws, ss = reduce_wait(CG_ITERS, 6)
+    scal_ref[last - 1] = wide(rr)
+    scal_ref[last] = wide(rr - 2.0 * alpha * (rw + beta * rs) + alpha * alpha * (ww + 2.0 * beta * ws + beta * beta * ss))
 
 
 def finish_kernel(chunk, scal, x, u, p, r, w, s, x_hbm, r_hbm, hist_hbm, x_new, r_new, hist, sem, hist_sem):
@@ -538,7 +541,7 @@
                 block, block, block, vm(nj, width), vm(ni, width), vm(ni, width), vm(-(-width // LANES) * LANES, LANES),
                 vm(2, nl, LANES), vm(nl // 2, LANES), vm(2, ni, LANES),
                 padded, padded, vm(ni + 1, nl, LANES), whole, whole, vm(ni, nl + 2 * PAD, LANES), whole,
-                whole,
+                whole, whole,
                 vm(slots, nl // 2, LANES), vm(slots, 2, ni, LANES),
                 vm(slots, 2, nl, LANES), vm(slots, nl // 2, LANES), vm(slots, 2, ni, LANES),
                 vm(CG_ITERS + 1, 1, LANES), vm(CG_ITERS + 1, devices, 1, LANES),

time: 70.6 us -> 72.9 us (1.033)
  Pallas kernels: 69.8 us -> 72.1 us
    pallas_call x1, Pallas kernels: 68.1 us -> 70.5 us  [local_solve(): pl.pallas_call(functools.partial(solve_kernel, (ni, nl, nj), counts), out...]
where the time goes in v7:
time: 72.9 us; the launch traced here: 72.8 us
  Pallas kernels  72.1 us (99%)
    pallas_call x1, Pallas kernels, local_solve(): pl.pallas_call(functools.partial(solve_kernel, (ni, nl, nj), counts), out...  70.5 us
    pallas_call x1, Pallas kernels, local_solve(): pl.pallas_call(functools.partial(finish_kernel, chunk), out_shape=(out_bl...  1.63 us

profile of v7, /device:TPU:0, one launch (start us, length us, event | category | flops | bytes accessed | tf_op | source)
XLA Modules:
  0.0 72.8 jit_solution(3185186465864729032)
XLA Ops:
  0.6 70.5 %shard_map.67 = (f32[48,48,128]{2,1,0:T(8,128)S(1)}, f32[48,48,128]{2,1,0:T(8,128)S(1)}, f32[48,48,128]{2,1,0:T(8,128)S(1)}, f32[2,48,48,128]{3,2,1,0:T(8,128)S(...) custom-call(f32[6,192,192]{2,1,0:T(8,128)} %kg_hbm.1, ...), custom_call_target="tpu_custom_call" | custom-call | tf_op jit(solution)/shard_map/pallas_call | solution.py:534
  71.1 1.6 %shard_map.68 = (f32[48,48,96]{2,1,0:T(8,128)}, f32[48,48,96]{2,1,0:T(8,128)}, f32[8]{0:T(128)}) custom-call(f32[10,1,128]{2,1,0:T(1,128)S(1)} %get-tuple-element.13.scal, f32[48,48,128]{2,1,0:T(8,128)S(1)} %get-tuple-element.14.x, f32[48,48,128]{2,1,0:T(8,128)S(1)} %get-tuple-element.15.u, f32[48,48,128]{2,1,0:T(8,128)S(1)} %get-tuple-element.16.p, ...), custom_call_target="tpu_custom_call" | custom-call | tf_op jit(solution)/shard_map/pallas_call | solution.py:555

commit v8 on v7

--- a/solution.py
+++ b/solution.py
@@ -18,7 +18,7 @@
 
 def solve_kernel(dims, counts, kg_hbm, k_hbm, f_hbm, u_hbm, x, n, p, r, w, s, scal_ref,
                  k_in, f_in, u_in, wall_x, wall_y, wall_z, wall_t, bx, by, bz,
-                 kp, mp, cx, cy, cyh, cz, inv, dg, z,
+                 kp, mp, cx, cy, cyh, cz, inv, z,
                  ys, zs, xr, yr, zr, red_s, red_r,
                  xs_sem, ys_sem, zs_sem, xr_sem, yr_sem, zr_sem, rs_sem, rr_sem, in_sem, near_sem):
     ni, nl, nj = dims
@@ -46,7 +46,7 @@
         return lax.rem(gz + a, ngz), lax.rem(gy + b, ngy), lax.rem(gx + c, ngx)
 
     def column_roll(slab, shift):
-        return pltpu.roll(slab, lax.rem(shift + 2 * LANES, LANES), 1)
+        return pltpu.roll(slab, shift + 2 * LANES, 1)
 
     def slabs(group, step, init):
         def body(g, carry):
@@ -351,7 +351,7 @@
     stencil(mp)
 
     def diagonal(i, _):
-        dg[i] = cx[i] + cx[i + 1] + cy[i] + cyh[i] + cz[i, rows, :] + cz[i, rows_up, :]
+        inv[i] = cx[i] + cx[i + 1] + cy[i] + cyh[i] + cz[i, rows, :] + cz[i, rows_up, :]
         return 0
 
     lax.fori_loop(0, ni, diagonal, 0)
@@ -362,31 +362,31 @@
     @pl.when(has_xlo)
     def _():
         bx[0] = jnp.where(inside, harmonic(xr[0, 0], kp[1, rows, :]), 0.0)
-        dg[0] = dg[0] + bx[0]
+        inv[0] = inv[0] + bx[0]
 
     @pl.when(has_xhi)
     def _():
         bx[1] = jnp.where(inside, harmonic(kp[ni, rows, :], xr[0, 1]), 0.0)
-        dg[ni - 1] = dg[ni - 1] + bx[1]
+        inv[ni - 1] = inv[ni - 1] + bx[1]
 
     @pl.when(has_zlo)
     def _():
         bz[0] = jnp.where(in_i, harmonic(zr[0, 0], zs[0, 1]), 0.0)
-        add_rows(dg, bz[0], 0)
+        add_rows(inv, bz[0], 0)
 
     @pl.when(has_zhi)
     def _():
         bz[1] = jnp.where(in_i, harmonic(zs[0, 0], zr[0, 1]), 0.0)
-        add_rows(dg, bz[1], nl - 1)
+        add_rows(inv, bz[1], nl - 1)
 
     y_face = jnp.where(lax.rem(lane_half, LANES // 2) < ni, harmonic(ys[0], yr[0]), 0.0)
     by[...] = y_face
-    add_columns(dg, y_face)
+    add_columns(inv, y_face)
     join_faces(mp, 1)
     inputs[5].wait()
 
     def first_residual(i, acc):
-        iv = jnp.where(inside, 1.0 / jnp.where(inside, dg[i], 1.0), 0.0)
+        iv = jnp.where(inside, 1.0 / jnp.where(inside, inv[i], 1.0), 0.0)
         inv[i] = iv
         x[i] = mp[i + 1, rows, :]
         r[0, i, :, 0:nj] = f_in[i]
@@ -406,6 +406,7 @@
 
     def first_w(i, acc):
         av = n[i]
+        w[i] = av
         acc = acc + fold(av * mp[i + 1, rows, :])
         mp[i + 1, rows, :] = av * inv[i]
         return acc
@@ -429,8 +430,8 @@
     def iteration(t, carry):
         gamma_old, pap_old, alpha_old, beta_old = carry
         now = lax.rem(t, 2)
+        reduce_send(t)
         exchange_start(mp, t + 3)
-        reduce_send(t)
         stencil(mp)
         rr_acc = advance_x(now, alpha_old, beta_old)
         join_faces(mp, t + 3)
@@ -439,7 +440,7 @@
 
         def update(i, acc):
             iv = inv[i]
-            w_old = dg[i] * mp[i + 1, rows, :]
+            w_old = w[i]
             z_new = n[i] + beta * z[i]
             s_new = w_old + beta * s[i]
             r_new = r[now, i] - alpha * s_new
@@ -448,6 +449,7 @@
             z[i] = z_new
             s[i] = s_new
             r[1 - now, i] = r_new
+            w[i] = w_new
             mp[i + 1, rows, :] = iv * w_new
             return acc[0] + fold(r_new * u_new), acc[1] + fold(w_new * u_new), acc[2] + fold(u_new * s_new)
 
@@ -465,8 +467,7 @@
 
     def last_dots(i, acc):
         rv, sv = r[now, i], s[i]
-        wv = dg[i] * mp[i + 1, rows, :]
-        w[i] = wv
+        wv = w[i]
         n[i] = inv[i] * rv
         pairs = ((rv, rv), (rv, wv), (rv, sv), (wv, wv), (wv, sv), (sv, sv))
         return tuple(a + fold(b * c) for a, (b, c) in zip(acc, pairs))
@@ -541,7 +542,7 @@
                 block, block, block, vm(nj, width), vm(ni, width), vm(ni, width), vm(-(-width // LANES) * LANES, LANES),
                 vm(2, nl, LANES), vm(nl // 2, LANES), vm(2, ni, LANES),
                 padded, padded, vm(ni + 1, nl, LANES), whole, whole, vm(ni, nl + 2 * PAD, LANES), whole,
-                whole, whole,
+                whole,
                 vm(slots, nl // 2, LANES), vm(slots, 2, ni, LANES),
                 vm(slots, 2, nl, LANES), vm(slots, nl // 2, LANES), vm(slots, 2, ni, LANES),
                 vm(CG_ITERS + 1, 1, LANES), vm(CG_ITERS + 1, devices, 1, LANES),

time: 72.9 us -> 70.5 us (0.967)
  Pallas kernels: 72.1 us -> 69.7 us
    pallas_call x1, Pallas kernels: 70.5 us -> 68.1 us  [local_solve(): pl.pallas_call(functools.partial(solve_kernel, (ni, nl, nj), counts), out...]
where the time goes in v8:
time: 70.5 us; the launch traced here: 70.4 us
  Pallas kernels  69.7 us (99%)
    pallas_call x1, Pallas kernels, local_solve(): pl.pallas_call(functools.partial(solve_kernel, (ni, nl, nj), counts), out...  68.1 us
    pallas_call x1, Pallas kernels, local_solve(): pl.pallas_call(functools.partial(finish_kernel, chunk), out_shape=(out_bl...  1.63 us

profile of v8, /device:TPU:0, one launch (start us, length us, event | category | flops | bytes accessed | tf_op | source)
XLA Modules:
  0.0 70.4 jit_solution(4793672205212477071)
XLA Ops:
  0.6 68.1 %shard_map.67 = (f32[48,48,128]{2,1,0:T(8,128)S(1)}, f32[48,48,128]{2,1,0:T(8,128)S(1)}, f32[48,48,128]{2,1,0:T(8,128)S(1)}, f32[2,48,48,128]{3,2,1,0:T(8,128)S(...) custom-call(f32[6,192,192]{2,1,0:T(8,128)} %kg_hbm.1, ...), custom_call_target="tpu_custom_call" | custom-call | tf_op jit(solution)/shard_map/pallas_call | solution.py:535
  68.7 1.6 %shard_map.68 = (f32[48,48,96]{2,1,0:T(8,128)}, f32[48,48,96]{2,1,0:T(8,128)}, f32[8]{0:T(128)}) custom-call(f32[10,1,128]{2,1,0:T(1,128)S(1)} %get-tuple-element.13.scal, f32[48,48,128]{2,1,0:T(8,128)S(1)} %get-tuple-element.14.x, f32[48,48,128]{2,1,0:T(8,128)S(1)} %get-tuple-element.15.u, f32[48,48,128]{2,1,0:T(8,128)S(1)} %get-tuple-element.16.p, ...), custom_call_target="tpu_custom_call" | custom-call | tf_op jit(solution)/shard_map/pallas_call | solution.py:556

commit v9 on v8

--- a/solution.py
+++ b/solution.py
@@ -39,11 +39,7 @@
     y_low_wall, y_high_wall = gy == 0, gy > 0
     zero_slab = jnp.zeros((nl, LANES), F32)
     zero_acc = jnp.zeros((8, LANES), F32)
-    relative = [(a, b, c) for a in reversed(range(ngz)) for b in reversed(range(ngy)) for c in reversed(range(ngx))
-                if a or b or c]
-
-    def other(a, b, c):
-        return lax.rem(gz + a, ngz), lax.rem(gy + b, ngy), lax.rem(gx + c, ngx)
+    others = ngx * ngy * ngz - 1
 
     def column_roll(slab, shift):
         return pltpu.roll(slab, shift + 2 * LANES, 1)
@@ -101,11 +97,11 @@
         return state
 
     def exchange_start(ref, slot):
+        y_copy(slot).start()
+        pl.when(has_zlo)(lambda: z_copy(slot, False).start())
+        pl.when(has_zhi)(lambda: z_copy(slot, True).start())
         pl.when(has_xlo)(lambda: x_copy(ref, slot, False).start())
         pl.when(has_xhi)(lambda: x_copy(ref, slot, True).start())
-        pl.when(has_zlo)(lambda: z_copy(slot, False).start())
-        pl.when(has_zhi)(lambda: z_copy(slot, True).start())
-        y_copy(slot).start()
 
     def exchange_wait(ref, slot):
         @pl.when(has_xlo)
@@ -205,15 +201,22 @@
         red_s[slot] = row
         red_r[slot, (gz * ngy + gy) * ngx + gx] = row
 
-    def reduce_send(slot):
+    def reduce_send(slot, planes):
         me = (gz * ngy + gy) * ngx + gx
-        for delta in relative:
-            pltpu.make_async_remote_copy(
-                src_ref=red_s.at[slot], dst_ref=red_r.at[slot, me], send_sem=rs_sem.at[slot],
-                recv_sem=rr_sem.at[slot], device_id=other(*delta), device_id_type=MESH).start()
+        for k in planes:
+            z_to = jnp.where(2 * gz < ngz, ngz - 1 - k, k)
+            for b in reversed(range(ngy)):
+                for c in (2, 3, 1, 0):
+                    copy = pltpu.make_async_remote_copy(
+                        src_ref=red_s.at[slot], dst_ref=red_r.at[slot, me], send_sem=rs_sem.at[slot], recv_sem=rr_sem.at[slot],
+                        device_id=(z_to, lax.rem(gy + b, ngy), lax.rem(gx + c, ngx)), device_id_type=MESH)
+                    if b or c:
+                        copy.start()
+                    else:
+                        pl.when(z_to != gz)(copy.start)
 
     def reduce_wait(slot, count):
-        whole = red_r.at[slot, pl.ds(0, len(relative))]
+        whole = red_r.at[slot, pl.ds(0, others)]
         done = pltpu.make_async_remote_copy(
             src_ref=whole, dst_ref=whole, send_sem=rs_sem.at[slot], recv_sem=rr_sem.at[slot],
             device_id=(gz, gy, gx), device_id_type=MESH)
@@ -430,8 +433,9 @@
     def iteration(t, carry):
         gamma_old, pap_old, alpha_old, beta_old = carry
         now = lax.rem(t, 2)
-        reduce_send(t)
+        reduce_send(t, (0,))
         exchange_start(mp, t + 3)
+        reduce_send(t, range(1, ngz))
         stencil(mp)
         rr_acc = advance_x(now, alpha_old, beta_old)
         join_faces(mp, t + 3)
@@ -463,7 +467,7 @@
         0, last, iteration, (one, one, jnp.float32(0.0), jnp.float32(0.0)))
 
     now = last % 2
-    reduce_send(last)
+    reduce_send(last, range(ngz))
 
     def last_dots(i, acc):
         rv, sv = r[now, i], s[i]
@@ -473,7 +477,7 @@
         return tuple(a + fold(b * c) for a, (b, c) in zip(acc, pairs))
 
     reduce_row(CG_ITERS, slabs(2, last_dots, (zero_acc,) * 6))
-    reduce_send(CG_ITERS)
+    reduce_send(CG_ITERS, range(ngz))
     advance_x(now, alpha_old, beta_old)
     sums = reduce_wait(last, 4)
     wide = lambda value: jnp.broadcast_to(value, (1, LANES))

time: 70.5 us -> 69.5 us (0.986)
  Pallas kernels: 69.7 us -> 68.8 us
    pallas_call x1, Pallas kernels: 68.1 us -> 67.1 us  [local_solve(): pl.pallas_call(functools.partial(solve_kernel, (ni, nl, nj), counts), out...]
where the time goes in v9:
time: 69.5 us; the launch traced here: 69.4 us
  Pallas kernels  68.8 us (99%)
    pallas_call x1, Pallas kernels, local_solve(): pl.pallas_call(functools.partial(solve_kernel, (ni, nl, nj), counts), out...  67.1 us
    pallas_call x1, Pallas kernels, local_solve(): pl.pallas_call(functools.partial(finish_kernel, chunk), out_shape=(out_bl...  1.63 us

profile of v9, /device:TPU:0, one launch (start us, length us, event | category | flops | bytes accessed | tf_op | source)
XLA Modules:
  0.0 69.4 jit_solution(5458222246711698478)
XLA Ops:
  0.6 67.1 %shard_map.67 = (f32[48,48,128]{2,1,0:T(8,128)S(1)}, f32[48,48,128]{2,1,0:T(8,128)S(1)}, f32[48,48,128]{2,1,0:T(8,128)S(1)}, f32[2,48,48,128]{3,2,1,0:T(8,128)S(...) custom-call(f32[6,192,192]{2,1,0:T(8,128)} %kg_hbm.1, ...), custom_call_target="tpu_custom_call" | custom-call | tf_op jit(solution)/shard_map/pallas_call | solution.py:539
  67.8 1.6 %shard_map.68 = (f32[48,48,96]{2,1,0:T(8,128)}, f32[48,48,96]{2,1,0:T(8,128)}, f32[8]{0:T(128)}) custom-call(f32[10,1,128]{2,1,0:T(1,128)S(1)} %get-tuple-element.13.scal, f32[48,48,128]{2,1,0:T(8,128)S(1)} %get-tuple-element.14.x, f32[48,48,128]{2,1,0:T(8,128)S(1)} %get-tuple-element.15.u, f32[48,48,128]{2,1,0:T(8,128)S(1)} %get-tuple-element.16.p, ...), custom_call_target="tpu_custom_call" | custom-call | tf_op jit(solution)/shard_map/pallas_call | solution.py:560

commit v10 on v9

--- a/solution.py
+++ b/solution.py
@@ -12,6 +12,7 @@
 PAD = 8
 GROUP = 6
 COLUMNS = 16
+UPDATE = 4
 MESH = pl.DeviceIdType.MESH
 F32 = jnp.float32
 
@@ -68,8 +69,8 @@
             src_ref=ys.at[slot], dst_ref=yr.at[slot], send_sem=ys_sem.at[slot], recv_sem=yr_sem.at[slot],
             device_id=(gz, 1 - gy, gx), device_id_type=MESH)
 
-    def pack_rolls(ref, slot, i):
-        row = lax.max(i, 0) if not isinstance(i, int) else i
+    def pack_rolls(ref, slot, i, behind=False):
+        row = lax.max(i, 0) if behind else i
         slab = ref[row + 1, rows, :]
         zs[slot, 1, pl.ds(row, 1), :] = slab[0:1, :]
         zs[slot, 0, pl.ds(row, 1), :] = slab[nl - 1:nl, :]
@@ -79,10 +80,10 @@
         acc = jnp.where(lane_half == i, rolled[0], acc)
         return jnp.where(lane_half == i + LANES // 2, rolled[1], acc)
 
-    def packed_pass(ref, slot, step, init, tail=lambda state: state):
+    def packed_pass(ref, slot, step, init):
         def body(g, carry):
             state, acc = carry
-            rolled = [pack_rolls(ref, slot, (g - 1) * GROUP + k) for k in range(GROUP)]
+            rolled = [pack_rolls(ref, slot, (g - 1) * GROUP + k, behind=True) for k in range(GROUP)]
             for k in range(GROUP):
                 state = step(g * GROUP + k, state)
             for k in range(GROUP):
@@ -90,11 +91,21 @@
             return state, acc
         state, acc = lax.fori_loop(0, ni // GROUP, body, (init, jnp.zeros((half, LANES), F32)))
         rolled = [pack_rolls(ref, slot, ni - GROUP + k) for k in range(GROUP)]
-        state = tail(state)
         for k in range(GROUP):
             acc = pack(ni - GROUP + k, rolled[k], acc)
         ys[slot] = acc
         return state
+
+    def pack_faces(ref, slot):
+        group = min(COLUMNS, ni)
+
+        def body(g, acc):
+            rolled = [pack_rolls(ref, slot, g * group + k) for k in range(group)]
+            for k in range(group):
+                acc = pack(g * group + k, rolled[k], acc)
+            return acc
+
+        ys[slot] = lax.fori_loop(0, ni // group, body, jnp.zeros((half, LANES), F32))
 
     def exchange_start(ref, slot):
         y_copy(slot).start()
@@ -414,7 +425,7 @@
         mp[i + 1, rows, :] = av * inv[i]
         return acc
 
-    packed_pass(mp, 3, first_w, zero_acc, lambda delta_acc: reduce_row(0, (gamma_acc, delta_acc)))
+    reduce_row(0, (gamma_acc, slabs(GROUP, first_w, zero_acc)))
 
     def scalars(t, sums, gamma_old, pap_old):
         gamma, delta, sigma = sums[0], sums[1], sums[2]
@@ -433,9 +444,10 @@
     def iteration(t, carry):
         gamma_old, pap_old, alpha_old, beta_old = carry
         now = lax.rem(t, 2)
-        reduce_send(t, (0,))
+        reduce_send(t, range(0, ngz // 2))
+        pack_faces(mp, t + 3)
         exchange_start(mp, t + 3)
-        reduce_send(t, range(1, ngz))
+        reduce_send(t, range(ngz // 2, ngz))
         stencil(mp)
         rr_acc = advance_x(now, alpha_old, beta_old)
         join_faces(mp, t + 3)
@@ -457,7 +469,7 @@
             mp[i + 1, rows, :] = iv * w_new
             return acc[0] + fold(r_new * u_new), acc[1] + fold(w_new * u_new), acc[2] + fold(u_new * s_new)
 
-        packed_pass(mp, t + 4, update, (zero_acc,) * 3, lambda accs: reduce_row(t + 1, accs + (rr_acc,)))
+        reduce_row(t + 1, slabs(UPDATE, update, (zero_acc,) * 3) + (rr_acc,))
         scal_ref[lax.rem(t + CG_ITERS - 2, CG_ITERS)] = jnp.broadcast_to(sums[3], (1, LANES))
         return gamma, pap, alpha, beta
 

time: 69.5 us -> 65.1 us (0.937)
  Pallas kernels: 68.8 us -> 64.3 us
    pallas_call x1, Pallas kernels: 67.1 us -> 62.7 us  [local_solve(): pl.pallas_call(functools.partial(solve_kernel, (ni, nl, nj), counts), out...]
where the time goes in v10:
time: 65.1 us; the launch traced here: 64.9 us
  Pallas kernels  64.3 us (99%)
    pallas_call x1, Pallas kernels, local_solve(): pl.pallas_call(functools.partial(solve_kernel, (ni, nl, nj), counts), out...  62.7 us
    pallas_call x1, Pallas kernels, local_solve(): pl.pallas_call(functools.partial(finish_kernel, chunk), out_shape=(out_bl...  1.63 us

profile of v10, /device:TPU:0, one launch (start us, length us, event | category | flops | bytes accessed | tf_op | source)
XLA Modules:
  0.0 64.9 jit_solution(17573065760627417413)
XLA Ops:
  0.6 62.7 %shard_map.67 = (f32[48,48,128]{2,1,0:T(8,128)S(1)}, f32[48,48,128]{2,1,0:T(8,128)S(1)}, f32[48,48,128]{2,1,0:T(8,128)S(1)}, f32[2,48,48,128]{3,2,1,0:T(8,128)S(...) custom-call(f32[6,192,192]{2,1,0:T(8,128)} %kg_hbm.1, ...), custom_call_target="tpu_custom_call" | custom-call | tf_op jit(solution)/shard_map/pallas_call | solution.py:551
  63.3 1.6 %shard_map.68 = (f32[48,48,96]{2,1,0:T(8,128)}, f32[48,48,96]{2,1,0:T(8,128)}, f32[8]{0:T(128)}) custom-call(f32[10,1,128]{2,1,0:T(1,128)S(1)} %get-tuple-element.13.scal, f32[48,48,128]{2,1,0:T(8,128)S(1)} %get-tuple-element.14.x, f32[48,48,128]{2,1,0:T(8,128)S(1)} %get-tuple-element.15.u, f32[48,48,128]{2,1,0:T(8,128)S(1)} %get-tuple-element.16.p, ...), custom_call_target="tpu_custom_call" | custom-call | tf_op jit(solution)/shard_map/pallas_call | solution.py:572

commit v11 on v10

--- a/solution.py
+++ b/solution.py
@@ -69,12 +69,14 @@
             src_ref=ys.at[slot], dst_ref=yr.at[slot], send_sem=ys_sem.at[slot], recv_sem=yr_sem.at[slot],
             device_id=(gz, 1 - gy, gx), device_id_type=MESH)
 
+    def pack_slab(slot, i, slab):
+        zs[slot, 1, pl.ds(i, 1), :] = slab[0:1, :]
+        zs[slot, 0, pl.ds(i, 1), :] = slab[nl - 1:nl, :]
+        return column_roll(slab[0:half], i - face_lane), column_roll(slab[half:nl], i - face_lane + LANES // 2)
+
     def pack_rolls(ref, slot, i, behind=False):
         row = lax.max(i, 0) if behind else i
-        slab = ref[row + 1, rows, :]
-        zs[slot, 1, pl.ds(row, 1), :] = slab[0:1, :]
-        zs[slot, 0, pl.ds(row, 1), :] = slab[nl - 1:nl, :]
-        return column_roll(slab[0:half], row - face_lane), column_roll(slab[half:nl], row - face_lane + LANES // 2)
+        return pack_slab(slot, row, ref[row + 1, rows, :])
 
     def pack(i, rolled, acc):
         acc = jnp.where(lane_half == i, rolled[0], acc)
@@ -96,11 +98,16 @@
         ys[slot] = acc
         return state
 
-    def pack_faces(ref, slot):
+    def scale_and_pack(slot):
         group = min(COLUMNS, ni)
 
         def body(g, acc):
-            rolled = [pack_rolls(ref, slot, g * group + k) for k in range(group)]
+            rolled = []
+            for k in range(group):
+                i = g * group + k
+                m = inv[i] * w[i]
+                mp[i + 1, rows, :] = m
+                rolled.append(pack_slab(slot, i, m))
             for k in range(group):
                 acc = pack(g * group + k, rolled[k], acc)
             return acc
@@ -184,10 +191,12 @@
             z_copy(slot, False).wait_recv()
             add_rows(n, bz[1] * (zs[slot, 0] - zr[slot, 1]), nl - 1)
 
-    def stencil(ref):
+    def stencil(ref, diagonal=False):
         def step(i, carry):
             v, flux_x = carry
             above = ref[i + 2, rows, :]
+            if diagonal:
+                inv[i] = cx[i] + cx[i + 1] + cy[i] + cyh[i] + cz[i, rows, :] + cz[i, rows_up, :]
             flux_next = cx[i + 1] * (above - v)
             flux_zl = cz[i, rows, :] * (v - ref[i + 1, rows_dn, :])
             flux_zh = cz[i, rows_up, :] * (ref[i + 1, rows_up, :] - v)
@@ -362,13 +371,7 @@
         cz[i, PAD:PAD + 1, :] = z_low[i:i + 1, :]
         cz[i, PAD + nl:PAD + nl + 1, :] = z_high[i:i + 1, :]
 
-    stencil(mp)
-
-    def diagonal(i, _):
-        inv[i] = cx[i] + cx[i + 1] + cy[i] + cyh[i] + cz[i, rows, :] + cz[i, rows_up, :]
-        return 0
-
-    lax.fori_loop(0, ni, diagonal, 0)
+    stencil(mp, diagonal=True)
     next_round(3)
 
     exchange_wait(kp, 0)
@@ -421,9 +424,7 @@
     def first_w(i, acc):
         av = n[i]
         w[i] = av
-        acc = acc + fold(av * mp[i + 1, rows, :])
-        mp[i + 1, rows, :] = av * inv[i]
-        return acc
+        return acc + fold(av * mp[i + 1, rows, :])
 
     reduce_row(0, (gamma_acc, slabs(GROUP, first_w, zero_acc)))
 
@@ -445,7 +446,7 @@
         gamma_old, pap_old, alpha_old, beta_old = carry
         now = lax.rem(t, 2)
         reduce_send(t, range(0, ngz // 2))
-        pack_faces(mp, t + 3)
+        scale_and_pack(t + 3)
         exchange_start(mp, t + 3)
         reduce_send(t, range(ngz // 2, ngz))
         stencil(mp)
@@ -466,7 +467,6 @@
             s[i] = s_new
             r[1 - now, i] = r_new
             w[i] = w_new
-            mp[i + 1, rows, :] = iv * w_new
             return acc[0] + fold(r_new * u_new), acc[1] + fold(w_new * u_new), acc[2] + fold(u_new * s_new)
 
         reduce_row(t + 1, slabs(UPDATE, update, (zero_acc,) * 3) + (rr_acc,))
@@ -484,13 +484,18 @@
     def last_dots(i, acc):
         rv, sv = r[now, i], s[i]
         wv = w[i]
-        n[i] = inv[i] * rv
         pairs = ((rv, rv), (rv, wv), (rv, sv), (wv, wv), (wv, sv), (sv, sv))
         return tuple(a + fold(b * c) for a, (b, c) in zip(acc, pairs))
 
-    reduce_row(CG_ITERS, slabs(2, last_dots, (zero_acc,) * 6))
+    reduce_row(CG_ITERS, slabs(3, last_dots, (zero_acc,) * 6))
     reduce_send(CG_ITERS, range(ngz))
     advance_x(now, alpha_old, beta_old)
+
+    def last_u(i, _):
+        n[i] = inv[i] * r[now, i]
+        return 0
+
+    lax.fori_loop(0, ni, last_u, 0)
     sums = reduce_wait(last, 4)
     wide = lambda value: jnp.broadcast_to(value, (1, LANES))
     scal_ref[last - 2] = wide(sums[3])

time: 65.1 us -> 64.3 us (0.988)
  Pallas kernels: 64.3 us -> 63.5 us
    pallas_call x1, Pallas kernels: 62.7 us -> 61.9 us  [local_solve(): pl.pallas_call(functools.partial(solve_kernel, (ni, nl, nj), counts), out...]
where the time goes in v11:
time: 64.3 us; the launch traced here: 64.2 us
  Pallas kernels  63.5 us (99%)
    pallas_call x1, Pallas kernels, local_solve(): pl.pallas_call(functools.partial(solve_kernel, (ni, nl, nj), counts), out...  61.9 us
    pallas_call x1, Pallas kernels, local_solve(): pl.pallas_call(functools.partial(finish_kernel, chunk), out_shape=(out_bl...  1.63 us

profile of v11, /device:TPU:0, one launch (start us, length us, event | category | flops | bytes accessed | tf_op | source)
XLA Modules:
  0.0 64.2 jit_solution(3181908435028044235)
XLA Ops:
  0.6 61.9 %shard_map.67 = (f32[48,48,128]{2,1,0:T(8,128)S(1)}, f32[48,48,128]{2,1,0:T(8,128)S(1)}, f32[48,48,128]{2,1,0:T(8,128)S(1)}, f32[2,48,48,128]{3,2,1,0:T(8,128)S(...) custom-call(f32[6,192,192]{2,1,0:T(8,128)} %kg_hbm.1, ...), custom_call_target="tpu_custom_call" | custom-call | tf_op jit(solution)/shard_map/pallas_call | solution.py:556
  62.5 1.6 %shard_map.68 = (f32[48,48,96]{2,1,0:T(8,128)}, f32[48,48,96]{2,1,0:T(8,128)}, f32[8]{0:T(128)}) custom-call(f32[10,1,128]{2,1,0:T(1,128)S(1)} %get-tuple-element.13.scal, f32[48,48,128]{2,1,0:T(8,128)S(1)} %get-tuple-element.14.x, f32[48,48,128]{2,1,0:T(8,128)S(1)} %get-tuple-element.15.u, f32[48,48,128]{2,1,0:T(8,128)S(1)} %get-tuple-element.16.p, ...), custom_call_target="tpu_custom_call" | custom-call | tf_op jit(solution)/shard_map/pallas_call | solution.py:577

commit v12 on v11

--- a/solution.py
+++ b/solution.py
@@ -17,9 +17,9 @@
 F32 = jnp.float32
 
 
-def solve_kernel(dims, counts, kg_hbm, k_hbm, f_hbm, u_hbm, x, n, p, r, w, s, scal_ref,
+def solve_kernel(dims, counts, kg_hbm, k_hbm, f_hbm, u_hbm, x_last, r_last, scal_ref,
                  k_in, f_in, u_in, wall_x, wall_y, wall_z, wall_t, bx, by, bz,
-                 kp, mp, cx, cy, cyh, cz, inv, z,
+                 kp, mp, cx, cy, cyh, cz, inv, x, r, w, s, z, p, n,
                  ys, zs, xr, yr, zr, red_s, red_r,
                  xs_sem, ys_sem, zs_sem, xr_sem, yr_sem, zr_sem, rs_sem, rr_sem, in_sem, near_sem):
     ni, nl, nj = dims
@@ -242,7 +242,10 @@
             device_id=(gz, gy, gx), device_id_type=MESH)
         done.wait_recv()
         done.wait_send()
-        total = jnp.sum(red_r[slot], axis=0)
+        parts = [red_r[slot, device] for device in range(others + 1)]
+        while len(parts) > 1:
+            parts = [a + b for a, b in zip(parts[0::2], parts[1::2])]
+        total = parts[0]
         return [jnp.sum(jnp.where(lane_row == q, total, 0.0), axis=1, keepdims=True) for q in range(count)]
 
     x_row, z_row = jnp.where(gx == 0, 0, 1), jnp.where(gz == 0, 4, 5)
@@ -351,17 +354,17 @@
     z_high = jnp.where(jnp.logical_and(in_i, gz == ngz - 1), harmonic(zs[0, 0], z_wall), 0.0)
     y_low_mask = jnp.logical_and(inside, jnp.logical_or(lane > 0, y_low_wall))
     y_high_mask = jnp.logical_and(inside, jnp.logical_or(lane < nj - 1, y_high_wall))
-    wall_lane = nj - 1 - face_lane
+    wall_lane = jnp.where(gy == 0, 0, nj)
 
     def coefs(i, _):
         here = kp[i + 1, rows, :]
         cx[i + 1] = jnp.where(inside, harmonic(here, kp[i + 2, rows, :]), 0.0)
         cz[i, rows_up, :] = jnp.where(inside, harmonic(here, kp[i + 1, rows_up, :]), 0.0)
         wall = column_roll(y_wall, wall_lane - i)
-        low = jnp.where(lane == 0, wall, pltpu.roll(here, 1, 1))
-        high = jnp.where(lane == nj - 1, wall, pltpu.roll(here, LANES - 1, 1))
-        cy[i] = jnp.where(y_low_mask, harmonic(low, here), 0.0)
-        cyh[i] = jnp.where(y_high_mask, harmonic(here, high), 0.0)
+        low = jnp.where(jnp.logical_and(lane == 0, y_low_wall), wall, pltpu.roll(here, 1, 1))
+        faces = harmonic(low, jnp.where(jnp.logical_and(lane == nj, y_high_wall), wall, here))
+        cy[i] = jnp.where(y_low_mask, faces, 0.0)
+        cyh[i] = jnp.where(y_high_mask, pltpu.roll(faces, LANES - 1, 1), 0.0)
         return 0
 
     slabs(GROUP, coefs, 0)
@@ -432,9 +435,14 @@
         gamma, delta, sigma = sums[0], sums[1], sums[2]
         beta = jnp.where(t == 0, 0.0, gamma / gamma_old)
         pap = delta + 2.0 * beta * sigma + beta * beta * pap_old
-        return gamma, pap, beta[0, 0], (gamma / pap)[0, 0]
+        return gamma, pap, beta, gamma / pap
+
+    def wide(value):
+        return jnp.broadcast_to(value, (nl, LANES))
 
     def advance_x(now, alpha, beta):
+        alpha, beta = wide(alpha), wide(beta)
+
         def step(i, acc):
             p_new = inv[i] * r[1 - now, i] + beta * p[i]
             p[i] = p_new
@@ -455,13 +463,15 @@
         sums = reduce_wait(t, 4)
         gamma, pap, beta, alpha = scalars(t, sums, gamma_old, pap_old)
 
+        alpha_w, beta_w = wide(alpha), wide(beta)
+
         def update(i, acc):
             iv = inv[i]
             w_old = w[i]
-            z_new = n[i] + beta * z[i]
-            s_new = w_old + beta * s[i]
-            r_new = r[now, i] - alpha * s_new
-            w_new = w_old - alpha * z_new
+            z_new = n[i] + beta_w * z[i]
+            s_new = w_old + beta_w * s[i]
+            r_new = r[now, i] - alpha_w * s_new
+            w_new = w_old - alpha_w * z_new
             u_new = iv * r_new
             z[i] = z_new
             s[i] = s_new
@@ -476,7 +486,7 @@
     one = jnp.ones((1, 1), F32)
     last = CG_ITERS - 1
     gamma_old, pap_old, alpha_old, beta_old = lax.fori_loop(
-        0, last, iteration, (one, one, jnp.float32(0.0), jnp.float32(0.0)))
+        0, last, iteration, (one, one, 0.0 * one, 0.0 * one))
 
     now = last % 2
     reduce_send(last, range(ngz))
@@ -491,46 +501,34 @@
     reduce_send(CG_ITERS, range(ngz))
     advance_x(now, alpha_old, beta_old)
 
-    def last_u(i, _):
-        n[i] = inv[i] * r[now, i]
-        return 0
-
-    lax.fori_loop(0, ni, last_u, 0)
     sums = reduce_wait(last, 4)
-    wide = lambda value: jnp.broadcast_to(value, (1, LANES))
-    scal_ref[last - 2] = wide(sums[3])
+    line = lambda value: jnp.broadcast_to(value, (1, LANES))
+    scal_ref[last - 2] = line(sums[3])
     gamma = sums[0]
     beta = gamma / gamma_old
     alpha = gamma / (sums[1] + 2.0 * beta * sums[2] + beta * beta * pap_old)
-    scal_ref[CG_ITERS] = wide(alpha)
-    scal_ref[CG_ITERS + 1] = wide(beta)
+    alpha_w, beta_w = wide(alpha), wide(beta)
+
+    def final(i, _):
+        r_old = r[now, i]
+        x_last[i] = (x[i] + alpha_w * (inv[i] * r_old + beta_w * p[i]))[:, 0:nj]
+        r_last[i] = (r_old - alpha_w * (w[i] + beta_w * s[i]))[:, 0:nj]
+        return 0
+
+    slabs(2, final, 0)
     rr, rw, rs, ww, ws, ss = reduce_wait(CG_ITERS, 6)
-    scal_ref[last - 1] = wide(rr)
-    scal_ref[last] = wide(rr - 2.0 * alpha * (rw + beta * rs) + alpha * alpha * (ww + 2.0 * beta * ws + beta * beta * ss))
-
-
-def finish_kernel(chunk, scal, x, u, p, r, w, s, x_hbm, r_hbm, hist_hbm, x_new, r_new, hist, sem, hist_sem):
-    ni, nl, nj = x_new.shape
-    alpha = jnp.broadcast_to(scal[CG_ITERS], (nl, LANES))
-    beta = jnp.broadcast_to(scal[CG_ITERS + 1], (nl, LANES))
-    copies = []
-
-    def step(i, _):
-        x_new[i] = (x[i] + alpha * (u[i] + beta * p[i]))[:, 0:nj]
-        r_new[i] = (r[1, i] - alpha * (w[i] + beta * s[i]))[:, 0:nj]
-        return 0
-
-    for g in range(ni // chunk):
-        lax.fori_loop(g * chunk, (g + 1) * chunk, step, 0)
-        part = pl.ds(g * chunk, chunk)
-        for j, (src, dst) in enumerate(((x_new, x_hbm), (r_new, r_hbm))):
-            copies.append(pltpu.make_async_copy(src.at[part], dst.at[part], sem.at[j, g]))
-            copies[-1].start()
-        if g == 0:
-            for t in range(CG_ITERS):
-                hist[t] = scal[t, 0, 0]
-            copies.append(pltpu.make_async_copy(hist, hist_hbm, hist_sem))
-            copies[-1].start()
+    scal_ref[last - 1] = line(rr)
+    scal_ref[last] = line(rr - 2.0 * alpha * (rw + beta * rs) + alpha * alpha * (ww + 2.0 * beta * ws + beta * beta * ss))
+
+
+def finish_kernel(scal, x, r, x_hbm, r_hbm, hist_hbm, hist, sem):
+    copies = [pltpu.make_async_copy(x, x_hbm, sem.at[0]), pltpu.make_async_copy(r, r_hbm, sem.at[1]),
+              pltpu.make_async_copy(hist, hist_hbm, sem.at[2])]
+    copies[0].start()
+    copies[1].start()
+    for t in range(CG_ITERS):
+        hist[t] = scal[t, 0, 0]
+    copies[2].start()
     for copy in copies:
         copy.wait()
 
@@ -551,19 +549,18 @@
         block = vm(ni, nl, nj)
         padded = vm(ni + 2, nl + 2 * PAD, LANES)
         dma = pltpu.SemaphoreType.DMA
-        kept = pltpu.VMEM((ni, nl, LANES), F32)
+        kept = pltpu.VMEM((ni, nl, nj), F32)
         vmem_spec = pl.BlockSpec(memory_space=pltpu.VMEM)
-        *state, scal = pl.pallas_call(
+        x_last, r_last, scal = pl.pallas_call(
             functools.partial(solve_kernel, (ni, nl, nj), counts),
-            out_shape=(kept, kept, kept, pltpu.VMEM((2, ni, nl, LANES), F32), kept, kept,
-                       pltpu.VMEM((CG_ITERS + 2, 1, LANES), F32)),
+            out_shape=(kept, kept, pltpu.VMEM((CG_ITERS, 1, LANES), F32)),
             in_specs=[any_spec] * 4,
-            out_specs=(vmem_spec,) * 7,
+            out_specs=(vmem_spec,) * 3,
             scratch_shapes=[
                 block, block, block, vm(nj, width), vm(ni, width), vm(ni, width), vm(-(-width // LANES) * LANES, LANES),
                 vm(2, nl, LANES), vm(nl // 2, LANES), vm(2, ni, LANES),
                 padded, padded, vm(ni + 1, nl, LANES), whole, whole, vm(ni, nl + 2 * PAD, LANES), whole,
-                whole,
+                whole, vm(2, ni, nl, LANES), whole, whole, whole, whole, whole,
                 vm(slots, nl // 2, LANES), vm(slots, 2, ni, LANES),
                 vm(slots, 2, nl, LANES), vm(slots, nl // 2, LANES), vm(slots, 2, ni, LANES),
                 vm(CG_ITERS + 1, 1, LANES), vm(CG_ITERS + 1, devices, 1, LANES),
@@ -572,16 +569,15 @@
             ],
             compiler_params=pltpu.CompilerParams(has_side_effects=True, collective_id=0, vmem_limit_bytes=28 << 20),
         )(*(pltpu.with_memory_space_constraint(a, pltpu.HBM) for a in (k_ghost, flip(k_cell), flip(f_rhs), flip(u_init))))
-        chunk = ni // 4
         out_block = jax.ShapeDtypeStruct((ni, nl, nj), F32)
         x_new, r_new, hist = pl.pallas_call(
-            functools.partial(finish_kernel, chunk),
+            finish_kernel,
             out_shape=(out_block, out_block, jax.ShapeDtypeStruct((CG_ITERS,), F32)),
-            in_specs=[vmem_spec] * 7,
+            in_specs=[vmem_spec] * 3,
             out_specs=(any_spec,) * 3,
-            scratch_shapes=[block, block, pltpu.SMEM((CG_ITERS,), F32), dma((2, ni // chunk)), dma],
+            scratch_shapes=[pltpu.SMEM((CG_ITERS,), F32), dma((3,))],
             compiler_params=pltpu.CompilerParams(vmem_limit_bytes=28 << 20),
-        )(scal, *state)
+        )(scal, x_last, r_last)
         return flip(x_new), flip(r_new), hist
 
     return jax.shard_map(local_solve, mesh=mesh, in_specs=(grid_spec, P(), grid_spec, grid_spec),

time: 64.3 us -> 63.8 us (level)
  no operation moved by 1% of the time
where the time goes in v12:
time: 63.8 us; the launch traced here: 63.6 us
  Pallas kernels  63 us (99%)
  between operations  0.64 us (1%)
    pallas_call x1, Pallas kernels, local_solve(): pl.pallas_call(functools.partial(solve_kernel, (ni, nl, nj), counts), out...  61.6 us
    pallas_call x1, Pallas kernels, local_solve(): pl.pallas_call(finish_kernel, out_shape=(out_block, out_block, jax.ShapeD...  1.44 us

profile of v12, /device:TPU:0, one launch (start us, length us, event | category | flops | bytes accessed | tf_op | source)
XLA Modules:
  0.0 63.6 jit_solution(15951118159800683957)
XLA Ops:
  0.6 61.6 %shard_map.67 = (f32[48,48,96]{2,1,0:T(8,128)S(1)}, f32[48,48,96]{2,1,0:T(8,128)S(1)}, f32[8,1,128]{2,1,0:T(1,128)S(1)}) custom-call(f32[6,192,192]{2,1,0:T(8,128)} %kg_hbm.1, f32[48,48,96]{2,1,0:T(8,128)} %bitcast.5, f32[48,48,96]{2,1,0:T(8,128)} %bitcast.6, f32[48,48,96]{2,1,0:T(8,128)} %bitcast.7), custom_call_target="tpu_custom_call" | custom-call | tf_op jit(solution)/shard_map/pallas_call | solution.py:554
  62.2 1.4 %shard_map.68 = (f32[48,48,96]{2,1,0:T(8,128)}, f32[48,48,96]{2,1,0:T(8,128)}, f32[8]{0:T(128)}) custom-call(f32[8,1,128]{2,1,0:T(1,128)S(1)} %get-tuple-element.9.scal, f32[48,48,96]{2,1,0:T(8,128)S(1)} %get-tuple-element.10.x, f32[48,48,96]{2,1,0:T(8,128)S(1)} %get-tuple-element.11.r), custom_call_target="tpu_custom_call" | custom-call | tf_op jit(solution)/shard_map/pallas_call | solution.py:573

commit v13 on v12

--- a/solution.py
+++ b/solution.py
@@ -223,17 +223,17 @@
 
     def reduce_send(slot, planes):
         me = (gz * ngy + gy) * ngx + gx
+        far, next_far = jnp.where(gz < 2, 3, 0), jnp.where(gz < 2, 2, 1)
+        order = (far, next_far, 6 - gz - far - next_far, gz)
         for k in planes:
-            z_to = jnp.where(2 * gz < ngz, ngz - 1 - k, k)
+            z_to = order[k]
             for b in reversed(range(ngy)):
                 for c in (2, 3, 1, 0):
                     copy = pltpu.make_async_remote_copy(
                         src_ref=red_s.at[slot], dst_ref=red_r.at[slot, me], send_sem=rs_sem.at[slot], recv_sem=rr_sem.at[slot],
                         device_id=(z_to, lax.rem(gy + b, ngy), lax.rem(gx + c, ngx)), device_id_type=MESH)
-                    if b or c:
+                    if b or c or k < ngz - 1:
                         copy.start()
-                    else:
-                        pl.when(z_to != gz)(copy.start)
 
     def reduce_wait(slot, count):
         whole = red_r.at[slot, pl.ds(0, others)]
@@ -453,10 +453,10 @@
     def iteration(t, carry):
         gamma_old, pap_old, alpha_old, beta_old = carry
         now = lax.rem(t, 2)
-        reduce_send(t, range(0, ngz // 2))
+        reduce_send(t, range(0, ngz - 1))
         scale_and_pack(t + 3)
         exchange_start(mp, t + 3)
-        reduce_send(t, range(ngz // 2, ngz))
+        reduce_send(t, (ngz - 1,))
         stencil(mp)
         rr_acc = advance_x(now, alpha_old, beta_old)
         join_faces(mp, t + 3)

time: 63.8 us -> 63.7 us (level)
  no operation moved by 1% of the time
where the time goes in v13:
time: 63.7 us; the launch traced here: 63.5 us
  Pallas kernels  62.9 us (99%)
  between operations  0.64 us (1%)
    pallas_call x1, Pallas kernels, local_solve(): pl.pallas_call(functools.partial(solve_kernel, (ni, nl, nj), counts), out...  61.5 us
    pallas_call x1, Pallas kernels, local_solve(): pl.pallas_call(finish_kernel, out_shape=(out_block, out_block, jax.ShapeD...  1.44 us

profile of v13, /device:TPU:0, one launch (start us, length us, event | category | flops | bytes accessed | tf_op | source)
XLA Modules:
  0.0 63.5 jit_solution(12298642794649633469)
XLA Ops:
  0.6 61.5 %shard_map.67 = (f32[48,48,96]{2,1,0:T(8,128)S(1)}, f32[48,48,96]{2,1,0:T(8,128)S(1)}, f32[8,1,128]{2,1,0:T(1,128)S(1)}) custom-call(f32[6,192,192]{2,1,0:T(8,128)} %kg_hbm.1, f32[48,48,96]{2,1,0:T(8,128)} %bitcast.5, f32[48,48,96]{2,1,0:T(8,128)} %bitcast.6, f32[48,48,96]{2,1,0:T(8,128)} %bitcast.7), custom_call_target="tpu_custom_call" | custom-call | tf_op jit(solution)/shard_map/pallas_call | solution.py:554
  62.1 1.4 %shard_map.68 = (f32[48,48,96]{2,1,0:T(8,128)}, f32[48,48,96]{2,1,0:T(8,128)}, f32[8]{0:T(128)}) custom-call(f32[8,1,128]{2,1,0:T(1,128)S(1)} %get-tuple-element.9.scal, f32[48,48,96]{2,1,0:T(8,128)S(1)} %get-tuple-element.10.x, f32[48,48,96]{2,1,0:T(8,128)S(1)} %get-tuple-element.11.r), custom_call_target="tpu_custom_call" | custom-call | tf_op jit(solution)/shard_map/pallas_call | solution.py:573

commit v14 on v13

--- a/solution.py
+++ b/solution.py
@@ -11,7 +11,7 @@
 LANES = 128
 PAD = 8
 GROUP = 6
-COLUMNS = 16
+COLUMNS = 24
 UPDATE = 4
 MESH = pl.DeviceIdType.MESH
 F32 = jnp.float32

time: 63.7 us -> 63.4 us (level)
  no operation moved by 1% of the time
where the time goes in v14:
time: 63.4 us; the launch traced here: 63.3 us
  Pallas kernels  62.6 us (99%)
  between operations  0.64 us (1%)
    pallas_call x1, Pallas kernels, local_solve(): pl.pallas_call(functools.partial(solve_kernel, (ni, nl, nj), counts), out...  61.2 us
    pallas_call x1, Pallas kernels, local_solve(): pl.pallas_call(finish_kernel, out_shape=(out_block, out_block, jax.ShapeD...  1.44 us

profile of v14, /device:TPU:0, one launch (start us, length us, event | category | flops | bytes accessed | tf_op | source)
XLA Modules:
  0.0 63.3 jit_solution(3361259523665693010)
XLA Ops:
  0.6 61.2 %shard_map.67 = (f32[48,48,96]{2,1,0:T(8,128)S(1)}, f32[48,48,96]{2,1,0:T(8,128)S(1)}, f32[8,1,128]{2,1,0:T(1,128)S(1)}) custom-call(f32[6,192,192]{2,1,0:T(8,128)} %kg_hbm.1, f32[48,48,96]{2,1,0:T(8,128)} %bitcast.5, f32[48,48,96]{2,1,0:T(8,128)} %bitcast.6, f32[48,48,96]{2,1,0:T(8,128)} %bitcast.7), custom_call_target="tpu_custom_call" | custom-call | tf_op jit(solution)/shard_map/pallas_call | solution.py:554
  61.8 1.4 %shard_map.68 = (f32[48,48,96]{2,1,0:T(8,128)}, f32[48,48,96]{2,1,0:T(8,128)}, f32[8]{0:T(128)}) custom-call(f32[8,1,128]{2,1,0:T(1,128)S(1)} %get-tuple-element.9.scal, f32[48,48,96]{2,1,0:T(8,128)S(1)} %get-tuple-element.10.x, f32[48,48,96]{2,1,0:T(8,128)S(1)} %get-tuple-element.11.r), custom_call_target="tpu_custom_call" | custom-call | tf_op jit(solution)/shard_map/pallas_call | solution.py:573

commit v15 on v14

--- a/solution.py
+++ b/solution.py
@@ -11,8 +11,8 @@
 LANES = 128
 PAD = 8
 GROUP = 6
-COLUMNS = 24
-UPDATE = 4
+COLUMNS = 48
+UPDATE = 8
 MESH = pl.DeviceIdType.MESH
 F32 = jnp.float32
 

time: 63.4 us -> 62.6 us (0.987)
  Pallas kernels: 62.6 us -> 61.8 us
    pallas_call x1, Pallas kernels: 61.2 us -> 60.4 us  [local_solve(): pl.pallas_call(functools.partial(solve_kernel, (ni, nl, nj), counts), out...]
where the time goes in v15:
time: 62.6 us; the launch traced here: 62.5 us
  Pallas kernels  61.8 us (99%)
  between operations  0.64 us (1%)
    pallas_call x1, Pallas kernels, local_solve(): pl.pallas_call(functools.partial(solve_kernel, (ni, nl, nj), counts), out...  60.4 us
    pallas_call x1, Pallas kernels, local_solve(): pl.pallas_call(finish_kernel, out_shape=(out_block, out_block, jax.ShapeD...  1.44 us

profile of v15, /device:TPU:0, one launch (start us, length us, event | category | flops | bytes accessed | tf_op | source)
XLA Modules:
  0.0 62.5 jit_solution(2251669280175485733)
XLA Ops:
  0.6 60.4 %shard_map.67 = (f32[48,48,96]{2,1,0:T(8,128)S(1)}, f32[48,48,96]{2,1,0:T(8,128)S(1)}, f32[8,1,128]{2,1,0:T(1,128)S(1)}) custom-call(f32[6,192,192]{2,1,0:T(8,128)} %kg_hbm.1, f32[48,48,96]{2,1,0:T(8,128)} %bitcast.5, f32[48,48,96]{2,1,0:T(8,128)} %bitcast.6, f32[48,48,96]{2,1,0:T(8,128)} %bitcast.7), custom_call_target="tpu_custom_call" | custom-call | tf_op jit(solution)/shard_map/pallas_call | solution.py:554
  61.0 1.4 %shard_map.68 = (f32[48,48,96]{2,1,0:T(8,128)}, f32[48,48,96]{2,1,0:T(8,128)}, f32[8]{0:T(128)}) custom-call(f32[8,1,128]{2,1,0:T(1,128)S(1)} %get-tuple-element.9.scal, f32[48,48,96]{2,1,0:T(8,128)S(1)} %get-tuple-element.10.x, f32[48,48,96]{2,1,0:T(8,128)S(1)} %get-tuple-element.11.r), custom_call_target="tpu_custom_call" | custom-call | tf_op jit(solution)/shard_map/pallas_call | solution.py:573

commit v16 on v15

--- a/solution.py
+++ b/solution.py
@@ -10,7 +10,7 @@
 CG_ITERS = 8
 LANES = 128
 PAD = 8
-GROUP = 6
+GROUP = 12
 COLUMNS = 48
 UPDATE = 8
 MESH = pl.DeviceIdType.MESH

time: 62.6 us -> 62.8 us (level)
  no operation moved by 1% of the time
where the time goes in v16:
time: 62.8 us; the launch traced here: 62.6 us
  Pallas kernels  62 us (99%)
  between operations  0.64 us (1%)
    pallas_call x1, Pallas kernels, local_solve(): pl.pallas_call(functools.partial(solve_kernel, (ni, nl, nj), counts), out...  60.6 us
    pallas_call x1, Pallas kernels, local_solve(): pl.pallas_call(finish_kernel, out_shape=(out_block, out_block, jax.ShapeD...  1.44 us

profile of v16, /device:TPU:0, one launch (start us, length us, event | category | flops | bytes accessed | tf_op | source)
XLA Modules:
  0.0 62.6 jit_solution(17382478318291855054)
XLA Ops:
  0.6 60.6 %shard_map.67 = (f32[48,48,96]{2,1,0:T(8,128)S(1)}, f32[48,48,96]{2,1,0:T(8,128)S(1)}, f32[8,1,128]{2,1,0:T(1,128)S(1)}) custom-call(f32[6,192,192]{2,1,0:T(8,128)} %kg_hbm.1, f32[48,48,96]{2,1,0:T(8,128)} %bitcast.5, f32[48,48,96]{2,1,0:T(8,128)} %bitcast.6, f32[48,48,96]{2,1,0:T(8,128)} %bitcast.7), custom_call_target="tpu_custom_call" | custom-call | tf_op jit(solution)/shard_map/pallas_call | solution.py:554
  61.2 1.4 %shard_map.68 = (f32[48,48,96]{2,1,0:T(8,128)}, f32[48,48,96]{2,1,0:T(8,128)}, f32[8]{0:T(128)}) custom-call(f32[8,1,128]{2,1,0:T(1,128)S(1)} %get-tuple-element.9.scal, f32[48,48,96]{2,1,0:T(8,128)S(1)} %get-tuple-element.10.x, f32[48,48,96]{2,1,0:T(8,128)S(1)} %get-tuple-element.11.r), custom_call_target="tpu_custom_call" | custom-call | tf_op jit(solution)/shard_map/pallas_call | solution.py:573

commit v17 on v15

--- a/solution.py
+++ b/solution.py
@@ -453,10 +453,10 @@
     def iteration(t, carry):
         gamma_old, pap_old, alpha_old, beta_old = carry
         now = lax.rem(t, 2)
-        reduce_send(t, range(0, ngz - 1))
+        reduce_send(t, range(0, ngz // 2))
         scale_and_pack(t + 3)
         exchange_start(mp, t + 3)
-        reduce_send(t, (ngz - 1,))
+        reduce_send(t, range(ngz // 2, ngz))
         stencil(mp)
         rr_acc = advance_x(now, alpha_old, beta_old)
         join_faces(mp, t + 3)

time: 62.6 us -> 63 us (level)
  no operation moved by 1% of the time
where the time goes in v17:
time: 63 us; the launch traced here: 62.8 us
  Pallas kernels  62.2 us (99%)
  between operations  0.64 us (1%)
    pallas_call x1, Pallas kernels, local_solve(): pl.pallas_call(functools.partial(solve_kernel, (ni, nl, nj), counts), out...  60.7 us
    pallas_call x1, Pallas kernels, local_solve(): pl.pallas_call(finish_kernel, out_shape=(out_block, out_block, jax.ShapeD...  1.44 us

profile of v17, /device:TPU:0, one launch (start us, length us, event | category | flops | bytes accessed | tf_op | source)
XLA Modules:
  0.0 62.8 jit_solution(3785863909491720030)
XLA Ops:
  0.6 60.7 %shard_map.67 = (f32[48,48,96]{2,1,0:T(8,128)S(1)}, f32[48,48,96]{2,1,0:T(8,128)S(1)}, f32[8,1,128]{2,1,0:T(1,128)S(1)}) custom-call(f32[6,192,192]{2,1,0:T(8,128)} %kg_hbm.1, f32[48,48,96]{2,1,0:T(8,128)} %bitcast.5, f32[48,48,96]{2,1,0:T(8,128)} %bitcast.6, f32[48,48,96]{2,1,0:T(8,128)} %bitcast.7), custom_call_target="tpu_custom_call" | custom-call | tf_op jit(solution)/shard_map/pallas_call | solution.py:554
  61.4 1.4 %shard_map.68 = (f32[48,48,96]{2,1,0:T(8,128)}, f32[48,48,96]{2,1,0:T(8,128)}, f32[8]{0:T(128)}) custom-call(f32[8,1,128]{2,1,0:T(1,128)S(1)} %get-tuple-element.9.scal, f32[48,48,96]{2,1,0:T(8,128)S(1)} %get-tuple-element.10.x, f32[48,48,96]{2,1,0:T(8,128)S(1)} %get-tuple-element.11.r), custom_call_target="tpu_custom_call" | custom-call | tf_op jit(solution)/shard_map/pallas_call | solution.py:573
